TPU v7x, 32 devices: a whole 2x2x4 slice. The times are simulated.
32 devices in a mesh: tok: 16 (over z, y, core), cand: 2 (over x).
Axes of the slice: x: 2, y: 2, z: 4, core: 2. Of those that a mesh axis runs over, the one named last changes fastest.
Arguments:
- dec_hidden: bfloat16 [2, 16, 32, 2048], P(None, 'cand'), may hold values from -6 to 6
- enc_keys: bfloat16 [2, 2048, 2048], P(None, 'tok'), may hold values from -250 to 250
- enc_values: bfloat16 [2, 2048, 2048], P(None, 'tok'), may hold values from -72 to 72
- enc_lengths: int32 [2], replicated, may hold values from 512 to 2048, as said below
- cand_counts: int32 [2], replicated, may hold values from 4 to 16, as said below
- gold_ids: int32 [2, 16, 32], P(None, 'cand'), may hold values from 0 to 32127
- gain_cross: float32 [2048], replicated, may hold values from 0.25 to 1.75
- w_query: bfloat16 [2048, 2048], P('cand', 'tok'), may hold values from -0.125 to 0.125
- w_out: bfloat16 [2048, 2048], P('tok', 'cand'), may hold values from -0.125 to 0.125
- gain_ffn: float32 [2048], replicated, may hold values from 0.25 to 1.75
- w_in_gate: bfloat16 [2048, 5120], P('cand', 'tok'), may hold values from -0.125 to 0.125
- w_in_up: bfloat16 [2048, 5120], P('cand', 'tok'), may hold values from -0.125 to 0.125
- w_ffn_out: bfloat16 [5120, 2048], P('tok', 'cand'), may hold values from -0.25 to 0.25
- gain_final: float32 [2048], replicated, may hold values from 0.25 to 1.75
- w_vocab: bfloat16 [2048, 32128], P('cand', 'tok'), may hold values from -20 to 20
Outputs:
- cand_scores: float32 [2, 16], P(None, 'cand')
- best_score: float32 [2], replicated
Inputs may be any that keep to these rules, and one draw needn't show every extreme that they name: `enc_lengths`: some query has all 2048 encoder tokens live. `cand_counts`: some query has all 16 candidates live.
All inputs are finite; a program needn't handle non-finite values.
Results may differ from a plain program's by a relative error of at most 0.0014.
The roundings to bfloat16 on the way count: a program that leaves them out, or rounds other values in their place, can miss the bound.
Values may be sent and summed in bfloat16 or wider, within the bound.
No kernel may reach another device: no remote copies, remote signals or barrier semaphores. Data moves between devices by JAX's collectives and lax.ppermute only.
A program may use at most 64 MiB of HBM per device.

v0:
```python
import functools

import jax
import jax.numpy as jnp
from jax import lax
from jax.experimental import pallas as pl
from jax.experimental.pallas import tpu as pltpu
from jax.sharding import PartitionSpec as P


HEAD_DIM = 64
NORM_EPS = 0.25
NEG = -1e30
VOCAB_STEP = 256


VMEM = pltpu.VMEM
SMEM = pltpu.SMEM


def vmem_spec():
    return pl.BlockSpec(memory_space=VMEM)


def smem_spec():
    return pl.BlockSpec(memory_space=SMEM)


def any_spec():
    return pl.BlockSpec(memory_space=pl.ANY)


def dot32(a, b):
    return jnp.dot(a, b, preferred_element_type=jnp.float32)


def dot32_t(a, b):
    return lax.dot_general(a, b, (((1,), (1,)), ((), ())), preferred_element_type=jnp.float32)


def gelu_tanh(v):
    inner = 0.7978845608028654 * (v + 0.044715 * (v * v * v))
    return 0.5 * v * (1.0 + jnp.tanh(inner))


def attention_kernel(live_ref, mine_ref, peer_ref, kv_ref, out_ref):
    src = kv_ref.shape[0] * kv_ref.shape[2]
    cols = kv_ref.shape[3]
    keys = kv_ref[:, 0].reshape(src, cols)
    values = kv_ref[:, 1].reshape(src, cols)
    token = lax.broadcasted_iota(jnp.int32, (1, src), 1)
    bias = jnp.where(token < live_ref[0], 0.0, NEG).astype(jnp.float32)
    lane_head = lax.broadcasted_iota(jnp.int32, (1, cols), 1) // HEAD_DIM
    rows = mine_ref.shape[0]
    step = min(rows, 128)
    for part, q_ref in enumerate((mine_ref, peer_ref)):
        for start in range(0, rows, step):
            q = q_ref[start : start + step, :]
            mixed = jnp.zeros((step, cols), jnp.float32)
            for head in range(cols // HEAD_DIM):
                q_head = jnp.where(lane_head == head, q, jnp.zeros_like(q))
                scores = dot32_t(q_head, keys) + bias
                row_max = jnp.max(scores, axis=-1, keepdims=True)
                weights = jnp.exp(scores - row_max)
                denominator = jnp.sum(weights, axis=-1, keepdims=True)
                head_out = dot32(weights.astype(jnp.bfloat16), values) / denominator
                mixed = jnp.where(lane_head == head, head_out, mixed)
            out_ref[part, start : start + step, :] = mixed.astype(jnp.bfloat16)


def attention(live, mine, peer, kv):
    rows, cols = mine.shape
    return pl.pallas_call(
        attention_kernel,
        out_shape=jax.ShapeDtypeStruct((2, rows, cols), jnp.bfloat16),
        in_specs=[smem_spec(), vmem_spec(), vmem_spec(), vmem_spec()],
        out_specs=vmem_spec(),
        name="attention",
    )(live, mine, peer, kv)


def project_kernel(n_cand, count, chip_ref, own_ref, par_ref, *refs):
    weights = refs[: 2 * n_cand]
    outs = refs[2 * n_cand : 2 * n_cand + count]
    own_s, par_s = refs[2 * n_cand + count :]
    share = own_ref.shape[0] // count
    for j in range(count):
        at = pl.multiple_of((chip_ref[0] ^ j) * share, share)
        own_s[j * share : (j + 1) * share, :] = own_ref[pl.ds(at, share), :]
        par_s[j * share : (j + 1) * share, :] = par_ref[pl.ds(at, share), :]
    own, par = own_s[...], par_s[...]
    width = weights[0].shape[1]
    for s in range(n_cand):
        block = dot32(own, weights[s][...]) + dot32(par, weights[n_cand + s][...])
        block = block.astype(jnp.bfloat16)
        for j in range(count):
            outs[j][:, s * width : (s + 1) * width] = block[j * share : (j + 1) * share, :]


def project(chip, own, par, weights, count):
    rows, cols = own.shape
    n_cand = len(weights) // 2
    model = weights[0].shape[1] * n_cand
    return pl.pallas_call(
        functools.partial(project_kernel, n_cand, count),
        out_shape=[jax.ShapeDtypeStruct((rows // count, model), jnp.bfloat16)] * count,
        in_specs=[smem_spec()] + [vmem_spec()] * (2 + len(weights)),
        out_specs=[vmem_spec()] * count,
        scratch_shapes=[VMEM((rows, cols), jnp.bfloat16)] * 2,
        name="project",
    )(chip, own, par, *weights)


def residual_kernel(count, base_ref, gain_ref, *refs):
    total = base_ref[...].astype(jnp.float32)
    for part in refs[:count]:
        total = total + part[...].astype(jnp.float32)
    squares = jnp.mean(total * total, axis=-1, keepdims=True)
    refs[count][...] = (total * lax.rsqrt(squares + NORM_EPS) * gain_ref[...]).astype(jnp.bfloat16)
    if len(refs) > count + 1:
        refs[count + 1][...] = total


def residual_norm(base, gain, parts, keep):
    shapes = [jax.ShapeDtypeStruct(base.shape, jnp.bfloat16)]
    if keep:
        shapes.append(jax.ShapeDtypeStruct(base.shape, jnp.float32))
    return pl.pallas_call(
        functools.partial(residual_kernel, len(parts)),
        out_shape=shapes,
        in_specs=[vmem_spec()] * (2 + len(parts)),
        out_specs=[vmem_spec()] * len(shapes),
        name="residual_norm",
    )(base, gain, *parts)


def ffn_kernel(n_cand, count, *refs):
    n_w = 2 * n_cand
    rows_in = refs[:count]
    gates = refs[count : count + n_w]
    ups = refs[count + n_w : count + 2 * n_w]
    downs = refs[count + 2 * n_w : count + 3 * n_w]
    outs = refs[count + 3 * n_w : 2 * count + 3 * n_w]
    scratch = refs[2 * count + 3 * n_w :]
    acts, gate_s, up_s, down_s, sems = scratch
    share = rows_in[0].shape[0]
    copies = []

    def fetch(source, target):
        copy = pltpu.make_async_copy(source, target, sems.at[len(copies)])
        copy.start()
        copies.append(copy)
        return copy

    row_copies = [fetch(rows_in[j], acts.at[pl.ds(j * share, share)]) for j in range(count)]
    gate_copies, up_copies, down_copies = [], [], []
    for i in range(n_w):
        gate_copies.append(fetch(gates[i], gate_s.at[i]))
        up_copies.append(fetch(ups[i], up_s.at[i]))
    for i in range(n_w):
        down_copies.append(fetch(downs[i], down_s.at[i]))
    for copy in row_copies:
        copy.wait()
    depth = gates[0].shape[1]
    hidden = []
    for side in range(2):
        gate_part, up_part = None, None
        for s in range(n_cand):
            i = side * n_cand + s
            block = acts[:, s * depth : (s + 1) * depth]
            gate_copies[i].wait()
            term = dot32_t(block, gate_s[i])
            gate_part = term if gate_part is None else gate_part + term
            up_copies[i].wait()
            term = dot32_t(block, up_s[i])
            up_part = term if up_part is None else up_part + term
        hidden.append((gelu_tanh(gate_part) * up_part).astype(jnp.bfloat16))
    width = downs[0].shape[1]
    for copy in down_copies:
        copy.wait()
    for s in range(n_cand):
        block = dot32(hidden[0], down_s[s]) + dot32(hidden[1], down_s[n_cand + s])
        block = block.astype(jnp.bfloat16)
        for j in range(count):
            outs[j][:, s * width : (s + 1) * width] = block[j * share : (j + 1) * share, :]


def feed_forward(rows_in, gates, ups, downs):
    count, n_w = len(rows_in), len(gates)
    n_cand = n_w // 2
    share, model = rows_in[0].shape
    return pl.pallas_call(
        functools.partial(ffn_kernel, n_cand, count),
        out_shape=[jax.ShapeDtypeStruct((share, model), jnp.bfloat16)] * count,
        in_specs=[any_spec()] * (count + 3 * n_w),
        out_specs=[vmem_spec()] * count,
        scratch_shapes=[
            VMEM((share * count, model), jnp.bfloat16),
            VMEM((n_w,) + gates[0].shape, jnp.bfloat16),
            VMEM((n_w,) + ups[0].shape, jnp.bfloat16),
            VMEM((n_w,) + downs[0].shape, jnp.bfloat16),
            pltpu.SemaphoreType.DMA((count + 3 * n_w,)),
        ],
        name="feed_forward",
    )(*rows_in, *gates, *ups, *downs)


def vocab_kernel(n_cand, count, n_src, first, end, start_ref, gold_ref, *refs):
    n_w = 2 * n_cand
    rows_in = refs[:count]
    weights = refs[count : count + n_w]
    carried = refs[count + n_w : count + n_w + n_src]
    out_ref, acts = refs[count + n_w + n_src :]
    step = pl.program_id(0)
    share = rows_in[0].shape[0]
    rows = share * count

    @pl.when(step == 0)
    def _():
        for j in range(count):
            acts[j * share : (j + 1) * share, :] = rows_in[j][...]
        if n_src:
            out_ref[...] = carried[0][...]
        else:
            out_ref[0] = jnp.full((8, rows), NEG, jnp.float32)
            out_ref[1] = jnp.zeros((8, rows), jnp.float32)
            out_ref[2] = jnp.zeros((8, rows), jnp.float32)

    width, depth = weights[0].shape
    column = (first + step) * width + lax.broadcasted_iota(jnp.int32, (width, 1), 0)
    inside = column < end
    for side in range(2):
        logits = None
        for s in range(n_cand):
            term = dot32_t(weights[side * n_cand + s][...], acts[:, s * depth : (s + 1) * depth])
            logits = term if logits is None else logits + term
        hit = (column == gold_ref[...] - start_ref[side]) & inside
        picked = jnp.where(hit, logits, 0.0).reshape(width // 8, 8, rows)
        out_ref[2] += jnp.sum(picked, axis=0)
        logits = jnp.where(inside, logits, NEG).reshape(width // 8, 8, rows)
        old = out_ref[0]
        new = jnp.maximum(old, jnp.max(logits, axis=0))
        terms = jnp.sum(jnp.exp(logits - new[None]), axis=0)
        out_ref[1] = out_ref[1] * jnp.exp(old - new) + terms
        out_ref[0] = new


def vocab_scores(starts, gold, rows_in, weights, whole, begin, end, carried):
    count, n_w = len(rows_in), len(weights)
    n_cand = n_w // 2
    share, model = rows_in[0].shape
    depth = weights[0].shape[1]
    rows = share * count
    width = VOCAB_STEP
    first = begin // width
    constant = pl.BlockSpec((share, model), lambda i: (0, 0))
    stats = pl.BlockSpec((3, 8, rows), lambda i: (0, 0, 0))
    columns = [
        pl.BlockSpec((width, depth), lambda i: (first + i, 0))
        if is_whole
        else pl.BlockSpec((width, depth), lambda i: (i, 0))
        for is_whole in whole
    ]
    return pl.pallas_call(
        functools.partial(vocab_kernel, n_cand, count, len(carried), first, end),
        grid=(pl.cdiv(end - begin, width),),
        out_shape=jax.ShapeDtypeStruct((3, 8, rows), jnp.float32),
        in_specs=[smem_spec(), pl.BlockSpec((1, rows), lambda i: (0, 0))]
        + [constant] * count
        + columns
        + [stats] * len(carried),
        out_specs=stats,
        scratch_shapes=[VMEM((rows, model), jnp.bfloat16)],
        name="vocab_scores",
    )(starts, gold, *rows_in, *weights, *carried)


def body(
    dec_hidden,
    enc_keys,
    enc_values,
    enc_lengths,
    cand_counts,
    gold_ids,
    gain_cross,
    w_query,
    w_out,
    gain_ffn,
    w_in_gate,
    w_in_up,
    w_ffn_out,
    gain_final,
    w_vocab,
):
    queries, cand_dev, length, model = dec_hidden.shape
    n_tok, n_cand = lax.axis_size("tok"), lax.axis_size("cand")
    tok, cand = lax.axis_index("tok"), lax.axis_index("cand")
    core, chip = tok % 2, tok // 2
    chips = n_tok // 2
    rows = cand_dev * length
    share = rows // chips
    block = model // n_cand
    head_cols = w_query.shape[1]
    half = n_cand // 2
    assert queries == 2 and n_cand % 2 == 0 and n_tok % 4 == 0 and n_tok & (n_tok - 1) == 0

    def swap(a, k):
        return lax.ppermute(a, "tok", [(i, i ^ k) for i in range(n_tok)])

    def across(a, shift):
        return lax.ppermute(a, "cand", [(i, (i - shift) % n_cand) for i in range(n_cand)])

    def from_cands(a):
        return [a] + [across(a, s) for s in range(1, n_cand)]

    def with_partner(parts):
        own = swap(parts[0], 1)
        return parts + [own] + [swap(a, 1) for a in parts[1:]]

    def rolled(a):
        return jnp.concatenate(
            [
                lax.dynamic_slice_in_dim(a, ((cand + s) % n_cand) * block, block, a.ndim - 1)
                for s in range(n_cand)
            ],
            axis=-1,
        )

    def gather_rows(a):
        out = [None] * chips
        out[0] = a
        for j in range(2, chips, 2):
            out[j] = swap(a, 2 * j)
        for j in range(0, chips, 2):
            out[j + 1] = swap(out[j], 2)
        return out

    def scatter_rows(parts):
        return [parts[0]] + [swap(parts[j], 2 * j) for j in range(1, chips)]

    query_at = cand // half

    pair = jnp.stack(
        [
            lax.dynamic_index_in_dim(enc_keys, query_at, 0, keepdims=False),
            lax.dynamic_index_in_dim(enc_values, query_at, 0, keepdims=False),
        ]
    )
    pair = pair.reshape(2, pair.shape[1], n_tok, head_cols).transpose(2, 0, 1, 3)
    key_values = lax.all_to_all(pair, "tok", 0, 0, tiled=True)

    query_parts = from_cands(w_query)
    out_parts = with_partner(from_cands(w_out))
    gate_parts = with_partner(from_cands(w_in_gate.T))
    up_parts = with_partner(from_cands(w_in_up.T))
    down_parts = with_partner(from_cands(w_ffn_out))
    vocab_all = w_vocab.T
    vocab_dev = vocab_all.shape[0]
    cut = pl.cdiv(vocab_dev, VOCAB_STEP) // 2 * VOCAB_STEP
    vocab_low = from_cands(vocab_all[:cut])[1:]
    vocab_high = from_cands(vocab_all[cut:])[1:]
    vocab_other = swap(vocab_all, 1)
    low = [vocab_all] + vocab_low + [vocab_other] + [swap(w, 1) for w in vocab_low]
    high = [vocab_all] + vocab_high + [vocab_other] + [swap(w, 1) for w in vocab_high]

    flat = rolled(dec_hidden.reshape(queries * rows, model))
    wide = flat.astype(jnp.float32)
    gain_first, gain_mid, gain_last = (
        rolled(g.reshape(1, model)) for g in (gain_cross, gain_ffn, gain_final)
    )
    squares = jnp.mean(wide * wide, axis=-1, keepdims=True)
    normed = (wide * lax.rsqrt(squares + NORM_EPS) * gain_first).astype(jnp.bfloat16)
    query = sum(
        dot32(normed[:, s * block : (s + 1) * block], query_parts[s]) for s in range(n_cand)
    ).astype(jnp.bfloat16)
    query = query.reshape(queries, rows, head_cols)
    mine = lax.dynamic_index_in_dim(query, query_at, 0, keepdims=False)
    other = lax.dynamic_index_in_dim(query, 1 - query_at, 0, keepdims=False)
    peer = across(other, half)
    live = lax.dynamic_slice_in_dim(enc_lengths, query_at, 1, 0)
    attended = attention(live, mine, peer, key_values)

    def route(a, flip):
        perm = []
        for t in range(n_tok):
            for c in range(n_cand):
                to_half = (t % 2) ^ flip
                to = (t - t % 2 + c // half) * n_cand + c % half + to_half * half
                perm.append((t * n_cand + c, to))
        return lax.ppermute(a, ("tok", "cand"), perm)

    own_rows, peer_rows = attended[0], attended[1]
    straight = core == query_at
    first = route(jnp.where(straight, own_rows, peer_rows), 0)
    second = route(jnp.where(straight, peer_rows, own_rows), 1)
    att_own = jnp.where(straight, first, second)
    att_par = jnp.where(straight, second, first)
    chip_at = chip.reshape(1)
    cross_terms = project(chip_at, att_own, att_par, out_parts, chips)
    cross_terms = scatter_rows(cross_terms)
    base = lax.dynamic_slice_in_dim(flat, core * rows + chip * share, share, 0)
    normed_ffn, after_cross = residual_norm(base, gain_mid, cross_terms, True)
    ffn_rows = gather_rows(normed_ffn)
    ffn_terms = feed_forward(ffn_rows, gate_parts, up_parts, down_parts)
    ffn_terms = scatter_rows(ffn_terms)
    (normed_final,) = residual_norm(after_cross, gain_last, ffn_terms, False)
    final_rows = gather_rows(normed_final)

    order = chip ^ jnp.arange(chips)
    gold = lax.dynamic_index_in_dim(gold_ids, core, 0, keepdims=False).reshape(chips, share)
    gold = gold[order].reshape(1, rows)
    starts = jnp.stack([tok * vocab_dev, (tok ^ 1) * vocab_dev])
    whole = ([True] + [False] * (n_cand - 1)) * 2
    stats = vocab_scores(starts, gold, final_rows, low, whole, 0, cut, [])
    stats = vocab_scores(starts, gold, final_rows, high, whole, cut, vocab_dev, [stats])
    top = jnp.max(stats[0], axis=0)
    stats = jnp.stack(
        [top, jnp.sum(stats[1] * jnp.exp(stats[0] - top), axis=0), jnp.sum(stats[2], axis=0)]
    )
    stats = stats.reshape(3, chips, share)[:, order].reshape(3, rows)
    k = 2
    while k < n_tok:
        theirs = swap(stats, k)
        top = jnp.maximum(stats[0], theirs[0])
        total = stats[1] * jnp.exp(stats[0] - top) + theirs[1] * jnp.exp(theirs[0] - top)
        stats = jnp.stack([top, total, stats[2] + theirs[2]])
        k *= 2
    logprob = stats[2] - stats[0] - jnp.log(stats[1])
    per_cand = jnp.mean(logprob.reshape(cand_dev, length), axis=1)
    both = jnp.stack([per_cand, swap(per_cand, 1)])
    both = jnp.where(core == 0, both, both[::-1])
    cand_index = cand * cand_dev + lax.iota(jnp.int32, cand_dev)
    valid = cand_index[None, :] < cand_counts[:, None]
    cand_scores = jnp.where(valid, both, 0.0)
    best = jnp.max(jnp.where(valid, both, NEG), axis=1)
    k = 1
    while k < n_cand:
        best = jnp.maximum(
            best, lax.ppermute(best, "cand", [(i, i ^ k) for i in range(n_cand)])
        )
        k *= 2
    return (cand_scores, best)


def solution(mesh):
    in_specs = (
        P(None, "cand", None, None),
        P(None, "tok", None),
        P(None, "tok", None),
        P(),
        P(),
        P(None, "cand", None),
        P(),
        P("cand", "tok"),
        P("tok", "cand"),
        P(),
        P("cand", "tok"),
        P("cand", "tok"),
        P("tok", "cand"),
        P(),
        P("cand", "tok"),
    )
    out_specs = (P(None, "cand"), P())
    return jax.shard_map(body, mesh=mesh, in_specs=in_specs, out_specs=out_specs, check_vma=False)
```

profile of v0, /device:TPU:0, one launch (start us, length us, event | category | flops | bytes accessed | tf_op | source)
XLA Modules:
  0.0 330.8 jit_solution(14562997829187365541)
XLA Ops:
  0.6 3.0 collective-permute-start.4
  7.1 6.3 %all-to-all-start = ((bf16[16,2,128,128]{3,2,1,0:T(8,128)(2,1)}), bf16[16,2,128,128]{3,2,1,0:T(8,128)(2,1)S(1)}, u32[]{:S(2)}, u32[]{:S(2)}) async-start(bf16[16,2,128,128]{3,2,1,0:T(8,128)(2,1)} %bitcast.15), calls=%async_computation | async-start | bytes 2097152 | tf_op jit(solution)/shard_map/all_to_all | solution.py:350
  25.7 3.1 slice.101
  28.9 17.3 %collective-permute-done.1.peer_ref = bf16[256,128]{1,0:T(8,128)(2,1)S(1)} collective-permute-done((bf16[256,128]{1,0:T(8,128)(2,1)S(1)}, bf16[256,128]{1,0:T(8,128)(2,1)S(1)}, u32[]{:S(2)}, u32[]{:S(2)}) %collective-permute-start.1) | collective-permute-done | bytes 65568 | tf_op jit(solution)/shard_map/ppermute | solution.py:311
  47.6 3.1 slice.100
  55.6 6.8 %attention.1 = bf16[2,256,128]{2,1,0:T(8,128)(2,1)} custom-call(s32[1]{0:T(128)} %dynamic_slice.54.live_ref, bf16[256,128]{1,0:T(8,128)(2,1)} %get-tuple-element.58.mine_ref, bf16[256,128]{1,0:T(8,128)(2,1)} %copy-done.28, bf16[16,2,128,128]{3,2,1,0:T(8,128)(2,1)} %copy-done.1), custom_call_target="tpu_custom_call" | custom-call | tf_op jit(solution)/shard_map/attention/pallas_call | solution.py:73
  64.1 86.6 %collective-permute-done.27.refs_17_ = bf16[320,1024]{1,0:T(8,128)(2,1)} collective-permute-done((bf16[320,1024]{1,0:T(8,128)(2,1)}, bf16[320,1024]{1,0:T(8,128)(2,1)}, u32[]{:S(2)}, u32[]{:S(2)}) %collective-permute-start.27) | collective-permute-done | bytes 655392 | tf_op jit(solution)/shard_map/ppermute | solution.py:311
  155.5 2.9 project.1
  162.3 3.3 collective-permute-start.12
  166.1 11.1 %collective-permute-done.10.refs_4_ = bf16[32,2048]{1,0:T(8,128)(2,1)S(1)} collective-permute-done((bf16[32,2048]{1,0:T(8,128)(2,1)}, bf16[32,2048]{1,0:T(8,128)(2,1)S(1)}, u32[]{:S(2)}, u32[]{:S(2)}) %collective-permute-start.10) | collective-permute-done | bytes 131104 | tf_op jit(solution)/shard_map/ppermute | solution.py:308
  181.5 5.2 %collective-permute-start.8 = (bf16[32,2048]{1,0:T(8,128)(2,1)}, bf16[32,2048]{1,0:T(8,128)(2,1)}, u32[]{:S(2)}, u32[]{:S(2)}) collective-permute-start(bf16[32,2048]{1,0:T(8,128)(2,1)} %get-tuple-element.22), channel_id=1, source_target_pairs={{0,8},{2,10},{4,12},{6,14},{8,0},{10,2},{12,4},{14,6},{16,24},{18,... | collective-permute-start | bytes 393224 | tf_op jit(solution)/shard_map/ppermute | solution.py:308
  187.5 3.9 %collective-permute-done.8.refs_2_ = bf16[32,2048]{1,0:T(8,128)(2,1)} collective-permute-done((bf16[32,2048]{1,0:T(8,128)(2,1)}, bf16[32,2048]{1,0:T(8,128)(2,1)}, u32[]{:S(2)}, u32[]{:S(2)}) %collective-permute-start.8) | collective-permute-done | bytes 131104 | tf_op jit(solution)/shard_map/ppermute | solution.py:308
  200.4 5.0 %collective-permute-done.15.refs_2_ = bf16[32,2048]{1,0:T(8,128)(2,1)S(1)} collective-permute-done((bf16[32,2048]{1,0:T(8,128)(2,1)}, bf16[32,2048]{1,0:T(8,128)(2,1)S(1)}, u32[]{:S(2)}, u32[]{:S(2)}) %collective-permute-start.15) | collective-permute-done | bytes 131104 | tf_op jit(solution)/shard_map/ppermute | solution.py:308
  207.8 4.6 %collective-permute-done.19.refs_6_ = bf16[32,2048]{1,0:T(8,128)(2,1)S(1)} collective-permute-done((bf16[32,2048]{1,0:T(8,128)(2,1)}, bf16[32,2048]{1,0:T(8,128)(2,1)S(1)}, u32[]{:S(2)}, u32[]{:S(2)}) %collective-permute-start.19) | collective-permute-done | bytes 131104 | tf_op jit(solution)/shard_map/ppermute | solution.py:308
  214.5 4.1 %collective-permute-done.16.refs_3_ = bf16[32,2048]{1,0:T(8,128)(2,1)S(1)} collective-permute-done((bf16[32,2048]{1,0:T(8,128)(2,1)S(1)}, bf16[32,2048]{1,0:T(8,128)(2,1)S(1)}, u32[]{:S(2)}, u32[]{:S(2)}) %collective-permute-start.16) | collective-permute-done | bytes 131104 | tf_op jit(solution)/shard_map/ppermute | solution.py:308
  220.9 2.8 collective-permute-done.20.refs_7_
  223.7 7.4 %feed_forward.1 = (bf16[32,2048]{1,0:T(8,128)(2,1)}, bf16[32,2048]{1,0:T(8,128)(2,1)}, bf16[32,2048]{1,0:T(8,128)(2,1)}, bf16[32,2048]{1,0:T(8,128)(2,1)}, bf16[...) custom-call(bf16[32,2048]{1,0:T(8,128)(2,1)} %get-tuple-element.29.refs_0_,, ...), custom_call_target="tpu_custom_call" | custom-call | tf_op jit(solution)/shard_map/feed_forward/pallas_call | solution.py:192
  232.0 3.0 collective-permute-start.31
  236.4 3.3 collective-permute-start.32
  239.6 4.5 %collective-permute-start.33 = (bf16[32,2048]{1,0:T(8,128)(2,1)}, bf16[32,2048]{1,0:T(8,128)(2,1)S(1)}, u32[]{:S(2)}, u32[]{:S(2)}) collective-permute-start(bf16[32,2048]{1,0:T(8,128)(2,1)} %get-tuple-element.34), channel_id=1, source_target_pairs={{0,16},{2,18},{4,20},{6,22},{8,24},{10,26},{12,28},{14,30},{16,0},... | collective-permute-start | bytes 393224 | tf_op jit(solution)/shard_map/ppermute | solution.py:308
  244.1 3.6 %collective-permute-start.34 = (bf16[32,2048]{1,0:T(8,128)(2,1)}, bf16[32,2048]{1,0:T(8,128)(2,1)S(1)}, u32[]{:S(2)}, u32[]{:S(2)}) collective-permute-start(bf16[32,2048]{1,0:T(8,128)(2,1)} %get-tuple-element.35), channel_id=1, source_target_pairs={{0,20},{2,22},{4,16},{6,18},{8,28},{10,30},{12,24},{14,26},{16,4},... | collective-permute-start | bytes 393224 | tf_op jit(solution)/shard_map/ppermute | solution.py:308
  247.7 7.6 %collective-permute-done.33.refs_4_ = bf16[32,2048]{1,0:T(8,128)(2,1)S(1)} collective-permute-done((bf16[32,2048]{1,0:T(8,128)(2,1)}, bf16[32,2048]{1,0:T(8,128)(2,1)S(1)}, u32[]{:S(2)}, u32[]{:S(2)}) %collective-permute-start.33) | collective-permute-done | bytes 131104 | tf_op jit(solution)/shard_map/ppermute | solution.py:308
  256.6 3.7 %collective-permute-start.36 = (bf16[32,2048]{1,0:T(8,128)(2,1)}, bf16[32,2048]{1,0:T(8,128)(2,1)S(1)}, u32[]{:S(2)}, u32[]{:S(2)}) collective-permute-start(bf16[32,2048]{1,0:T(8,128)(2,1)} %get-tuple-element.37), channel_id=1, source_target_pairs={{0,28},{2,30},{4,24},{6,26},{8,20},{10,22},{12,16},{14,18},{16,12}... | collective-permute-start | bytes 393224 | tf_op jit(solution)/shard_map/ppermute | solution.py:308
  268.8 4.6 %collective-permute-start.40 = (bf16[32,2048]{1,0:T(8,128)(2,1)}, bf16[32,2048]{1,0:T(8,128)(2,1)S(1)}, u32[]{:S(2)}, u32[]{:S(2)}) collective-permute-start(bf16[32,2048]{1,0:T(8,128)(2,1)} %residual_norm.3.refs_0_), channel_id=1, source_target_pairs={{0,16},{2,18},{4,20},{6,22},{8,24},{10,26},{12,28},{14,30},{16,0},... | collective-permute-start | bytes 393224 | tf_op jit(solution)/shard_map/ppermute | solution.py:308
  273.4 6.0 %collective-permute-start.42 = (bf16[32,2048]{1,0:T(8,128)(2,1)}, bf16[32,2048]{1,0:T(8,128)(2,1)S(1)}, u32[]{:S(2)}, u32[]{:S(2)}) collective-permute-start(bf16[32,2048]{1,0:T(8,128)(2,1)} %residual_norm.3.refs_0_), channel_id=1, source_target_pairs={{0,24},{2,26},{4,28},{6,30},{8,16},{10,18},{12,20},{14,22},{16,8},... | collective-permute-start | bytes 393224 | tf_op jit(solution)/shard_map/ppermute | solution.py:308
  279.9 2.7 collective-permute-done.42.refs_6_
  282.6 3.5 %collective-permute-start.39 = (bf16[32,2048]{1,0:T(8,128)(2,1)S(1)}, bf16[32,2048]{1,0:T(8,128)(2,1)S(1)}, u32[]{:S(2)}, u32[]{:S(2)}) collective-permute-start(bf16[32,2048]{1,0:T(8,128)(2,1)S(1)} %collective-permute-done.38.refs_2_), channel_id=1, source_target_pairs={{0,4},{2,6},{4,0},{6,2},{8,12},{10,14},{12,8},{14,10},{16,20},{18,... | collective-permute-start | bytes 393224 | tf_op jit(solution)/shard_map/ppermute | solution.py:308
  296.0 6.9 %vocab_scores.2.refs_12_ = f32[3,8,256]{2,1,0:T(8,128)} custom-call(s32[2]{0:T(128)} %pad_add_fusion.start_ref, s32[1,256]{1,0:T(1,128)} %reshape.120.gold_ref, bf16[32,2048]{1,0:T(8,128)(2,1)} %residual_norm.3.refs_0_, bf16[32,2048]{1,0:T(8,128)(2,1)} %copy-done.8, bf16[32,2048]{1,0:T(8,128)(2,1)} %copy-done.5, bf16[32,2048]{1,0:T(8,128)(2,1)} %copy-done.9, ...), custom_call_target="tpu_custom_call" | custom-call | tf_op jit(solution)/shard_map/vocab_scores/pallas_call | solution.py:264
  303.0 6.9 %vocab_scores.3 = f32[3,8,256]{2,1,0:T(8,128)} custom-call(s32[2]{0:T(128)} %pad_add_fusion.start_ref, s32[1,256]{1,0:T(1,128)} %reshape.120.gold_ref, bf16[32,2048]{1,0:T(8,128)(2,1)} %residual_norm.3.refs_0_, bf16[32,2048]{1,0:T(8,128)(2,1)} %copy-done.8, bf16[32,2048]{1,0:T(8,128)(2,1)} %copy-done.5, bf16[32,2048]{1,0:T(8,128)(2,1)} %copy-done.9, ...), custom_call_target="tpu_custom_call" | custom-call | tf_op jit(solution)/shard_map/vocab_scores/pallas_call | solution.py:264
  316.1 3.6 %collective-permute-done.50 = f32[3,256]{1,0:T(4,128)S(1)} collective-permute-done((f32[3,256]{1,0:T(4,128)S(1)}, f32[3,256]{1,0:T(4,128)S(1)}, u32[]{:S(2)}, u32[]{:S(2)}) %collective-permute-start.50) | collective-permute-done | bytes 3104 | tf_op jit(solution)/shard_map/ppermute | solution.py:308
  321.1 3.2 collective-permute-done.51
  327.7 2.6 collective-permute-done.53
  (217 shorter events, 87.5 us)
Async XLA Ops:
  0.6 20.9 %collective-permute-start.4 = (bf16[128,1024]{1,0:T(8,128)(2,1)}, bf16[128,1024]{1,0:T(8,128)(2,1)S(1)}, u32[]{:S(2)}, u32[]{:S(2)}) collective-permute-start(bf16[128,1024]{1,0:T(8,128)(2,1)} %refs_0_.1), channel_id=1, source_target_pairs={{0,1},{1,0},{2,3},{3,2},{4,5},{5,4},{6,7},{7,6},{8,9},{9,8},{10,11... | collective-permute-start | bytes 786440 | tf_op jit(solution)/shard_map/ppermute | solution.py:311
  3.7 21.9 %collective-permute-start.5 = (bf16[128,1024]{1,0:T(8,128)(2,1)}, bf16[128,1024]{1,0:T(8,128)(2,1)}, u32[]{:S(2)}, u32[]{:S(2)}) collective-permute-start(bf16[128,1024]{1,0:T(8,128)(2,1)} %refs_0_.1), channel_id=1, source_target_pairs={{0,2},{2,0},{4,6},{6,4},{8,10},{10,8},{12,14},{14,12},{16,18},{18,... | collective-permute-start | bytes 786440 | tf_op jit(solution)/shard_map/ppermute | solution.py:308
  3.7 18.0 %collective-permute-start = (bf16[1024,128]{1,0:T(8,128)(2,1)}, bf16[1024,128]{1,0:T(8,128)(2,1)}, u32[]{:S(2)}, u32[]{:S(2)}) collective-permute-start(bf16[1024,128]{1,0:T(8,128)(2,1)} %param.22), channel_id=1, source_target_pairs={{0,1},{1,0},{2,3},{3,2},{4,5},{5,4},{6,7},{7,6},{8,9},{9,8},{10,11... | collective-permute-start | bytes 786440 | tf_op jit(solution)/shard_map/ppermute | solution.py:311
  7.1 47.5 %all-to-all-start = ((bf16[16,2,128,128]{3,2,1,0:T(8,128)(2,1)}), bf16[16,2,128,128]{3,2,1,0:T(8,128)(2,1)S(1)}, u32[]{:S(2)}, u32[]{:S(2)}) async-start(bf16[16,2,128,128]{3,2,1,0:T(8,128)(2,1)} %bitcast.15), calls=%async_computation | async-start | bytes 2097152 | tf_op jit(solution)/shard_map/all_to_all | solution.py:350
  13.4 38.5 %collective-permute-start.21 = (bf16[320,1024]{1,0:T(8,128)(2,1)}, bf16[320,1024]{1,0:T(8,128)(2,1)}, u32[]{:S(2)}, u32[]{:S(2)}) collective-permute-start(bf16[320,1024]{1,0:T(8,128)(2,1)} %bitcast.20.refs_8_), channel_id=1, source_target_pairs={{0,1},{1,0},{2,3},{3,2},{4,5},{5,4},{6,7},{7,6},{8,9},{9,8},{10,11... | collective-permute-start | bytes 1966088 | tf_op jit(solution)/shard_map/ppermute | solution.py:311
  15.0 37.0 %collective-permute-start.24 = (bf16[320,1024]{1,0:T(8,128)(2,1)}, bf16[320,1024]{1,0:T(8,128)(2,1)}, u32[]{:S(2)}, u32[]{:S(2)}) collective-permute-start(bf16[320,1024]{1,0:T(8,128)(2,1)} %bitcast.21.refs_12_), channel_id=1, source_target_pairs={{0,1},{1,0},{2,3},{3,2},{4,5},{5,4},{6,7},{7,6},{8,9},{9,8},{10,11... | collective-permute-start | bytes 1966088 | tf_op jit(solution)/shard_map/ppermute | solution.py:311
  21.6 29.1 %collective-permute-start.6 = (bf16[128,1024]{1,0:T(8,128)(2,1)S(1)}, bf16[128,1024]{1,0:T(8,128)(2,1)S(1)}, u32[]{:S(2)}, u32[]{:S(2)}) collective-permute-start(bf16[128,1024]{1,0:T(8,128)(2,1)S(1)} %collective-permute-done.4.refs_1_), channel_id=1, source_target_pairs={{0,2},{2,0},{4,6},{6,4},{8,10},{10,8},{12,14},{14,12},{16,18},{18,... | collective-permute-start | bytes 786440 | tf_op jit(solution)/shard_map/ppermute | solution.py:308
  24.0 22.1 %collective-permute-start.1 = (bf16[256,128]{1,0:T(8,128)(2,1)S(1)}, bf16[256,128]{1,0:T(8,128)(2,1)S(1)}, u32[]{:S(2)}, u32[]{:S(2)}) collective-permute-start(bf16[256,128]{1,0:T(8,128)(2,1)S(1)} %get-tuple-element.57), channel_id=1, source_target_pairs={{0,1},{1,0},{2,3},{3,2},{4,5},{5,4},{6,7},{7,6},{8,9},{9,8},{10,11... | collective-permute-start | bytes 196616 | tf_op jit(solution)/shard_map/ppermute | solution.py:311
  25.5 27.0 %collective-permute-start.22 = (bf16[320,1024]{1,0:T(8,128)(2,1)}, bf16[320,1024]{1,0:T(8,128)(2,1)}, u32[]{:S(2)}, u32[]{:S(2)}) collective-permute-start(bf16[320,1024]{1,0:T(8,128)(2,1)} %bitcast.20.refs_8_), channel_id=1, source_target_pairs={{0,2},{2,0},{4,6},{6,4},{8,10},{10,8},{12,14},{14,12},{16,18},{18,... | collective-permute-start | bytes 1966088 | tf_op jit(solution)/shard_map/ppermute | solution.py:308
  46.2 119.4 %collective-permute-start.47 = (bf16[1024,1024]{1,0:T(8,128)(2,1)}, bf16[1024,1024]{1,0:T(8,128)(2,1)}, u32[]{:S(2)}, u32[]{:S(2)}) collective-permute-start(bf16[1024,1024]{1,0:T(8,128)(2,1)} %slice.101), channel_id=1, source_target_pairs={{0,1},{1,0},{2,3},{3,2},{4,5},{5,4},{6,7},{7,6},{8,9},{9,8},{10,11... | collective-permute-start | bytes 6291464 | tf_op jit(solution)/shard_map/ppermute | solution.py:311
  51.4 110.9 %collective-permute-start.44 = (bf16[984,1024]{1,0:T(8,128)(2,1)}, bf16[984,1024]{1,0:T(8,128)(2,1)}, u32[]{:S(2)}, u32[]{:S(2)}) collective-permute-start(bf16[984,1024]{1,0:T(8,128)(2,1)} %slice.100), channel_id=1, source_target_pairs={{0,1},{1,0},{2,3},{3,2},{4,5},{5,4},{6,7},{7,6},{8,9},{9,8},{10,11... | collective-permute-start | bytes 6045704 | tf_op jit(solution)/shard_map/ppermute | solution.py:311
  52.0 242.0 %collective-permute-start.45 = (bf16[2008,1024]{1,0:T(8,128)(2,1)}, bf16[2008,1024]{1,0:T(8,128)(2,1)}, u32[]{:S(2)}, u32[]{:S(2)}) collective-permute-start(bf16[2008,1024]{1,0:T(8,128)(2,1)} %bitcast.22.refs_8_), channel_id=1, source_target_pairs={{0,2},{2,0},{4,6},{6,4},{8,10},{10,8},{12,14},{14,12},{16,18},{18,... | collective-permute-start | bytes 12337160 | tf_op jit(solution)/shard_map/ppermute | solution.py:308
  52.0 11.2 %collective-permute-start.25 = (bf16[320,1024]{1,0:T(8,128)(2,1)}, bf16[320,1024]{1,0:T(8,128)(2,1)}, u32[]{:S(2)}, u32[]{:S(2)}) collective-permute-start(bf16[320,1024]{1,0:T(8,128)(2,1)} %bitcast.21.refs_12_), channel_id=1, source_target_pairs={{0,2},{2,0},{4,6},{6,4},{8,10},{10,8},{12,14},{14,12},{16,18},{18,... | collective-permute-start | bytes 1966088 | tf_op jit(solution)/shard_map/ppermute | solution.py:308
  52.5 98.2 %collective-permute-start.27 = (bf16[320,1024]{1,0:T(8,128)(2,1)}, bf16[320,1024]{1,0:T(8,128)(2,1)}, u32[]{:S(2)}, u32[]{:S(2)}) collective-permute-start(bf16[320,1024]{1,0:T(8,128)(2,1)} %refs_16_.1), channel_id=1, source_target_pairs={{0,1},{1,0},{2,3},{3,2},{4,5},{5,4},{6,7},{7,6},{8,9},{9,8},{10,11... | collective-permute-start | bytes 1966088 | tf_op jit(solution)/shard_map/ppermute | solution.py:311
  63.2 89.7 %collective-permute-start.2 = (bf16[256,128]{1,0:T(8,128)(2,1)S(1)}, bf16[256,128]{1,0:T(8,128)(2,1)S(1)}, u32[]{:S(2)}, u32[]{:S(2)}) collective-permute-start(bf16[256,128]{1,0:T(8,128)(2,1)S(1)} %get-tuple-element.56), channel_id=1, source_target_pairs={{0,0},{1,2},{2,1},{3,3},{4,4},{5,6},{6,5},{7,7},{8,8},{9,10},{10,9... | collective-permute-start | bytes 196616 | tf_op jit(solution)/shard_map/ppermute | solution.py:390
  158.4 18.8 %collective-permute-start.10 = (bf16[32,2048]{1,0:T(8,128)(2,1)}, bf16[32,2048]{1,0:T(8,128)(2,1)S(1)}, u32[]{:S(2)}, u32[]{:S(2)}) collective-permute-start(bf16[32,2048]{1,0:T(8,128)(2,1)} %get-tuple-element.24), channel_id=1, source_target_pairs={{0,16},{2,18},{4,20},{6,22},{8,24},{10,26},{12,28},{14,30},{16,0},... | collective-permute-start | bytes 393224 | tf_op jit(solution)/shard_map/ppermute | solution.py:308
  160.9 20.2 %collective-permute-start.11 = (bf16[32,2048]{1,0:T(8,128)(2,1)}, bf16[32,2048]{1,0:T(8,128)(2,1)}, u32[]{:S(2)}, u32[]{:S(2)}) collective-permute-start(bf16[32,2048]{1,0:T(8,128)(2,1)} %get-tuple-element.25), channel_id=1, source_target_pairs={{0,20},{2,22},{4,16},{6,18},{8,28},{10,30},{12,24},{14,26},{16,4},... | collective-permute-start | bytes 393224 | tf_op jit(solution)/shard_map/ppermute | solution.py:308
  162.3 18.7 %collective-permute-start.12 = (bf16[32,2048]{1,0:T(8,128)(2,1)}, bf16[32,2048]{1,0:T(8,128)(2,1)}, u32[]{:S(2)}, u32[]{:S(2)}) collective-permute-start(bf16[32,2048]{1,0:T(8,128)(2,1)} %get-tuple-element.26), channel_id=1, source_target_pairs={{0,24},{2,26},{4,28},{6,30},{8,16},{10,18},{12,20},{14,22},{16,8},... | collective-permute-start | bytes 393224 | tf_op jit(solution)/shard_map/ppermute | solution.py:308
  165.6 15.9 %collective-permute-start.13 = (bf16[32,2048]{1,0:T(8,128)(2,1)}, bf16[32,2048]{1,0:T(8,128)(2,1)}, u32[]{:S(2)}, u32[]{:S(2)}) collective-permute-start(bf16[32,2048]{1,0:T(8,128)(2,1)} %get-tuple-element.27), channel_id=1, source_target_pairs={{0,28},{2,30},{4,24},{6,26},{8,20},{10,22},{12,16},{14,18},{16,12}... | collective-permute-start | bytes 393224 | tf_op jit(solution)/shard_map/ppermute | solution.py:308
  177.2 9.6 %collective-permute-start.7 = (bf16[32,2048]{1,0:T(8,128)(2,1)}, bf16[32,2048]{1,0:T(8,128)(2,1)}, u32[]{:S(2)}, u32[]{:S(2)}) collective-permute-start(bf16[32,2048]{1,0:T(8,128)(2,1)} %get-tuple-element.21), channel_id=1, source_target_pairs={{0,4},{2,6},{4,0},{6,2},{8,12},{10,14},{12,8},{14,10},{16,20},{18,... | collective-permute-start | bytes 393224 | tf_op jit(solution)/shard_map/ppermute | solution.py:308
  181.0 15.3 %collective-permute-start.26 = (bf16[320,1024]{1,0:T(8,128)(2,1)}, bf16[320,1024]{1,0:T(8,128)(2,1)}, u32[]{:S(2)}, u32[]{:S(2)}) collective-permute-start(bf16[320,1024]{1,0:T(8,128)(2,1)} %collective-permute-done.24.refs_13_), channel_id=1, source_target_pairs={{0,2},{2,0},{4,6},{6,4},{8,10},{10,8},{12,14},{14,12},{16,18},{18,... | collective-permute-start | bytes 1966088 | tf_op jit(solution)/shard_map/ppermute | solution.py:308
  181.0 17.1 %collective-permute-start.29 = (bf16[320,1024]{1,0:T(8,128)(2,1)}, bf16[320,1024]{1,0:T(8,128)(2,1)}, u32[]{:S(2)}, u32[]{:S(2)}) collective-permute-start(bf16[320,1024]{1,0:T(8,128)(2,1)} %collective-permute-done.27.refs_17_), channel_id=1, source_target_pairs={{0,2},{2,0},{4,6},{6,4},{8,10},{10,8},{12,14},{14,12},{16,18},{18,... | collective-permute-start | bytes 1966088 | tf_op jit(solution)/shard_map/ppermute | solution.py:308
  181.5 9.9 %collective-permute-start.8 = (bf16[32,2048]{1,0:T(8,128)(2,1)}, bf16[32,2048]{1,0:T(8,128)(2,1)}, u32[]{:S(2)}, u32[]{:S(2)}) collective-permute-start(bf16[32,2048]{1,0:T(8,128)(2,1)} %get-tuple-element.22), channel_id=1, source_target_pairs={{0,8},{2,10},{4,12},{6,14},{8,0},{10,2},{12,4},{14,6},{16,24},{18,... | collective-permute-start | bytes 393224 | tf_op jit(solution)/shard_map/ppermute | solution.py:308
  191.4 102.6 %collective-permute-start.48 = (bf16[1024,1024]{1,0:T(8,128)(2,1)}, bf16[1024,1024]{1,0:T(8,128)(2,1)S(1)}, u32[]{:S(2)}, u32[]{:S(2)}) collective-permute-start(bf16[1024,1024]{1,0:T(8,128)(2,1)} %collective-permute-done.47.refs_9_), channel_id=1, source_target_pairs={{0,2},{2,0},{4,6},{6,4},{8,10},{10,8},{12,14},{14,12},{16,18},{18,... | collective-permute-start | bytes 6291464 | tf_op jit(solution)/shard_map/ppermute | solution.py:308
  193.5 109.5 %collective-permute-start.46 = (bf16[984,1024]{1,0:T(8,128)(2,1)}, bf16[984,1024]{1,0:T(8,128)(2,1)}, u32[]{:S(2)}, u32[]{:S(2)}) collective-permute-start(bf16[984,1024]{1,0:T(8,128)(2,1)} %collective-permute-done.44.refs_9_), channel_id=1, source_target_pairs={{0,2},{2,0},{4,6},{6,4},{8,10},{10,8},{12,14},{14,12},{16,18},{18,... | collective-permute-start | bytes 6045704 | tf_op jit(solution)/shard_map/ppermute | solution.py:308
  196.4 9.0 %collective-permute-start.15 = (bf16[32,2048]{1,0:T(8,128)(2,1)}, bf16[32,2048]{1,0:T(8,128)(2,1)S(1)}, u32[]{:S(2)}, u32[]{:S(2)}) collective-permute-start(bf16[32,2048]{1,0:T(8,128)(2,1)} %get-tuple-element.29.refs_0_), channel_id=1, source_target_pairs={{0,8},{2,10},{4,12},{6,14},{8,0},{10,2},{12,4},{14,6},{16,24},{18,... | collective-permute-start | bytes 393224 | tf_op jit(solution)/shard_map/ppermute | solution.py:308
  198.2 8.3 %collective-permute-start.17 = (bf16[32,2048]{1,0:T(8,128)(2,1)}, bf16[32,2048]{1,0:T(8,128)(2,1)S(1)}, u32[]{:S(2)}, u32[]{:S(2)}) collective-permute-start(bf16[32,2048]{1,0:T(8,128)(2,1)} %get-tuple-element.29.refs_0_), channel_id=1, source_target_pairs={{0,16},{2,18},{4,20},{6,22},{8,24},{10,26},{12,28},{14,30},{16,0},... | collective-permute-start | bytes 393224 | tf_op jit(solution)/shard_map/ppermute | solution.py:308
  239.6 15.7 %collective-permute-start.33 = (bf16[32,2048]{1,0:T(8,128)(2,1)}, bf16[32,2048]{1,0:T(8,128)(2,1)S(1)}, u32[]{:S(2)}, u32[]{:S(2)}) collective-permute-start(bf16[32,2048]{1,0:T(8,128)(2,1)} %get-tuple-element.34), channel_id=1, source_target_pairs={{0,16},{2,18},{4,20},{6,22},{8,24},{10,26},{12,28},{14,30},{16,0},... | collective-permute-start | bytes 393224 | tf_op jit(solution)/shard_map/ppermute | solution.py:308
  244.1 12.5 %collective-permute-start.34 = (bf16[32,2048]{1,0:T(8,128)(2,1)}, bf16[32,2048]{1,0:T(8,128)(2,1)S(1)}, u32[]{:S(2)}, u32[]{:S(2)}) collective-permute-start(bf16[32,2048]{1,0:T(8,128)(2,1)} %get-tuple-element.35), channel_id=1, source_target_pairs={{0,20},{2,22},{4,16},{6,18},{8,28},{10,30},{12,24},{14,26},{16,4},... | collective-permute-start | bytes 393224 | tf_op jit(solution)/shard_map/ppermute | solution.py:308
  256.6 8.1 %collective-permute-start.36 = (bf16[32,2048]{1,0:T(8,128)(2,1)}, bf16[32,2048]{1,0:T(8,128)(2,1)S(1)}, u32[]{:S(2)}, u32[]{:S(2)}) collective-permute-start(bf16[32,2048]{1,0:T(8,128)(2,1)} %get-tuple-element.37), channel_id=1, source_target_pairs={{0,28},{2,30},{4,24},{6,26},{8,20},{10,22},{12,16},{14,18},{16,12}... | collective-permute-start | bytes 393224 | tf_op jit(solution)/shard_map/ppermute | solution.py:308
  268.8 10.6 %collective-permute-start.40 = (bf16[32,2048]{1,0:T(8,128)(2,1)}, bf16[32,2048]{1,0:T(8,128)(2,1)S(1)}, u32[]{:S(2)}, u32[]{:S(2)}) collective-permute-start(bf16[32,2048]{1,0:T(8,128)(2,1)} %residual_norm.3.refs_0_), channel_id=1, source_target_pairs={{0,16},{2,18},{4,20},{6,22},{8,24},{10,26},{12,28},{14,30},{16,0},... | collective-permute-start | bytes 393224 | tf_op jit(solution)/shard_map/ppermute | solution.py:308
  273.4 9.2 %collective-permute-start.42 = (bf16[32,2048]{1,0:T(8,128)(2,1)}, bf16[32,2048]{1,0:T(8,128)(2,1)S(1)}, u32[]{:S(2)}, u32[]{:S(2)}) collective-permute-start(bf16[32,2048]{1,0:T(8,128)(2,1)} %residual_norm.3.refs_0_), channel_id=1, source_target_pairs={{0,24},{2,26},{4,28},{6,30},{8,16},{10,18},{12,20},{14,22},{16,8},... | collective-permute-start | bytes 393224 | tf_op jit(solution)/shard_map/ppermute | solution.py:308
  (57 other events, 846.4 us)
where the time goes:
time: 332 us; the launch traced here: 331 us
  waiting for transfers between devices  174 us (52%)
  starting transfers between devices  87.2 us (26%)
  Pallas kernels  35.4 us (11%)
  local copies, waits for them, and re-layouts  20.6 us (6%)
  other arithmetic  9.52 us (3%)
  matrix products  3.41 us (1%)
    ppermute x8, waiting for transfers between devices, across(): lax.ppermute(a, 'cand', [(i, (i - shift) % n_cand) for i in range(n_cand)])  104 us
    ppermute x43, starting transfers between devices, swap(): return lax.ppermute(a, 'tok', [(i, i ^ k) for i in range(n_tok)])  66.6 us
    ppermute x43, waiting for transfers between devices, swap(): return lax.ppermute(a, 'tok', [(i, i ^ k) for i in range(n_tok)])  65.2 us
    pallas_call x2, Pallas kernels, vocab_scores(): pl.pallas_call(functools.partial(vocab_kernel, n_cand, count, len(carried...  13.9 us
    ppermute x8, starting transfers between devices, across(): lax.ppermute(a, 'cand', [(i, (i - shift) % n_cand) for i in range(n_cand)])  10.3 us
    pallas_call x1, Pallas kernels, feed_forward(): pl.pallas_call(functools.partial(ffn_kernel, n_cand, count), out_shape=[j...  7.4 us
    pallas_call x1, Pallas kernels, attention(): pl.pallas_call(attention_kernel, out_shape=jax.ShapeDtypeStruct((2, rows,...  6.79 us
  transfers between devices with their start and end apart: 55, of which 24 were waited for; matrix products, arithmetic and copies ran while one was open for 7% of the time, Pallas kernels for 9%

commit v1 on v0

--- a/solution.py
+++ b/solution.py
@@ -43,7 +43,7 @@
     return 0.5 * v * (1.0 + jnp.tanh(inner))
 
 
-def attention_kernel(live_ref, mine_ref, peer_ref, kv_ref, out_ref):
+def attention_kernel(live_ref, mine_ref, peer_ref, kv_ref, first_ref, second_ref):
     src = kv_ref.shape[0] * kv_ref.shape[2]
     cols = kv_ref.shape[3]
     keys = kv_ref[:, 0].reshape(src, cols)
@@ -53,9 +53,14 @@
     lane_head = lax.broadcasted_iota(jnp.int32, (1, cols), 1) // HEAD_DIM
     rows = mine_ref.shape[0]
     step = min(rows, 128)
-    for part, q_ref in enumerate((mine_ref, peer_ref)):
+    straight = live_ref[1] == 1
+    for out_ref, one_ref, two_ref in (
+        (first_ref, mine_ref, peer_ref),
+        (second_ref, peer_ref, mine_ref),
+    ):
         for start in range(0, rows, step):
-            q = q_ref[start : start + step, :]
+            at = slice(start, start + step)
+            q = jnp.where(straight, one_ref[at, :], two_ref[at, :])
             mixed = jnp.zeros((step, cols), jnp.float32)
             for head in range(cols // HEAD_DIM):
                 q_head = jnp.where(lane_head == head, q, jnp.zeros_like(q))
@@ -65,29 +70,32 @@
                 denominator = jnp.sum(weights, axis=-1, keepdims=True)
                 head_out = dot32(weights.astype(jnp.bfloat16), values) / denominator
                 mixed = jnp.where(lane_head == head, head_out, mixed)
-            out_ref[part, start : start + step, :] = mixed.astype(jnp.bfloat16)
+            out_ref[at, :] = mixed.astype(jnp.bfloat16)
 
 
 def attention(live, mine, peer, kv):
     rows, cols = mine.shape
     return pl.pallas_call(
         attention_kernel,
-        out_shape=jax.ShapeDtypeStruct((2, rows, cols), jnp.bfloat16),
+        out_shape=[jax.ShapeDtypeStruct((rows, cols), jnp.bfloat16)] * 2,
         in_specs=[smem_spec(), vmem_spec(), vmem_spec(), vmem_spec()],
-        out_specs=vmem_spec(),
+        out_specs=[vmem_spec()] * 2,
         name="attention",
     )(live, mine, peer, kv)
 
 
-def project_kernel(n_cand, count, chip_ref, own_ref, par_ref, *refs):
+def project_kernel(n_cand, count, chip_ref, first_ref, second_ref, *refs):
     weights = refs[: 2 * n_cand]
     outs = refs[2 * n_cand : 2 * n_cand + count]
     own_s, par_s = refs[2 * n_cand + count :]
-    share = own_ref.shape[0] // count
+    share = first_ref.shape[0] // count
+    straight = chip_ref[1] == 1
     for j in range(count):
         at = pl.multiple_of((chip_ref[0] ^ j) * share, share)
-        own_s[j * share : (j + 1) * share, :] = own_ref[pl.ds(at, share), :]
-        par_s[j * share : (j + 1) * share, :] = par_ref[pl.ds(at, share), :]
+        to = slice(j * share, (j + 1) * share)
+        first, second = first_ref[pl.ds(at, share), :], second_ref[pl.ds(at, share), :]
+        own_s[to, :] = jnp.where(straight, first, second)
+        par_s[to, :] = jnp.where(straight, second, first)
     own, par = own_s[...], par_s[...]
     width = weights[0].shape[1]
     for s in range(n_cand):
@@ -97,8 +105,8 @@
             outs[j][:, s * width : (s + 1) * width] = block[j * share : (j + 1) * share, :]
 
 
-def project(chip, own, par, weights, count):
-    rows, cols = own.shape
+def project(chip, first, second, weights, count):
+    rows, cols = first.shape
     n_cand = len(weights) // 2
     model = weights[0].shape[1] * n_cand
     return pl.pallas_call(
@@ -108,7 +116,7 @@
         out_specs=[vmem_spec()] * count,
         scratch_shapes=[VMEM((rows, cols), jnp.bfloat16)] * 2,
         name="project",
-    )(chip, own, par, *weights)
+    )(chip, first, second, *weights)
 
 
 def residual_kernel(count, base_ref, gain_ref, *refs):
@@ -336,7 +344,14 @@
         return out
 
     def scatter_rows(parts):
-        return [parts[0]] + [swap(parts[j], 2 * j) for j in range(1, chips)]
+        order = [j for j in range(2, chips, 2)]
+        order = order[1:] + order[:1] + [0]
+        near = {j: swap(parts[j + 1], 2) for j in order}
+        back = [parts[0], near[0]]
+        for j in order[:-1]:
+            pair = parts[j].astype(jnp.float32) + near[j].astype(jnp.float32)
+            back.append(swap(pair.astype(jnp.bfloat16), 2 * j))
+        return back
 
     query_at = cand // half
 
@@ -357,11 +372,8 @@
     vocab_all = w_vocab.T
     vocab_dev = vocab_all.shape[0]
     cut = pl.cdiv(vocab_dev, VOCAB_STEP) // 2 * VOCAB_STEP
-    vocab_low = from_cands(vocab_all[:cut])[1:]
-    vocab_high = from_cands(vocab_all[cut:])[1:]
+    vocab_low, vocab_high = vocab_all[:cut], vocab_all[cut:]
     vocab_other = swap(vocab_all, 1)
-    low = [vocab_all] + vocab_low + [vocab_other] + [swap(w, 1) for w in vocab_low]
-    high = [vocab_all] + vocab_high + [vocab_other] + [swap(w, 1) for w in vocab_high]
 
     flat = rolled(dec_hidden.reshape(queries * rows, model))
     wide = flat.astype(jnp.float32)
@@ -377,8 +389,10 @@
     mine = lax.dynamic_index_in_dim(query, query_at, 0, keepdims=False)
     other = lax.dynamic_index_in_dim(query, 1 - query_at, 0, keepdims=False)
     peer = across(other, half)
-    live = lax.dynamic_slice_in_dim(enc_lengths, query_at, 1, 0)
-    attended = attention(live, mine, peer, key_values)
+    straight = (core == query_at).astype(jnp.int32)
+    live = jnp.stack([lax.dynamic_index_in_dim(enc_lengths, query_at, 0, keepdims=False), straight])
+    live, vocab_low, vocab_high = lax.optimization_barrier((live, vocab_low, vocab_high))
+    first, second = attention(live, mine, peer, key_values)
 
     def route(a, flip):
         perm = []
@@ -389,14 +403,13 @@
                 perm.append((t * n_cand + c, to))
         return lax.ppermute(a, ("tok", "cand"), perm)
 
-    own_rows, peer_rows = attended[0], attended[1]
-    straight = core == query_at
-    first = route(jnp.where(straight, own_rows, peer_rows), 0)
-    second = route(jnp.where(straight, peer_rows, own_rows), 1)
-    att_own = jnp.where(straight, first, second)
-    att_par = jnp.where(straight, second, first)
-    chip_at = chip.reshape(1)
-    cross_terms = project(chip_at, att_own, att_par, out_parts, chips)
+    first, second = route(first, 0), route(second, 1)
+    chip_at = jnp.stack([chip, straight])
+    vocab_low = from_cands(vocab_low)[1:]
+    vocab_high = from_cands(vocab_high)[1:]
+    low = [vocab_all] + vocab_low + [vocab_other] + [swap(w, 1) for w in vocab_low]
+    high = [vocab_all] + vocab_high + [vocab_other] + [swap(w, 1) for w in vocab_high]
+    cross_terms = project(chip_at, first, second, out_parts, chips)
     cross_terms = scatter_rows(cross_terms)
     base = lax.dynamic_slice_in_dim(flat, core * rows + chip * share, share, 0)
     normed_ffn, after_cross = residual_norm(base, gain_mid, cross_terms, True)

time: 332 us -> 263 us (0.79)
  waiting for transfers between devices: 174 us -> 114 us
  starting transfers between devices: 87.2 us -> 75 us
  other arithmetic: 9.52 us -> 14.8 us
    ppermute x8, waiting for transfers between devices: 104 us -> 49.7 us  [across(): lax.ppermute(a, 'cand', [(i, (i - shift) % n_cand) for i in range(n_cand)])]
    ppermute x43, starting transfers between devices: 66.6 us -> 52 us  [swap(): return lax.ppermute(a, 'tok', [(i, i ^ k) for i in range(n_tok)])]
    convert_element_type x0 -> x6, other arithmetic: none -> 6.29 us  [scatter_rows(): back.append(swap(pair.astype(jnp.bfloat16), 2 * j))]
    ppermute x43, waiting for transfers between devices: 65.2 us -> 60.7 us  [swap(): return lax.ppermute(a, 'tok', [(i, i ^ k) for i in range(n_tok)])]
  transfers between devices with their start and end apart: 55 -> 55, of which waited for: 24 -> 27; matrix products, arithmetic and copies ran while one was open for 7% -> 11% of each run, Pallas kernels for 9% -> 10%
where the time goes in v1:
time: 263 us; the launch traced here: 262 us
  waiting for transfers between devices  114 us (43%)
  starting transfers between devices  75 us (29%)
  Pallas kernels  34.4 us (13%)
  local copies, waits for them, and re-layouts  21.1 us (8%)
  other arithmetic  14.8 us (6%)
    ppermute x43, waiting for transfers between devices, swap(): return lax.ppermute(a, 'tok', [(i, i ^ k) for i in range(n_tok)])  60.7 us
    ppermute x43, starting transfers between devices, swap(): return lax.ppermute(a, 'tok', [(i, i ^ k) for i in range(n_tok)])  52 us
    ppermute x8, waiting for transfers between devices, across(): lax.ppermute(a, 'cand', [(i, (i - shift) % n_cand) for i in range(n_cand)])  49.7 us
    pallas_call x2, Pallas kernels, vocab_scores(): pl.pallas_call(functools.partial(vocab_kernel, n_cand, count, len(carried...  13.8 us
    ppermute x8, starting transfers between devices, across(): lax.ppermute(a, 'cand', [(i, (i - shift) % n_cand) for i in range(n_cand)])  12.1 us
    pallas_call x1, Pallas kernels, feed_forward(): pl.pallas_call(functools.partial(ffn_kernel, n_cand, count), out_shape=[j...  7.34 us
    all_to_all x1, starting transfers between devices, body(): key_values = lax.all_to_all(pair, 'tok', 0, 0, tiled=True)  6.31 us
    convert_element_type x6, other arithmetic, scatter_rows(): back.append(swap(pair.astype(jnp.bfloat16), 2 * j))  6.29 us
  transfers between devices with their start and end apart: 55, of which 27 were waited for; matrix products, arithmetic and copies ran while one was open for 11% of the time, Pallas kernels for 10%

profile of v1, /device:TPU:0, one launch (start us, length us, event | category | flops | bytes accessed | tf_op | source)
XLA Modules:
  0.0 262.0 jit_solution(1327961844234586656)
XLA Ops:
  0.6 3.0 %collective-permute-start.21 = (bf16[320,1024]{1,0:T(8,128)(2,1)}, bf16[320,1024]{1,0:T(8,128)(2,1)}, u32[]{:S(2)}, u32[]{:S(2)}) collective-permute-start(bf16[320,1024]{1,0:T(8,128)(2,1)} %bitcast.80), channel_id=1, source_target_pairs={{0,1},{1,0},{2,3},{3,2},{4,5},{5,4},{6,7},{7,6},{8,9},{9,8},{10,11... | collective-permute-start | bytes 1966088 | tf_op jit(solution)/shard_map/ppermute | solution.py:319
  7.1 6.3 %all-to-all-start = ((bf16[16,2,128,128]{3,2,1,0:T(8,128)(2,1)}), bf16[16,2,128,128]{3,2,1,0:T(8,128)(2,1)S(1)}, u32[]{:S(2)}, u32[]{:S(2)}) async-start(bf16[16,2,128,128]{3,2,1,0:T(8,128)(2,1)} %bitcast.17), calls=%async_computation | async-start | bytes 2097152 | tf_op jit(solution)/shard_map/all_to_all | solution.py:365
  19.4 5.8 %collective-permute-done = bf16[1024,128]{1,0:T(8,128)(2,1)} collective-permute-done((bf16[1024,128]{1,0:T(8,128)(2,1)}, bf16[1024,128]{1,0:T(8,128)(2,1)}, u32[]{:S(2)}, u32[]{:S(2)}) %collective-permute-start) | collective-permute-done | bytes 262176 | tf_op jit(solution)/shard_map/ppermute | solution.py:319
  30.8 14.5 %collective-permute-done.1.peer_ref = bf16[256,128]{1,0:T(8,128)(2,1)S(1)} collective-permute-done((bf16[256,128]{1,0:T(8,128)(2,1)S(1)}, bf16[256,128]{1,0:T(8,128)(2,1)S(1)}, u32[]{:S(2)}, u32[]{:S(2)}) %collective-permute-start.1) | collective-permute-done | bytes 65568 | tf_op jit(solution)/shard_map/ppermute | solution.py:319
  45.3 3.1 %slice.88 = bf16[1024,1024]{1,0:T(8,128)(2,1)} slice(bf16[2008,1024]{1,0:T(8,128)(2,1)} %bitcast.73), slice={[0:1024], [0:1024]} | slice | bytes 4194304 | tf_op jit(solution)/shard_map/slice | solution.py:375
  48.5 3.1 %slice.89 = bf16[984,1024]{1,0:T(8,128)(2,1)} slice(bf16[2008,1024]{1,0:T(8,128)(2,1)} %bitcast.74), slice={[1024:2008], [0:1024]} | slice | bytes 4030464 | tf_op jit(solution)/shard_map/slice | solution.py:375
  54.5 6.2 %attention.1 = (bf16[256,128]{1,0:T(8,128)(2,1)}, bf16[256,128]{1,0:T(8,128)(2,1)}) custom-call(s32[2]{0:T(128)} %pad_add_fusion.2.live_ref, bf16[256,128]{1,0:T(8,128)(2,1)} %get-tuple-element.64.mine_ref, bf16[256,128]{1,0:T(8,128)(2,1)} %copy-done.26, bf16[16,2,128,128]{3,2,1,0:T(8,128)(2,1)} %copy-done.1), custom_call_target="tpu_custom_call" | custom-call | tf_op jit(solution)/shard_map/attention/pallas_call | solution.py:78
  64.9 3.3 %collective-permute-start.27 = (bf16[320,1024]{1,0:T(8,128)(2,1)}, bf16[320,1024]{1,0:T(8,128)(2,1)S(1)}, u32[]{:S(2)}, u32[]{:S(2)}) collective-permute-start(bf16[320,1024]{1,0:T(8,128)(2,1)} %refs_16_.1), channel_id=1, source_target_pairs={{0,1},{1,0},{2,3},{3,2},{4,5},{5,4},{6,7},{7,6},{8,9},{9,8},{10,11... | collective-permute-start | bytes 1966088 | tf_op jit(solution)/shard_map/ppermute | solution.py:319
  68.8 2.9 %project.1 = (bf16[32,2048]{1,0:T(8,128)(2,1)}, bf16[32,2048]{1,0:T(8,128)(2,1)}, bf16[32,2048]{1,0:T(8,128)(2,1)}, bf16[32,2048]{1,0:T(8,128)(2,1)}, bf16[32,20...) custom-call(s32[2]{0:T(128)} %pad_add_fusion.1.chip_ref, ...), custom_call_target="tpu_custom_call" | custom-call | tf_op jit(solution)/shard_map/project/pallas_call | solution.py:112
  73.6 4.4 %collective-permute-done.12 = bf16[32,2048]{1,0:T(8,128)(2,1)S(1)} collective-permute-done((bf16[32,2048]{1,0:T(8,128)(2,1)}, bf16[32,2048]{1,0:T(8,128)(2,1)S(1)}, u32[]{:S(2)}, u32[]{:S(2)}) %collective-permute-start.12) | collective-permute-done | bytes 131104 | tf_op jit(solution)/shard_map/ppermute | solution.py:316
  84.0 3.2 %collective-permute-start.8 = (bf16[32,2048]{1,0:T(8,128)(2,1)}, bf16[32,2048]{1,0:T(8,128)(2,1)S(1)}, u32[]{:S(2)}, u32[]{:S(2)}) collective-permute-start(bf16[32,2048]{1,0:T(8,128)(2,1)} %get-tuple-element.31), channel_id=1, source_target_pairs={{0,4},{2,6},{4,0},{6,2},{8,12},{10,14},{12,8},{14,10},{16,20},{18,... | collective-permute-start | bytes 393224 | tf_op jit(solution)/shard_map/ppermute | solution.py:316
  88.3 2.8 %collective-permute-done.8 = bf16[32,2048]{1,0:T(8,128)(2,1)S(1)} collective-permute-done((bf16[32,2048]{1,0:T(8,128)(2,1)}, bf16[32,2048]{1,0:T(8,128)(2,1)S(1)}, u32[]{:S(2)}, u32[]{:S(2)}) %collective-permute-start.8) | collective-permute-done | bytes 131104 | tf_op jit(solution)/shard_map/ppermute | solution.py:316
  92.7 3.4 %collective-permute-start.11 = (bf16[32,2048]{1,0:T(8,128)(2,1)S(1)}, bf16[32,2048]{1,0:T(8,128)(2,1)}, u32[]{:S(2)}, u32[]{:S(2)}) collective-permute-start(bf16[32,2048]{1,0:T(8,128)(2,1)S(1)} %add_convert_fusion.4), channel_id=1, source_target_pairs={{0,24},{2,26},{4,28},{6,30},{8,16},{10,18},{12,20},{14,22},{16,8},... | collective-permute-start | bytes 393224 | tf_op jit(solution)/shard_map/ppermute | solution.py:316
  100.9 4.9 %collective-permute-done.9.refs_2_ = bf16[32,2048]{1,0:T(8,128)(2,1)} collective-permute-done((bf16[32,2048]{1,0:T(8,128)(2,1)}, bf16[32,2048]{1,0:T(8,128)(2,1)}, u32[]{:S(2)}, u32[]{:S(2)}) %collective-permute-start.9) | collective-permute-done | bytes 131104 | tf_op jit(solution)/shard_map/ppermute | solution.py:316
  110.5 3.4 %collective-permute-start.17 = (bf16[32,2048]{1,0:T(8,128)(2,1)}, bf16[32,2048]{1,0:T(8,128)(2,1)S(1)}, u32[]{:S(2)}, u32[]{:S(2)}) collective-permute-start(bf16[32,2048]{1,0:T(8,128)(2,1)} %get-tuple-element.37.refs_0_), channel_id=1, source_target_pairs={{0,16},{2,18},{4,20},{6,22},{8,24},{10,26},{12,28},{14,30},{16,0},... | collective-permute-start | bytes 393224 | tf_op jit(solution)/shard_map/ppermute | solution.py:316
  113.9 4.7 %collective-permute-done.15.refs_2_ = bf16[32,2048]{1,0:T(8,128)(2,1)S(1)} collective-permute-done((bf16[32,2048]{1,0:T(8,128)(2,1)}, bf16[32,2048]{1,0:T(8,128)(2,1)S(1)}, u32[]{:S(2)}, u32[]{:S(2)}) %collective-permute-start.15) | collective-permute-done | bytes 131104 | tf_op jit(solution)/shard_map/ppermute | solution.py:316
  122.7 3.2 %collective-permute-done.19.refs_6_ = bf16[32,2048]{1,0:T(8,128)(2,1)S(1)} collective-permute-done((bf16[32,2048]{1,0:T(8,128)(2,1)}, bf16[32,2048]{1,0:T(8,128)(2,1)S(1)}, u32[]{:S(2)}, u32[]{:S(2)}) %collective-permute-start.19) | collective-permute-done | bytes 131104 | tf_op jit(solution)/shard_map/ppermute | solution.py:316
  127.9 3.7 %collective-permute-done.16.refs_3_ = bf16[32,2048]{1,0:T(8,128)(2,1)S(1)} collective-permute-done((bf16[32,2048]{1,0:T(8,128)(2,1)S(1)}, bf16[32,2048]{1,0:T(8,128)(2,1)S(1)}, u32[]{:S(2)}, u32[]{:S(2)}) %collective-permute-start.16) | collective-permute-done | bytes 131104 | tf_op jit(solution)/shard_map/ppermute | solution.py:316
  137.3 7.3 %feed_forward.1 = (bf16[32,2048]{1,0:T(8,128)(2,1)}, bf16[32,2048]{1,0:T(8,128)(2,1)}, bf16[32,2048]{1,0:T(8,128)(2,1)}, bf16[32,2048]{1,0:T(8,128)(2,1)}, bf16[...) custom-call(bf16[32,2048]{1,0:T(8,128)(2,1)} %get-tuple-element.37.refs_0_,, ...), custom_call_target="tpu_custom_call" | custom-call | tf_op jit(solution)/shard_map/feed_forward/pallas_call | solution.py:200
  146.2 25.8 %collective-permute-done.44.refs_9_ = bf16[984,1024]{1,0:T(8,128)(2,1)} collective-permute-done((bf16[984,1024]{1,0:T(8,128)(2,1)}, bf16[984,1024]{1,0:T(8,128)(2,1)}, u32[]{:S(2)}, u32[]{:S(2)}) %collective-permute-start.44) | collective-permute-done | bytes 2015264 | tf_op jit(solution)/shard_map/ppermute | solution.py:319
  175.5 3.6 %collective-permute-done.33 = bf16[32,2048]{1,0:T(8,128)(2,1)S(1)} collective-permute-done((bf16[32,2048]{1,0:T(8,128)(2,1)}, bf16[32,2048]{1,0:T(8,128)(2,1)S(1)}, u32[]{:S(2)}, u32[]{:S(2)}) %collective-permute-start.33) | collective-permute-done | bytes 131104 | tf_op jit(solution)/shard_map/ppermute | solution.py:316
  184.5 3.6 %collective-permute-start.34 = (bf16[32,2048]{1,0:T(8,128)(2,1)S(1)}, bf16[32,2048]{1,0:T(8,128)(2,1)S(1)}, u32[]{:S(2)}, u32[]{:S(2)}) collective-permute-start(bf16[32,2048]{1,0:T(8,128)(2,1)S(1)} %add_convert_fusion.1), channel_id=1, source_target_pairs={{0,24},{2,26},{4,28},{6,30},{8,16},{10,18},{12,20},{14,22},{16,8},... | collective-permute-start | bytes 393224 | tf_op jit(solution)/shard_map/ppermute | solution.py:316
  188.1 2.8 %collective-permute-start.32 = (bf16[32,2048]{1,0:T(8,128)(2,1)S(1)}, bf16[32,2048]{1,0:T(8,128)(2,1)S(1)}, u32[]{:S(2)}, u32[]{:S(2)}) collective-permute-start(bf16[32,2048]{1,0:T(8,128)(2,1)S(1)} %add_convert_fusion.2), channel_id=1, source_target_pairs={{0,16},{2,18},{4,20},{6,22},{8,24},{10,26},{12,28},{14,30},{16,0},... | collective-permute-start | bytes 393224 | tf_op jit(solution)/shard_map/ppermute | solution.py:316
  192.6 5.0 %collective-permute-done.32.refs_2_ = bf16[32,2048]{1,0:T(8,128)(2,1)S(1)} collective-permute-done((bf16[32,2048]{1,0:T(8,128)(2,1)S(1)}, bf16[32,2048]{1,0:T(8,128)(2,1)S(1)}, u32[]{:S(2)}, u32[]{:S(2)}) %collective-permute-start.32) | collective-permute-done | bytes 131104 | tf_op jit(solution)/shard_map/ppermute | solution.py:316
  200.3 3.2 %collective-permute-start.40 = (bf16[32,2048]{1,0:T(8,128)(2,1)}, bf16[32,2048]{1,0:T(8,128)(2,1)S(1)}, u32[]{:S(2)}, u32[]{:S(2)}) collective-permute-start(bf16[32,2048]{1,0:T(8,128)(2,1)} %residual_norm.3.refs_0_), channel_id=1, source_target_pairs={{0,16},{2,18},{4,20},{6,22},{8,24},{10,26},{12,28},{14,30},{16,0},... | collective-permute-start | bytes 393224 | tf_op jit(solution)/shard_map/ppermute | solution.py:316
  203.5 3.7 %collective-permute-done.38.refs_2_ = bf16[32,2048]{1,0:T(8,128)(2,1)S(1)} collective-permute-done((bf16[32,2048]{1,0:T(8,128)(2,1)}, bf16[32,2048]{1,0:T(8,128)(2,1)S(1)}, u32[]{:S(2)}, u32[]{:S(2)}) %collective-permute-start.38) | collective-permute-done | bytes 131104 | tf_op jit(solution)/shard_map/ppermute | solution.py:316
  210.7 3.5 %collective-permute-done.42.refs_6_ = bf16[32,2048]{1,0:T(8,128)(2,1)S(1)} collective-permute-done((bf16[32,2048]{1,0:T(8,128)(2,1)}, bf16[32,2048]{1,0:T(8,128)(2,1)S(1)}, u32[]{:S(2)}, u32[]{:S(2)}) %collective-permute-start.42) | collective-permute-done | bytes 131104 | tf_op jit(solution)/shard_map/ppermute | solution.py:316
  216.4 3.9 %collective-permute-done.39.refs_3_ = bf16[32,2048]{1,0:T(8,128)(2,1)S(1)} collective-permute-done((bf16[32,2048]{1,0:T(8,128)(2,1)S(1)}, bf16[32,2048]{1,0:T(8,128)(2,1)S(1)}, u32[]{:S(2)}, u32[]{:S(2)}) %collective-permute-start.39) | collective-permute-done | bytes 131104 | tf_op jit(solution)/shard_map/ppermute | solution.py:316
  227.2 6.9 %vocab_scores.2.refs_12_ = f32[3,8,256]{2,1,0:T(8,128)} custom-call(s32[2]{0:T(128)} %pad_add_fusion.start_ref, s32[1,256]{1,0:T(1,128)} %reshape.113.gold_ref, bf16[32,2048]{1,0:T(8,128)(2,1)} %residual_norm.3.refs_0_, bf16[32,2048]{1,0:T(8,128)(2,1)} %copy-done.8, bf16[32,2048]{1,0:T(8,128)(2,1)} %copy-done.5, bf16[32,2048]{1,0:T(8,128)(2,1)} %copy-done.9, ...), custom_call_target="tpu_custom_call" | custom-call | tf_op jit(solution)/shard_map/vocab_scores/pallas_call | solution.py:272
  234.2 6.9 %vocab_scores.3 = f32[3,8,256]{2,1,0:T(8,128)} custom-call(s32[2]{0:T(128)} %pad_add_fusion.start_ref, s32[1,256]{1,0:T(1,128)} %reshape.113.gold_ref, bf16[32,2048]{1,0:T(8,128)(2,1)} %residual_norm.3.refs_0_, bf16[32,2048]{1,0:T(8,128)(2,1)} %copy-done.8, bf16[32,2048]{1,0:T(8,128)(2,1)} %copy-done.5, bf16[32,2048]{1,0:T(8,128)(2,1)} %copy-done.9, ...), custom_call_target="tpu_custom_call" | custom-call | tf_op jit(solution)/shard_map/vocab_scores/pallas_call | solution.py:272
  247.2 3.6 %collective-permute-done.50 = f32[3,256]{1,0:T(4,128)S(1)} collective-permute-done((f32[3,256]{1,0:T(4,128)S(1)}, f32[3,256]{1,0:T(4,128)S(1)}, u32[]{:S(2)}, u32[]{:S(2)}) %collective-permute-start.50) | collective-permute-done | bytes 3104 | tf_op jit(solution)/shard_map/ppermute | solution.py:316
  258.2 3.3 %collective-permute-done.53 = f32[2]{0:T(128)S(1)} collective-permute-done((f32[2]{0:T(128)S(1)}, f32[2]{0:T(128)S(1)}, u32[]{:S(2)}, u32[]{:S(2)}) %collective-permute-start.53) | collective-permute-done | bytes 40 | tf_op jit(solution)/shard_map/ppermute | solution.py:452
  (221 shorter events, 95.8 us)
Async XLA Ops:
  0.6 64.2 %collective-permute-start.21 = (bf16[320,1024]{1,0:T(8,128)(2,1)}, bf16[320,1024]{1,0:T(8,128)(2,1)}, u32[]{:S(2)}, u32[]{:S(2)}) collective-permute-start(bf16[320,1024]{1,0:T(8,128)(2,1)} %bitcast.80), channel_id=1, source_target_pairs={{0,1},{1,0},{2,3},{3,2},{4,5},{5,4},{6,7},{7,6},{8,9},{9,8},{10,11... | collective-permute-start | bytes 1966088 | tf_op jit(solution)/shard_map/ppermute | solution.py:319
  3.7 69.7 %collective-permute-start.22 = (bf16[320,1024]{1,0:T(8,128)(2,1)}, bf16[320,1024]{1,0:T(8,128)(2,1)}, u32[]{:S(2)}, u32[]{:S(2)}) collective-permute-start(bf16[320,1024]{1,0:T(8,128)(2,1)} %bitcast.81), channel_id=1, source_target_pairs={{0,2},{2,0},{4,6},{6,4},{8,10},{10,8},{12,14},{14,12},{16,18},{18,... | collective-permute-start | bytes 1966088 | tf_op jit(solution)/shard_map/ppermute | solution.py:316
  3.7 21.5 %collective-permute-start = (bf16[1024,128]{1,0:T(8,128)(2,1)}, bf16[1024,128]{1,0:T(8,128)(2,1)}, u32[]{:S(2)}, u32[]{:S(2)}) collective-permute-start(bf16[1024,128]{1,0:T(8,128)(2,1)} %param.22), channel_id=1, source_target_pairs={{0,1},{1,0},{2,3},{3,2},{4,5},{5,4},{6,7},{7,6},{8,9},{9,8},{10,11... | collective-permute-start | bytes 786440 | tf_op jit(solution)/shard_map/ppermute | solution.py:319
  7.1 46.3 %all-to-all-start = ((bf16[16,2,128,128]{3,2,1,0:T(8,128)(2,1)}), bf16[16,2,128,128]{3,2,1,0:T(8,128)(2,1)S(1)}, u32[]{:S(2)}, u32[]{:S(2)}) async-start(bf16[16,2,128,128]{3,2,1,0:T(8,128)(2,1)} %bitcast.17), calls=%async_computation | async-start | bytes 2097152 | tf_op jit(solution)/shard_map/all_to_all | solution.py:365
  13.5 17.3 %collective-permute-start.4 = (bf16[128,1024]{1,0:T(8,128)(2,1)S(1)}, bf16[128,1024]{1,0:T(8,128)(2,1)}, u32[]{:S(2)}, u32[]{:S(2)}) collective-permute-start(bf16[128,1024]{1,0:T(8,128)(2,1)S(1)} %copy-done.12), channel_id=1, source_target_pairs={{0,1},{1,0},{2,3},{3,2},{4,5},{5,4},{6,7},{7,6},{8,9},{9,8},{10,11... | collective-permute-start | bytes 786440 | tf_op jit(solution)/shard_map/ppermute | solution.py:319
  15.0 56.7 %collective-permute-start.24 = (bf16[320,1024]{1,0:T(8,128)(2,1)}, bf16[320,1024]{1,0:T(8,128)(2,1)}, u32[]{:S(2)}, u32[]{:S(2)}) collective-permute-start(bf16[320,1024]{1,0:T(8,128)(2,1)} %bitcast.21.refs_12_), channel_id=1, source_target_pairs={{0,1},{1,0},{2,3},{3,2},{4,5},{5,4},{6,7},{7,6},{8,9},{9,8},{10,11... | collective-permute-start | bytes 1966088 | tf_op jit(solution)/shard_map/ppermute | solution.py:319
  27.2 18.1 %collective-permute-start.1 = (bf16[256,128]{1,0:T(8,128)(2,1)S(1)}, bf16[256,128]{1,0:T(8,128)(2,1)S(1)}, u32[]{:S(2)}, u32[]{:S(2)}) collective-permute-start(bf16[256,128]{1,0:T(8,128)(2,1)S(1)} %get-tuple-element.63), channel_id=1, source_target_pairs={{0,1},{1,0},{2,3},{3,2},{4,5},{5,4},{6,7},{7,6},{8,9},{9,8},{10,11... | collective-permute-start | bytes 196616 | tf_op jit(solution)/shard_map/ppermute | solution.py:319
  30.8 29.8 %collective-permute-start.5 = (bf16[128,1024]{1,0:T(8,128)(2,1)S(1)}, bf16[128,1024]{1,0:T(8,128)(2,1)}, u32[]{:S(2)}, u32[]{:S(2)}) collective-permute-start(bf16[128,1024]{1,0:T(8,128)(2,1)S(1)} %copy-done.12), channel_id=1, source_target_pairs={{0,2},{2,0},{4,6},{6,4},{8,10},{10,8},{12,14},{14,12},{16,18},{18,... | collective-permute-start | bytes 786440 | tf_op jit(solution)/shard_map/ppermute | solution.py:316
  45.3 16.8 %collective-permute-start.6 = (bf16[128,1024]{1,0:T(8,128)(2,1)}, bf16[128,1024]{1,0:T(8,128)(2,1)}, u32[]{:S(2)}, u32[]{:S(2)}) collective-permute-start(bf16[128,1024]{1,0:T(8,128)(2,1)} %collective-permute-done.4.refs_1_), channel_id=1, source_target_pairs={{0,2},{2,0},{4,6},{6,4},{8,10},{10,8},{12,14},{14,12},{16,18},{18,... | collective-permute-start | bytes 786440 | tf_op jit(solution)/shard_map/ppermute | solution.py:316
  64.9 15.5 %collective-permute-start.25 = (bf16[320,1024]{1,0:T(8,128)(2,1)}, bf16[320,1024]{1,0:T(8,128)(2,1)S(1)}, u32[]{:S(2)}, u32[]{:S(2)}) collective-permute-start(bf16[320,1024]{1,0:T(8,128)(2,1)} %bitcast.21.refs_12_), channel_id=1, source_target_pairs={{0,2},{2,0},{4,6},{6,4},{8,10},{10,8},{12,14},{14,12},{16,18},{18,... | collective-permute-start | bytes 1966088 | tf_op jit(solution)/shard_map/ppermute | solution.py:316
  64.9 19.1 %collective-permute-start.27 = (bf16[320,1024]{1,0:T(8,128)(2,1)}, bf16[320,1024]{1,0:T(8,128)(2,1)S(1)}, u32[]{:S(2)}, u32[]{:S(2)}) collective-permute-start(bf16[320,1024]{1,0:T(8,128)(2,1)} %refs_16_.1), channel_id=1, source_target_pairs={{0,1},{1,0},{2,3},{3,2},{4,5},{5,4},{6,7},{7,6},{8,9},{9,8},{10,11... | collective-permute-start | bytes 1966088 | tf_op jit(solution)/shard_map/ppermute | solution.py:319
  68.2 15.9 %collective-permute-start.28 = (bf16[320,1024]{1,0:T(8,128)(2,1)}, bf16[320,1024]{1,0:T(8,128)(2,1)}, u32[]{:S(2)}, u32[]{:S(2)}) collective-permute-start(bf16[320,1024]{1,0:T(8,128)(2,1)} %refs_16_.1), channel_id=1, source_target_pairs={{0,2},{2,0},{4,6},{6,4},{8,10},{10,8},{12,14},{14,12},{16,18},{18,... | collective-permute-start | bytes 1966088 | tf_op jit(solution)/shard_map/ppermute | solution.py:316
  73.3 14.9 %collective-permute-start.23 = (bf16[320,1024]{1,0:T(8,128)(2,1)}, bf16[320,1024]{1,0:T(8,128)(2,1)}, u32[]{:S(2)}, u32[]{:S(2)}) collective-permute-start(bf16[320,1024]{1,0:T(8,128)(2,1)} %collective-permute-done.21.refs_9_), channel_id=1, source_target_pairs={{0,2},{2,0},{4,6},{6,4},{8,10},{10,8},{12,14},{14,12},{16,18},{18,... | collective-permute-start | bytes 1966088 | tf_op jit(solution)/shard_map/ppermute | solution.py:316
  77.9 9.3 %collective-permute-start.10 = (bf16[32,2048]{1,0:T(8,128)(2,1)}, bf16[32,2048]{1,0:T(8,128)(2,1)S(1)}, u32[]{:S(2)}, u32[]{:S(2)}) collective-permute-start(bf16[32,2048]{1,0:T(8,128)(2,1)} %get-tuple-element.33), channel_id=1, source_target_pairs={{0,4},{2,6},{4,0},{6,2},{8,12},{10,14},{12,8},{14,10},{16,20},{18,... | collective-permute-start | bytes 393224 | tf_op jit(solution)/shard_map/ppermute | solution.py:316
  80.4 91.6 %collective-permute-start.47 = (bf16[1024,1024]{1,0:T(8,128)(2,1)}, bf16[1024,1024]{1,0:T(8,128)(2,1)}, u32[]{:S(2)}, u32[]{:S(2)}) collective-permute-start(bf16[1024,1024]{1,0:T(8,128)(2,1)} %slice.88), channel_id=1, source_target_pairs={{0,1},{1,0},{2,3},{3,2},{4,5},{5,4},{6,7},{7,6},{8,9},{9,8},{10,11... | collective-permute-start | bytes 6291464 | tf_op jit(solution)/shard_map/ppermute | solution.py:319
  84.0 88.0 %collective-permute-start.44 = (bf16[984,1024]{1,0:T(8,128)(2,1)}, bf16[984,1024]{1,0:T(8,128)(2,1)}, u32[]{:S(2)}, u32[]{:S(2)}) collective-permute-start(bf16[984,1024]{1,0:T(8,128)(2,1)} %slice.89), channel_id=1, source_target_pairs={{0,1},{1,0},{2,3},{3,2},{4,5},{5,4},{6,7},{7,6},{8,9},{9,8},{10,11... | collective-permute-start | bytes 6045704 | tf_op jit(solution)/shard_map/ppermute | solution.py:319
  84.0 7.1 %collective-permute-start.8 = (bf16[32,2048]{1,0:T(8,128)(2,1)}, bf16[32,2048]{1,0:T(8,128)(2,1)S(1)}, u32[]{:S(2)}, u32[]{:S(2)}) collective-permute-start(bf16[32,2048]{1,0:T(8,128)(2,1)} %get-tuple-element.31), channel_id=1, source_target_pairs={{0,4},{2,6},{4,0},{6,2},{8,12},{10,14},{12,8},{14,10},{16,20},{18,... | collective-permute-start | bytes 393224 | tf_op jit(solution)/shard_map/ppermute | solution.py:316
  88.2 137.0 %collective-permute-start.45 = (bf16[2008,1024]{1,0:T(8,128)(2,1)}, bf16[2008,1024]{1,0:T(8,128)(2,1)}, u32[]{:S(2)}, u32[]{:S(2)}) collective-permute-start(bf16[2008,1024]{1,0:T(8,128)(2,1)} %bitcast.75), channel_id=1, source_target_pairs={{0,2},{2,0},{4,6},{6,4},{8,10},{10,8},{12,14},{14,12},{16,18},{18,... | collective-permute-start | bytes 12337160 | tf_op jit(solution)/shard_map/ppermute | solution.py:316
  92.7 8.2 %collective-permute-start.11 = (bf16[32,2048]{1,0:T(8,128)(2,1)S(1)}, bf16[32,2048]{1,0:T(8,128)(2,1)}, u32[]{:S(2)}, u32[]{:S(2)}) collective-permute-start(bf16[32,2048]{1,0:T(8,128)(2,1)S(1)} %add_convert_fusion.4), channel_id=1, source_target_pairs={{0,24},{2,26},{4,28},{6,30},{8,16},{10,18},{12,20},{14,22},{16,8},... | collective-permute-start | bytes 393224 | tf_op jit(solution)/shard_map/ppermute | solution.py:316
  97.8 8.1 %collective-permute-start.9 = (bf16[32,2048]{1,0:T(8,128)(2,1)}, bf16[32,2048]{1,0:T(8,128)(2,1)}, u32[]{:S(2)}, u32[]{:S(2)}) collective-permute-start(bf16[32,2048]{1,0:T(8,128)(2,1)} %add_convert_fusion.5), channel_id=1, source_target_pairs={{0,16},{2,18},{4,20},{6,22},{8,24},{10,26},{12,28},{14,30},{16,0},... | collective-permute-start | bytes 393224 | tf_op jit(solution)/shard_map/ppermute | solution.py:316
  100.9 9.0 %collective-permute-start.26 = (bf16[320,1024]{1,0:T(8,128)(2,1)}, bf16[320,1024]{1,0:T(8,128)(2,1)}, u32[]{:S(2)}, u32[]{:S(2)}) collective-permute-start(bf16[320,1024]{1,0:T(8,128)(2,1)} %collective-permute-done.24.refs_13_), channel_id=1, source_target_pairs={{0,2},{2,0},{4,6},{6,4},{8,10},{10,8},{12,14},{14,12},{16,18},{18,... | collective-permute-start | bytes 1966088 | tf_op jit(solution)/shard_map/ppermute | solution.py:316
  109.9 8.7 %collective-permute-start.15 = (bf16[32,2048]{1,0:T(8,128)(2,1)}, bf16[32,2048]{1,0:T(8,128)(2,1)S(1)}, u32[]{:S(2)}, u32[]{:S(2)}) collective-permute-start(bf16[32,2048]{1,0:T(8,128)(2,1)} %get-tuple-element.37.refs_0_), channel_id=1, source_target_pairs={{0,8},{2,10},{4,12},{6,14},{8,0},{10,2},{12,4},{14,6},{16,24},{18,... | collective-permute-start | bytes 393224 | tf_op jit(solution)/shard_map/ppermute | solution.py:316
  110.5 10.6 %collective-permute-start.17 = (bf16[32,2048]{1,0:T(8,128)(2,1)}, bf16[32,2048]{1,0:T(8,128)(2,1)S(1)}, u32[]{:S(2)}, u32[]{:S(2)}) collective-permute-start(bf16[32,2048]{1,0:T(8,128)(2,1)} %get-tuple-element.37.refs_0_), channel_id=1, source_target_pairs={{0,16},{2,18},{4,20},{6,22},{8,24},{10,26},{12,28},{14,30},{16,0},... | collective-permute-start | bytes 393224 | tf_op jit(solution)/shard_map/ppermute | solution.py:316
  118.6 7.3 %collective-permute-start.19 = (bf16[32,2048]{1,0:T(8,128)(2,1)}, bf16[32,2048]{1,0:T(8,128)(2,1)S(1)}, u32[]{:S(2)}, u32[]{:S(2)}) collective-permute-start(bf16[32,2048]{1,0:T(8,128)(2,1)} %get-tuple-element.37.refs_0_), channel_id=1, source_target_pairs={{0,24},{2,26},{4,28},{6,30},{8,16},{10,18},{12,20},{14,22},{16,8},... | collective-permute-start | bytes 393224 | tf_op jit(solution)/shard_map/ppermute | solution.py:316
  144.6 29.6 %collective-permute-start.35 = (bf16[32,2048]{1,0:T(8,128)(2,1)}, bf16[32,2048]{1,0:T(8,128)(2,1)S(1)}, u32[]{:S(2)}, u32[]{:S(2)}) collective-permute-start(bf16[32,2048]{1,0:T(8,128)(2,1)} %get-tuple-element.45), channel_id=1, source_target_pairs={{0,4},{2,6},{4,0},{6,2},{8,12},{10,14},{12,8},{14,10},{16,20},{18,... | collective-permute-start | bytes 393224 | tf_op jit(solution)/shard_map/ppermute | solution.py:316
  172.0 62.2 %collective-permute-start.46 = (bf16[984,1024]{1,0:T(8,128)(2,1)}, bf16[984,1024]{1,0:T(8,128)(2,1)}, u32[]{:S(2)}, u32[]{:S(2)}) collective-permute-start(bf16[984,1024]{1,0:T(8,128)(2,1)} %collective-permute-done.44.refs_9_), channel_id=1, source_target_pairs={{0,2},{2,0},{4,6},{6,4},{8,10},{10,8},{12,14},{14,12},{16,18},{18,... | collective-permute-start | bytes 6045704 | tf_op jit(solution)/shard_map/ppermute | solution.py:316
  172.0 53.3 %collective-permute-start.48 = (bf16[1024,1024]{1,0:T(8,128)(2,1)}, bf16[1024,1024]{1,0:T(8,128)(2,1)S(1)}, u32[]{:S(2)}, u32[]{:S(2)}) collective-permute-start(bf16[1024,1024]{1,0:T(8,128)(2,1)} %collective-permute-done.47.refs_9_), channel_id=1, source_target_pairs={{0,2},{2,0},{4,6},{6,4},{8,10},{10,8},{12,14},{14,12},{16,18},{18,... | collective-permute-start | bytes 6291464 | tf_op jit(solution)/shard_map/ppermute | solution.py:316
  174.2 7.5 %collective-permute-start.31 = (bf16[32,2048]{1,0:T(8,128)(2,1)}, bf16[32,2048]{1,0:T(8,128)(2,1)S(1)}, u32[]{:S(2)}, u32[]{:S(2)}) collective-permute-start(bf16[32,2048]{1,0:T(8,128)(2,1)} %get-tuple-element.41), channel_id=1, source_target_pairs={{0,4},{2,6},{4,0},{6,2},{8,12},{10,14},{12,8},{14,10},{16,20},{18,... | collective-permute-start | bytes 393224 | tf_op jit(solution)/shard_map/ppermute | solution.py:316
  184.5 8.1 %collective-permute-start.34 = (bf16[32,2048]{1,0:T(8,128)(2,1)S(1)}, bf16[32,2048]{1,0:T(8,128)(2,1)S(1)}, u32[]{:S(2)}, u32[]{:S(2)}) collective-permute-start(bf16[32,2048]{1,0:T(8,128)(2,1)S(1)} %add_convert_fusion.1), channel_id=1, source_target_pairs={{0,24},{2,26},{4,28},{6,30},{8,16},{10,18},{12,20},{14,22},{16,8},... | collective-permute-start | bytes 393224 | tf_op jit(solution)/shard_map/ppermute | solution.py:316
  188.1 9.5 %collective-permute-start.32 = (bf16[32,2048]{1,0:T(8,128)(2,1)S(1)}, bf16[32,2048]{1,0:T(8,128)(2,1)S(1)}, u32[]{:S(2)}, u32[]{:S(2)}) collective-permute-start(bf16[32,2048]{1,0:T(8,128)(2,1)S(1)} %add_convert_fusion.2), channel_id=1, source_target_pairs={{0,16},{2,18},{4,20},{6,22},{8,24},{10,26},{12,28},{14,30},{16,0},... | collective-permute-start | bytes 393224 | tf_op jit(solution)/shard_map/ppermute | solution.py:316
  200.3 8.8 %collective-permute-start.40 = (bf16[32,2048]{1,0:T(8,128)(2,1)}, bf16[32,2048]{1,0:T(8,128)(2,1)S(1)}, u32[]{:S(2)}, u32[]{:S(2)}) collective-permute-start(bf16[32,2048]{1,0:T(8,128)(2,1)} %residual_norm.3.refs_0_), channel_id=1, source_target_pairs={{0,16},{2,18},{4,20},{6,22},{8,24},{10,26},{12,28},{14,30},{16,0},... | collective-permute-start | bytes 393224 | tf_op jit(solution)/shard_map/ppermute | solution.py:316
  216.0 8.0 %collective-permute-start.41 = (bf16[32,2048]{1,0:T(8,128)(2,1)S(1)}, bf16[32,2048]{1,0:T(8,128)(2,1)S(1)}, u32[]{:S(2)}, u32[]{:S(2)}) collective-permute-start(bf16[32,2048]{1,0:T(8,128)(2,1)S(1)} %collective-permute-done.40.refs_4_), channel_id=1, source_target_pairs={{0,4},{2,6},{4,0},{6,2},{8,12},{10,14},{12,8},{14,10},{16,20},{18,... | collective-permute-start | bytes 393224 | tf_op jit(solution)/shard_map/ppermute | solution.py:316
  (56 other events, 666.4 us)

commit v2 on v1

v2 whole, which is shorter than its diff:
```python
import functools

import jax
import jax.numpy as jnp
from jax import lax
from jax.experimental import pallas as pl
from jax.experimental.pallas import tpu as pltpu
from jax.sharding import PartitionSpec as P


HEAD_DIM = 64
NORM_EPS = 0.25
NEG = -1e30


VMEM = pltpu.VMEM
SMEM = pltpu.SMEM


def vmem_spec():
    return pl.BlockSpec(memory_space=VMEM)


def smem_spec():
    return pl.BlockSpec(memory_space=SMEM)


def hbm_spec():
    return pl.BlockSpec(memory_space=pltpu.MemorySpace.HBM)


def dot32(a, b):
    return jnp.dot(a, b, preferred_element_type=jnp.float32)


def dot32_t(a, b):
    return lax.dot_general(a, b, (((1,), (1,)), ((), ())), preferred_element_type=jnp.float32)


def gelu_tanh(v):
    inner = 0.7978845608028654 * (v + 0.044715 * (v * v * v))
    return 0.5 * v * (1.0 + jnp.tanh(inner))


def by_heads_kernel(count, query_ref, keys_ref, values_ref, out_ref, sems):
    cols = out_ref.shape[3]
    copies = []
    for d in range(count):
        for k, ref in enumerate((keys_ref, values_ref)):
            copies.append(
                pltpu.make_async_copy(
                    ref.at[query_ref[0], :, pl.ds(d * cols, cols)], out_ref.at[d, k], sems.at[d, k]
                )
            )
            copies[-1].start()
    for copy in copies:
        copy.wait()


def by_heads(query, keys, values, count):
    src, model = keys.shape[1:]
    cols = model // count
    if cols % 128:
        pair = jnp.stack([lax.dynamic_index_in_dim(a, query[0], 0, False) for a in (keys, values)])
        return pair.reshape(2, src, count, cols).transpose(2, 0, 1, 3)
    return pl.pallas_call(
        functools.partial(by_heads_kernel, count),
        out_shape=jax.ShapeDtypeStruct((count, 2, src, cols), keys.dtype),
        in_specs=[smem_spec(), hbm_spec(), hbm_spec()],
        out_specs=vmem_spec(),
        scratch_shapes=[pltpu.SemaphoreType.DMA((count, 2))],
        compiler_params=pltpu.CompilerParams(vmem_limit_bytes=63 << 20),
        name="by_heads",
    )(query, keys, values)


def attention_kernel(live_ref, mine_ref, peer_ref, kv_ref, first_ref, second_ref):
    src = kv_ref.shape[0] * kv_ref.shape[2]
    cols = kv_ref.shape[3]
    keys = kv_ref[:, 0].reshape(src, cols)
    values = kv_ref[:, 1].reshape(src, cols)
    token = lax.broadcasted_iota(jnp.int32, (1, src), 1)
    bias = jnp.where(token < live_ref[0], 0.0, NEG).astype(jnp.float32)
    lane_head = lax.broadcasted_iota(jnp.int32, (1, cols), 1) // HEAD_DIM
    rows = mine_ref.shape[0]
    step = min(rows, 128)
    straight = live_ref[1] == 1
    for out_ref, one_ref, two_ref in (
        (first_ref, mine_ref, peer_ref),
        (second_ref, peer_ref, mine_ref),
    ):
        for start in range(0, rows, step):
            at = slice(start, start + step)
            q = jnp.where(straight, one_ref[at, :], two_ref[at, :])
            mixed = jnp.zeros((step, cols), jnp.float32)
            for head in range(cols // HEAD_DIM):
                q_head = jnp.where(lane_head == head, q, jnp.zeros_like(q))
                scores = dot32_t(q_head, keys) + bias
                row_max = jnp.max(scores, axis=-1, keepdims=True)
                weights = jnp.exp(scores - row_max)
                denominator = jnp.sum(weights, axis=-1, keepdims=True)
                head_out = dot32(weights.astype(jnp.bfloat16), values) / denominator
                mixed = jnp.where(lane_head == head, head_out, mixed)
            out_ref[at, :] = mixed.astype(jnp.bfloat16)


def attention(live, mine, peer, kv):
    rows, cols = mine.shape
    return pl.pallas_call(
        attention_kernel,
        out_shape=[jax.ShapeDtypeStruct((rows, cols), jnp.bfloat16)] * 2,
        in_specs=[smem_spec(), vmem_spec(), vmem_spec(), vmem_spec()],
        out_specs=[vmem_spec()] * 2,
        compiler_params=pltpu.CompilerParams(vmem_limit_bytes=24 << 20),
        name="attention",
    )(live, mine, peer, kv)


def project_kernel(n_cand, count, chip_ref, first_ref, second_ref, *refs):
    weights = refs[: 2 * n_cand]
    outs = refs[2 * n_cand : 2 * n_cand + count]
    own_s, par_s = refs[2 * n_cand + count :]
    share = first_ref.shape[0] // count
    straight = chip_ref[1] == 1
    for j in range(count):
        at = pl.multiple_of((chip_ref[0] ^ j) * share, share)
        to = slice(j * share, (j + 1) * share)
        first, second = first_ref[pl.ds(at, share), :], second_ref[pl.ds(at, share), :]
        own_s[to, :] = jnp.where(straight, first, second)
        par_s[to, :] = jnp.where(straight, second, first)
    own, par = own_s[...], par_s[...]
    width = weights[0].shape[1]
    for s in range(n_cand):
        block = dot32(own, weights[s][...]) + dot32(par, weights[n_cand + s][...])
        block = block.astype(jnp.bfloat16)
        for j in range(count):
            outs[j][:, s * width : (s + 1) * width] = block[j * share : (j + 1) * share, :]


def project(chip, first, second, weights, count):
    rows, cols = first.shape
    n_cand = len(weights) // 2
    model = weights[0].shape[1] * n_cand
    return pl.pallas_call(
        functools.partial(project_kernel, n_cand, count),
        out_shape=[jax.ShapeDtypeStruct((rows // count, model), jnp.bfloat16)] * count,
        in_specs=[smem_spec()] + [vmem_spec()] * (2 + len(weights)),
        out_specs=[vmem_spec()] * count,
        scratch_shapes=[VMEM((rows, cols), jnp.bfloat16)] * 2,
        compiler_params=pltpu.CompilerParams(vmem_limit_bytes=8 << 20),
        name="project",
    )(chip, first, second, *weights)


def residual_kernel(count, base_ref, gain_ref, *refs):
    total = base_ref[...].astype(jnp.float32)
    for part in refs[:count]:
        total = total + part[...].astype(jnp.float32)
    squares = jnp.mean(total * total, axis=-1, keepdims=True)
    refs[count][...] = (total * lax.rsqrt(squares + NORM_EPS) * gain_ref[...]).astype(jnp.bfloat16)
    if len(refs) > count + 1:
        refs[count + 1][...] = total


def residual_norm(base, gain, parts, keep):
    shapes = [jax.ShapeDtypeStruct(base.shape, jnp.bfloat16)]
    if keep:
        shapes.append(jax.ShapeDtypeStruct(base.shape, jnp.float32))
    return pl.pallas_call(
        functools.partial(residual_kernel, len(parts)),
        out_shape=shapes,
        in_specs=[vmem_spec()] * (2 + len(parts)),
        out_specs=[vmem_spec()] * len(shapes),
        compiler_params=pltpu.CompilerParams(vmem_limit_bytes=4 << 20),
        name="residual_norm",
    )(base, gain, *parts)


def ffn_kernel(n_cand, count, *refs):
    n_w = 2 * n_cand
    rows_in = refs[:count]
    gates = refs[count : count + n_w]
    ups = refs[count + n_w : count + 2 * n_w]
    downs = refs[count + 2 * n_w : count + 3 * n_w]
    outs = refs[count + 3 * n_w : 2 * count + 3 * n_w]
    acts = refs[2 * count + 3 * n_w]
    share = rows_in[0].shape[0]
    for j in range(count):
        acts[j * share : (j + 1) * share, :] = rows_in[j][...]
    depth = gates[0].shape[1]
    hidden = []
    for side in range(2):
        gate_part, up_part = None, None
        for s in range(n_cand):
            i = side * n_cand + s
            block = acts[:, s * depth : (s + 1) * depth]
            term = dot32_t(block, gates[i][...])
            gate_part = term if gate_part is None else gate_part + term
            term = dot32_t(block, ups[i][...])
            up_part = term if up_part is None else up_part + term
        hidden.append((gelu_tanh(gate_part) * up_part).astype(jnp.bfloat16))
    width = downs[0].shape[1]
    for s in range(n_cand):
        block = dot32(hidden[0], downs[s][...]) + dot32(hidden[1], downs[n_cand + s][...])
        block = block.astype(jnp.bfloat16)
        for j in range(count):
            outs[j][:, s * width : (s + 1) * width] = block[j * share : (j + 1) * share, :]


def feed_forward(rows_in, gates, ups, downs):
    count, n_w = len(rows_in), len(gates)
    n_cand = n_w // 2
    share, model = rows_in[0].shape
    return pl.pallas_call(
        functools.partial(ffn_kernel, n_cand, count),
        out_shape=[jax.ShapeDtypeStruct((share, model), jnp.bfloat16)] * count,
        in_specs=[vmem_spec()] * (count + 3 * n_w),
        out_specs=[vmem_spec()] * count,
        scratch_shapes=[VMEM((share * count, model), jnp.bfloat16)],
        compiler_params=pltpu.CompilerParams(vmem_limit_bytes=24 << 20),
        name="feed_forward",
    )(*rows_in, *gates, *ups, *downs)


def vocab_kernel(n_cand, count, width, live, flag_ref, gold_ref, *refs):
    rows_in = refs[: 2 * count]
    n_w = 2 * n_cand
    own = refs[2 * count : 2 * count + n_cand]
    swapped = refs[2 * count + n_cand : 2 * count + n_w]
    out_ref, acts, held, max_s, sum_s, gold_s, sems = refs[2 * count + n_w :]
    share = rows_in[0].shape[0]
    rows = 2 * count * share
    vocab, depth = own[0].shape
    slots = held.shape[0]
    chunks = [(at, min(width, vocab - at)) for at in range(0, vocab, width)]
    mine = flag_ref[0] == 1

    def copy(i, s, source):
        at, size = chunks[i]
        return pltpu.make_async_copy(
            source.at[pl.ds(at, size)], held.at[i % slots, s, pl.ds(0, size)], sems.at[i % slots, s]
        )

    def start(i):
        for s in range(n_cand):
            here, there = (own, swapped) if s == 0 else (swapped, own)

            @pl.when(mine)
            def _():
                copy(i, s, here[s]).start()

            @pl.when(jnp.logical_not(mine))
            def _():
                copy(i, s, there[s]).start()

    for i in range(min(slots, len(chunks))):
        start(i)
    for j in range(count):
        at = pl.multiple_of((flag_ref[2] ^ j) * share, share)
        acts[pl.ds(at, share), :] = rows_in[j][...]
        for s in range(n_cand):
            p = (s - n_cand // 2) % n_cand
            acts[pl.ds(at + rows // 2, share), s * depth : (s + 1) * depth] = rows_in[count + j][
                :, p * depth : (p + 1) * depth
            ]
    max_s[...] = jnp.full_like(max_s, NEG)
    sum_s[...] = jnp.zeros_like(sum_s)
    gold_s[...] = jnp.zeros_like(gold_s)
    for i, (first, size) in enumerate(chunks):
        logits = None
        for s in range(n_cand):
            copy(i, s, own[s]).wait()
            term = dot32_t(held[i % slots, s, :size], acts[:, s * depth : (s + 1) * depth])
            logits = term if logits is None else logits + term
        if i + slots < len(chunks):
            start(i + slots)
        column = first + lax.broadcasted_iota(jnp.int32, (size, 1), 0)
        hit = column == gold_ref[...] - flag_ref[1]
        if first + size > live:
            hit = hit & (column < live)
            logits = jnp.where(column < live, logits, NEG)
        picked = jnp.where(hit, logits, 0.0)
        gold_s[...] += jnp.sum(picked.reshape(size // 8, 8, rows), axis=0)
        logits = logits.reshape(size // 8, 8, rows)
        old = max_s[...]
        new = jnp.maximum(old, jnp.max(logits, axis=0))
        terms = jnp.sum(jnp.exp(logits - new[None]), axis=0)
        sum_s[...] = sum_s[...] * jnp.exp(old - new) + terms
        max_s[...] = new
    top = jnp.max(max_s[...], axis=0, keepdims=True)
    total = jnp.sum(sum_s[...] * jnp.exp(max_s[...] - top), axis=0, keepdims=True)
    gold = jnp.sum(gold_s[...], axis=0, keepdims=True)
    for k, value in enumerate((top, total, gold)):
        for i in range(rows // 128):
            out_ref[k, i : i + 1, :] = value[:, i * 128 : (i + 1) * 128]


def vocab_scores(flags, gold, rows_in, own, swapped, live):
    count, n_cand = len(rows_in) // 2, len(own)
    share, model = rows_in[0].shape
    vocab, depth = own[0].shape
    rows = share * count * 2
    slots = 3
    width = pl.cdiv(pl.cdiv(vocab, 3), 16) * 16
    assert rows % 256 == 0
    return pl.pallas_call(
        functools.partial(vocab_kernel, n_cand, count, width, live),
        out_shape=jax.ShapeDtypeStruct((3, rows // 128, 128), jnp.float32),
        in_specs=[smem_spec()] + [vmem_spec()] * (1 + len(rows_in)) + [hbm_spec()] * (2 * n_cand),
        out_specs=vmem_spec(),
        scratch_shapes=[
            VMEM((rows, model), jnp.bfloat16),
            VMEM((slots, n_cand, width, depth), jnp.bfloat16),
        ]
        + [VMEM((8, rows), jnp.float32)] * 3
        + [pltpu.SemaphoreType.DMA((slots, n_cand))],
        compiler_params=pltpu.CompilerParams(vmem_limit_bytes=60 << 20),
        name="vocab_scores",
    )(flags, gold, *rows_in, *own, *swapped)


def mean_kernel(length, info_ref, here_ref, there_ref, out_ref):
    middle = here_ref.shape[1] // 2
    sub = lax.broadcasted_iota(jnp.int32, (middle, 128), 0)
    row = sub * 128 + lax.broadcasted_iota(jnp.int32, (middle, 128), 1)
    lane = lax.broadcasted_iota(jnp.int32, (1, 128), 1)
    cands = middle * 128 // length
    best = jnp.full((1, 1), NEG, jnp.float32)
    for part in range(2):
        one, two = slice(part * middle, (part + 1) * middle), slice((1 - part) * middle, (2 - part) * middle)
        top_here, top_there = here_ref[0, one, :], there_ref[0, two, :]
        top = jnp.maximum(top_here, top_there)
        total = here_ref[1, one, :] * jnp.exp(top_here - top)
        total = total + there_ref[1, two, :] * jnp.exp(top_there - top)
        logprob = here_ref[2, one, :] + there_ref[2, two, :] - top - jnp.log(total)
        first = info_ref[1 + part]
        means = jnp.zeros((1, 128), jnp.float32)
        for c in range(cands):
            picked = jnp.where((row >= c * length) & (row < (c + 1) * length), logprob, 0.0)
            mean = jnp.sum(jnp.sum(picked, axis=0, keepdims=True), axis=1, keepdims=True) / length
            means = jnp.where(lane == c, mean, means)
            best = jnp.maximum(best, jnp.where(first + c < info_ref[0], mean, NEG))
        if part == 0:
            own = means
    out_ref[...] = jnp.where(lane < cands, own, best)


def candidate_means(info, here, there, length):
    return pl.pallas_call(
        functools.partial(mean_kernel, length),
        out_shape=jax.ShapeDtypeStruct((1, 128), jnp.float32),
        in_specs=[smem_spec(), vmem_spec(), vmem_spec()],
        out_specs=vmem_spec(),
        compiler_params=pltpu.CompilerParams(vmem_limit_bytes=2 << 20),
        name="candidate_means",
    )(info, here, there)


def result_kernel(info_ref, here_ref, there_ref, scores_ref, best_ref):
    cands = scores_ref.shape[1]
    low = info_ref[0] == 0
    here, there = here_ref[...], there_ref[...]
    lane = lax.broadcasted_iota(jnp.int32, (1, cands), 1) + info_ref[1]
    for q in range(2):
        line = jnp.where(low, here, there) if q == 0 else jnp.where(low, there, here)
        scores_ref[q : q + 1, :] = jnp.where(lane < info_ref[2 + q], line[:, :cands], 0.0)
        best_ref[:, q : q + 1] = line[:, cands : cands + 1]


def results(info, here, there, cands):
    return pl.pallas_call(
        result_kernel,
        out_shape=[
            jax.ShapeDtypeStruct((2, cands), jnp.float32),
            jax.ShapeDtypeStruct((1, 2), jnp.float32),
        ],
        in_specs=[smem_spec(), vmem_spec(), vmem_spec()],
        out_specs=[vmem_spec(), vmem_spec()],
        compiler_params=pltpu.CompilerParams(vmem_limit_bytes=2 << 20),
        name="results",
    )(info, here, there)


def body(
    dec_hidden,
    enc_keys,
    enc_values,
    enc_lengths,
    cand_counts,
    gold_ids,
    gain_cross,
    w_query,
    w_out,
    gain_ffn,
    w_in_gate,
    w_in_up,
    w_ffn_out,
    gain_final,
    w_vocab,
):
    queries, cand_dev, length, model = dec_hidden.shape
    n_tok, n_cand = lax.axis_size("tok"), lax.axis_size("cand")
    tok, cand = lax.axis_index("tok"), lax.axis_index("cand")
    core, chip = tok % 2, tok // 2
    chips = n_tok // 2
    rows = cand_dev * length
    half = n_cand // 2
    share = rows // chips
    block = model // n_cand
    head_cols = w_query.shape[1]
    assert queries == 2 and n_cand % 2 == 0 and n_tok % 4 == 0 and n_tok & (n_tok - 1) == 0

    def swap(a, k):
        return lax.ppermute(a, "tok", [(i, i ^ k) for i in range(n_tok)])

    def across(a, shift):
        return lax.ppermute(a, "cand", [(i, (i - shift) % n_cand) for i in range(n_cand)])

    def from_cands(a):
        return [a] + [across(a, s) for s in range(1, n_cand)]

    def with_partner(parts):
        own = swap(parts[0], 1)
        return parts + [own] + [swap(a, 1) for a in parts[1:]]

    def rolled(a):
        return jnp.concatenate(
            [
                lax.dynamic_slice_in_dim(a, ((cand + s) % n_cand) * block, block, a.ndim - 1)
                for s in range(n_cand)
            ],
            axis=-1,
        )

    def gather_rows(a, both):
        out, peer = [None] * chips, [None] * chips
        out[0] = a
        for j in range(2, chips, 2):
            out[j] = swap(a, 2 * j)
        for j in range(0, chips, 2):
            out[j + 1] = swap(out[j], 2)
        if not both:
            return out
        for j in range(chips):
            if j % 2 == 0 or j < chips // 2:
                peer[j] = across(out[j], half)
            else:
                peer[j] = swap(peer[j - 1], 2)
        return out + peer

    def scatter_rows(parts):
        order = [j for j in range(2, chips, 2)]
        order = order[1:] + order[:1] + [0]
        near = {j: swap(parts[j + 1], 2) for j in order}
        back = [parts[0], near[0]]
        for j in order[:-1]:
            pair = parts[j].astype(jnp.float32) + near[j].astype(jnp.float32)
            back.append(swap(pair.astype(jnp.bfloat16), 2 * j))
        return back

    query_at = cand // half

    pair = by_heads(query_at.reshape(1), enc_keys, enc_values, n_tok)
    key_values = lax.all_to_all(pair, "tok", 0, 0, tiled=True)

    query_parts = from_cands(w_query)
    out_parts = with_partner(from_cands(w_out))
    gate_parts = with_partner(from_cands(w_in_gate.T))
    up_parts = with_partner(from_cands(w_in_up.T))
    down_parts = with_partner(from_cands(w_ffn_out))
    vocab_dev = w_vocab.shape[1]
    vocab_own = w_vocab.T
    if vocab_dev % 8:
        vocab_own = jnp.pad(vocab_own, ((0, -vocab_dev % 8), (0, 0)))
    vocab_swapped = swap(vocab_own, 1)
    gold = lax.dynamic_index_in_dim(gold_ids, core, 0, keepdims=False).reshape(1, rows)
    gold = jnp.concatenate([gold, across(gold, half)], axis=1)

    flat = dec_hidden.reshape(queries * rows, model)
    base = rolled(lax.dynamic_slice_in_dim(flat, core * rows + chip * share, share, 0))
    flat = rolled(flat)
    wide = flat.astype(jnp.float32)
    gain_first, gain_mid, gain_last = (
        rolled(g.reshape(1, model)) for g in (gain_cross, gain_ffn, gain_final)
    )
    squares = jnp.mean(wide * wide, axis=-1, keepdims=True)
    normed = (wide * lax.rsqrt(squares + NORM_EPS) * gain_first).astype(jnp.bfloat16)
    query = sum(
        dot32(normed[:, s * block : (s + 1) * block], query_parts[s]) for s in range(n_cand)
    ).astype(jnp.bfloat16)
    query = query.reshape(queries, rows, head_cols)
    mine = lax.dynamic_index_in_dim(query, query_at, 0, keepdims=False)
    other = lax.dynamic_index_in_dim(query, 1 - query_at, 0, keepdims=False)
    peer = across(other, half)
    straight = (core == query_at).astype(jnp.int32)
    live = jnp.stack([lax.dynamic_index_in_dim(enc_lengths, query_at, 0, keepdims=False), straight])
    count_here = lax.dynamic_index_in_dim(cand_counts, core, 0, keepdims=False)
    plane_first, plane_other = cand * cand_dev, ((cand + half) % n_cand) * cand_dev
    mean_info = jnp.stack([count_here, plane_first, plane_other])
    result_info = jnp.stack([core, plane_first, cand_counts[0], cand_counts[1]])
    chip_at = jnp.stack([chip, straight])
    flags = jnp.stack([straight, (chip * 2 + query_at) * vocab_dev, chip])
    live, base, gain_mid, gain_last, gold, mean_info, result_info, chip_at, flags = (
        lax.optimization_barrier(
            (live, base, gain_mid, gain_last, gold, mean_info, result_info, chip_at, flags)
        )
    )
    first, second = attention(live, mine, peer, key_values)

    def route(a, flip):
        perm = []
        for t in range(n_tok):
            for c in range(n_cand):
                to_half = (t % 2) ^ flip
                to = (t - t % 2 + c // half) * n_cand + c % half + to_half * half
                perm.append((t * n_cand + c, to))
        return lax.ppermute(a, ("tok", "cand"), perm)

    first, second = route(first, 0), route(second, 1)
    vocab_own = [vocab_own]
    for s in range(1, n_cand):
        perm = []
        for c in range(n_cand):
            side = c // half
            for t in range(0, n_tok, 2):
                perm.append(((t + side) * n_cand + (c + s) % n_cand, (t + 1 - side) * n_cand + c))
        vocab_own.append(lax.ppermute(vocab_own[0], ("tok", "cand"), perm))
    vocab_swapped = [vocab_swapped] + [swap(w, 1) for w in vocab_own[1:]]
    cross_terms = project(chip_at, first, second, out_parts, chips)
    cross_terms = scatter_rows(cross_terms)
    normed_ffn, after_cross = residual_norm(base, gain_mid, cross_terms, True)
    ffn_rows = gather_rows(normed_ffn, False)
    ffn_terms = feed_forward(ffn_rows, gate_parts, up_parts, down_parts)
    ffn_terms = scatter_rows(ffn_terms)
    (normed_final,) = residual_norm(after_cross, gain_last, ffn_terms, False)
    final_rows = gather_rows(normed_final, True)

    stats = vocab_scores(flags, gold, final_rows, vocab_own, vocab_swapped, vocab_dev)

    def combine(parts):
        top = functools.reduce(jnp.maximum, [p[0] for p in parts])
        total = sum(p[1] * jnp.exp(p[0] - top) for p in parts)
        return jnp.stack([top, total, sum(p[2] for p in parts)])

    stats = combine([stats, swap(stats, 2)])
    stats = combine([stats] + [swap(stats, 2 * j) for j in range(2, chips, 2)])
    theirs = across(stats, half)
    means = candidate_means(mean_info, stats, theirs, length)
    k = 1
    while k < half:
        other_best = lax.ppermute(means, "cand", [(i, i ^ k) for i in range(n_cand)])
        past = lax.iota(jnp.int32, 128)[None, :] >= cand_dev
        means = jnp.where(past, jnp.maximum(means, other_best), means)
        k *= 2
    cand_scores, best = results(result_info, means, swap(means, 1), cand_dev)
    return (cand_scores, best.reshape(2))


def solution(mesh):
    in_specs = (
        P(None, "cand", None, None),
        P(None, "tok", None),
        P(None, "tok", None),
        P(),
        P(),
        P(None, "cand", None),
        P(),
        P("cand", "tok"),
        P("tok", "cand"),
        P(),
        P("cand", "tok"),
        P("cand", "tok"),
        P("tok", "cand"),
        P(),
        P("cand", "tok"),
    )
    out_specs = (P(None, "cand"), P())
    return jax.shard_map(body, mesh=mesh, in_specs=in_specs, out_specs=out_specs, check_vma=False)
```

time: 263 us -> 251 us (0.954)
  waiting for transfers between devices: 114 us -> 134 us
  local copies, waits for them, and re-layouts: 21.1 us -> 5.75 us
  other arithmetic: 14.8 us -> 5.92 us
  Pallas kernels: 34.4 us -> 26.5 us
    ppermute x8 -> x14, waiting for transfers between devices: 49.7 us -> 73.9 us  [across(): lax.ppermute(a, 'cand', [(i, (i - shift) % n_cand) for i in range(n_cand)])]
    ppermute x43 -> x45, starting transfers between devices: 52 us -> 44.9 us  [swap(): return lax.ppermute(a, 'tok', [(i, i ^ k) for i in range(n_tok)])]
    slice x5 -> x0, local copies, waits for them, and re-layouts: 6.28 us -> none  [the longest x2 6.24 us: body(): vocab_low, vocab_high = (vocab_all[:cut], vocab_all[cut:])]
    convert_element_type x6, other arithmetic: 6.29 us -> 0.2 us  [scatter_rows(): back.append(swap(pair.astype(jnp.bfloat16), 2 * j))]
    unnamed x68 -> x54, local copies, waits for them, and re-layouts: 5.53 us -> 0.99 us
    ppermute x8 -> x14, starting transfers between devices: 12.1 us -> 16.2 us  [across(): lax.ppermute(a, 'cand', [(i, (i - shift) % n_cand) for i in range(n_cand)])]
    pallas_call x2, Pallas kernels: 4.13 us -> 0.4 us  [residual_norm(): pl.pallas_call(functools.partial(residual_kernel, len(parts)), out_shape=...]
    ppermute x1, waiting for transfers between devices: 3.27 us -> 0.01 us  [body(): vocab_own.append(lax.ppermute(vocab_own[0], ('tok', 'cand'), perm))]
  transfers between devices with their start and end apart: 55 -> 63, of which waited for: 27 -> 37; matrix products, arithmetic and copies ran while one was open for 11% -> 5% of each run, Pallas kernels for 10% -> 6%
where the time goes in v2:
time: 251 us
  waiting for transfers between devices  134 us (53%)
  starting transfers between devices  73.9 us (29%)
  Pallas kernels  26.5 us (11%)
  other arithmetic  5.92 us (2%)
  local copies, waits for them, and re-layouts  5.75 us (2%)
  matrix products  2.87 us (1%)
    ppermute x14, waiting for transfers between devices, across(): lax.ppermute(a, 'cand', [(i, (i - shift) % n_cand) for i in range(n_cand)])  73.9 us
    ppermute x45, waiting for transfers between devices, swap(): return lax.ppermute(a, 'tok', [(i, i ^ k) for i in range(n_tok)])  60.5 us
    ppermute x45, starting transfers between devices, swap(): return lax.ppermute(a, 'tok', [(i, i ^ k) for i in range(n_tok)])  44.9 us
    ppermute x14, starting transfers between devices, across(): lax.ppermute(a, 'cand', [(i, (i - shift) % n_cand) for i in range(n_cand)])  16.2 us
    pallas_call x1, Pallas kernels, vocab_scores(): pl.pallas_call(functools.partial(vocab_kernel, n_cand, count, width, live...  10.1 us
    all_to_all x1, starting transfers between devices, body(): key_values = lax.all_to_all(pair, 'tok', 0, 0, tiled=True)  5.95 us
    pallas_call x1, Pallas kernels, attention(): pl.pallas_call(attention_kernel, out_shape=[jax.ShapeDtypeStruct((rows, c...  5.22 us
  transfers between devices with their start and end apart: 63, of which 37 were waited for; matrix products, arithmetic and copies ran while one was open for 5% of the time, Pallas kernels for 6%

profile of v2, /device:TPU:0, one launch (start us, length us, event | category | flops | bytes accessed | tf_op | source)
XLA Modules:
  0.0 250.7 jit_solution(10591124171214302798)
XLA Ops:
  1.2 2.6 %collective-permute-start.22 = (bf16[320,1024]{1,0:T(8,128)(2,1)}, bf16[320,1024]{1,0:T(8,128)(2,1)}, u32[]{:S(2)}, u32[]{:S(2)}) collective-permute-start(bf16[320,1024]{1,0:T(8,128)(2,1)} %bitcast.27), channel_id=1, source_target_pairs={{0,1},{1,0},{2,3},{3,2},{4,5},{5,4},{6,7},{7,6},{8,9},{9,8},{10,11... | collective-permute-start | bytes 1966088 | tf_op jit(solution)/shard_map/ppermute | solution.py:417
  5.9 2.5 by_heads.1
  8.4 6.0 %all-to-all-start = ((bf16[16,2,128,128]{3,2,1,0:T(8,128)(2,1)}), bf16[16,2,128,128]{3,2,1,0:T(8,128)(2,1)S(1)}, u32[]{:S(2)}, u32[]{:S(2)}) async-start(bf16[16,2,128,128]{3,2,1,0:T(8,128)(2,1)} %by_heads.1), calls=%async_computation | async-start | bytes 2097152 | tf_op jit(solution)/shard_map/all_to_all | solution.py:464
  14.3 2.7 %collective-permute-start.53 = (bf16[2008,1024]{1,0:T(8,128)(2,1)}, bf16[2008,1024]{1,0:T(8,128)(2,1)}, u32[]{:S(2)}, u32[]{:S(2)}) collective-permute-start(bf16[2008,1024]{1,0:T(8,128)(2,1)} %bitcast.32), channel_id=1, source_target_pairs={{1,2},{5,6},{9,10},{13,14},{17,18},{21,22},{25,26},{29,30},{2,1},{... | collective-permute-start | bytes 12337160 | tf_op jit(solution)/shard_map/ppermute | solution.py:527
  25.1 2.3 collective-permute-start.5
  30.1 45.3 %collective-permute-done.5.refs_1_ = bf16[128,1024]{1,0:T(8,128)(2,1)} collective-permute-done((bf16[128,1024]{1,0:T(8,128)(2,1)S(1)}, bf16[128,1024]{1,0:T(8,128)(2,1)}, u32[]{:S(2)}, u32[]{:S(2)}) %collective-permute-start.5) | collective-permute-done | bytes 262176 | tf_op jit(solution)/shard_map/ppermute | solution.py:417
  78.6 5.2 %attention.1 = (bf16[256,128]{1,0:T(8,128)(2,1)S(1)}, bf16[256,128]{1,0:T(8,128)(2,1)S(1)}) custom-call(s32[2]{0:T(128)S(1)} %pad_add_fusion.1.live_ref, bf16[256,128]{1,0:T(8,128)(2,1)S(1)} %get-tuple-element.73.mine_ref, bf16[256,128]{1,0:T(8,128)(2,1)} %collective-permute-done.2.peer_ref, bf16[16,2,128,128]{3,2,1,0:T(8,128)(2,1)S(1)} %all-to-all-done.kv_ref), custom_call_target="tpu_custom_call" | custom-call | tf_op jit(solution)/shard_map/attention/pallas_call | solution.py:109
  84.7 3.4 %collective-permute-start.4 = (bf16[256,128]{1,0:T(8,128)(2,1)S(1)}, bf16[256,128]{1,0:T(8,128)(2,1)S(1)}, u32[]{:S(2)}, u32[]{:S(2)}) collective-permute-start(bf16[256,128]{1,0:T(8,128)(2,1)S(1)} %get-tuple-element.42), channel_id=1, source_target_pairs={{0,1},{1,3},{2,0},{3,2},{4,5},{5,7},{6,4},{7,6},{8,9},{9,11},{10,8... | collective-permute-start | bytes 196616 | tf_op jit(solution)/shard_map/ppermute | solution.py:517
  90.0 2.4 collective-permute-start.25
  96.1 3.2 %collective-permute-done.9 = bf16[32,2048]{1,0:T(8,128)(2,1)S(1)} collective-permute-done((bf16[32,2048]{1,0:T(8,128)(2,1)S(1)}, bf16[32,2048]{1,0:T(8,128)(2,1)S(1)}, u32[]{:S(2)}, u32[]{:S(2)}) %collective-permute-start.9) | collective-permute-done | bytes 131104 | tf_op jit(solution)/shard_map/ppermute | solution.py:414
  101.1 6.8 %collective-permute-done.25.refs_13_ = bf16[320,1024]{1,0:T(8,128)(2,1)S(1)} collective-permute-done((bf16[320,1024]{1,0:T(8,128)(2,1)S(1)}, bf16[320,1024]{1,0:T(8,128)(2,1)S(1)}, u32[]{:S(2)}, u32[]{:S(2)}) %collective-permute-start.25) | collective-permute-done | bytes 655392 | tf_op jit(solution)/shard_map/ppermute | solution.py:417
  110.0 11.5 %collective-permute-done.28.refs_17_ = bf16[320,1024]{1,0:T(8,128)(2,1)S(1)} collective-permute-done((bf16[320,1024]{1,0:T(8,128)(2,1)S(1)}, bf16[320,1024]{1,0:T(8,128)(2,1)S(1)}, u32[]{:S(2)}, u32[]{:S(2)}) %collective-permute-start.28) | collective-permute-done | bytes 655392 | tf_op jit(solution)/shard_map/ppermute | solution.py:417
  123.1 2.6 %collective-permute-start.10 = (bf16[32,2048]{1,0:T(8,128)(2,1)S(1)}, bf16[32,2048]{1,0:T(8,128)(2,1)S(1)}, u32[]{:S(2)}, u32[]{:S(2)}) collective-permute-start(bf16[32,2048]{1,0:T(8,128)(2,1)S(1)} %add_convert_fusion.5), channel_id=1, source_target_pairs={{0,16},{2,18},{4,20},{6,22},{8,24},{10,26},{12,28},{14,30},{16,0},... | collective-permute-start | bytes 393224 | tf_op jit(solution)/shard_map/ppermute | solution.py:414
  128.1 7.2 %collective-permute-done.10.refs_2_ = bf16[32,2048]{1,0:T(8,128)(2,1)S(1)} collective-permute-done((bf16[32,2048]{1,0:T(8,128)(2,1)S(1)}, bf16[32,2048]{1,0:T(8,128)(2,1)S(1)}, u32[]{:S(2)}, u32[]{:S(2)}) %collective-permute-start.10) | collective-permute-done | bytes 131104 | tf_op jit(solution)/shard_map/ppermute | solution.py:414
  137.6 2.4 collective-permute-start.20
  142.0 3.9 %collective-permute-done.20.refs_6_ = bf16[32,2048]{1,0:T(8,128)(2,1)S(1)} collective-permute-done((bf16[32,2048]{1,0:T(8,128)(2,1)S(1)}, bf16[32,2048]{1,0:T(8,128)(2,1)S(1)}, u32[]{:S(2)}, u32[]{:S(2)}) %collective-permute-start.20) | collective-permute-done | bytes 131104 | tf_op jit(solution)/shard_map/ppermute | solution.py:414
  146.4 6.1 %collective-permute-done.18.refs_4_ = bf16[32,2048]{1,0:T(8,128)(2,1)S(1)} collective-permute-done((bf16[32,2048]{1,0:T(8,128)(2,1)S(1)}, bf16[32,2048]{1,0:T(8,128)(2,1)S(1)}, u32[]{:S(2)}, u32[]{:S(2)}) %collective-permute-start.18) | collective-permute-done | bytes 131104 | tf_op jit(solution)/shard_map/ppermute | solution.py:414
  155.1 3.8 %collective-permute-done.21.refs_7_ = bf16[32,2048]{1,0:T(8,128)(2,1)S(1)} collective-permute-done((bf16[32,2048]{1,0:T(8,128)(2,1)S(1)}, bf16[32,2048]{1,0:T(8,128)(2,1)S(1)}, u32[]{:S(2)}, u32[]{:S(2)}) %collective-permute-start.21) | collective-permute-done | bytes 131104 | tf_op jit(solution)/shard_map/ppermute | solution.py:414
  158.9 2.7 %collective-permute-done.19.refs_5_ = bf16[32,2048]{1,0:T(8,128)(2,1)S(1)} collective-permute-done((bf16[32,2048]{1,0:T(8,128)(2,1)S(1)}, bf16[32,2048]{1,0:T(8,128)(2,1)S(1)}, u32[]{:S(2)}, u32[]{:S(2)}) %collective-permute-start.19) | collective-permute-done | bytes 131104 | tf_op jit(solution)/shard_map/ppermute | solution.py:414
  162.9 4.8 %feed_forward.1 = (bf16[32,2048]{1,0:T(8,128)(2,1)S(1)}, bf16[32,2048]{1,0:T(8,128)(2,1)S(1)}, bf16[32,2048]{1,0:T(8,128)(2,1)S(1)}, bf16[32,2048]{1,0:T(8,128)(...) custom-call(bf16[32,2048]{1,0:T(8,128)(2,1)S(1)} %get-tuple-element., ...), custom_call_target="tpu_custom_call" | custom-call | tf_op jit(solution)/shard_map/feed_forward/pallas_call | solution.py:214
  170.4 3.8 %collective-permute-done.32 = bf16[32,2048]{1,0:T(8,128)(2,1)S(1)} collective-permute-done((bf16[32,2048]{1,0:T(8,128)(2,1)S(1)}, bf16[32,2048]{1,0:T(8,128)(2,1)S(1)}, u32[]{:S(2)}, u32[]{:S(2)}) %collective-permute-start.32) | collective-permute-done | bytes 131104 | tf_op jit(solution)/shard_map/ppermute | solution.py:414
  174.8 4.0 %collective-permute-done.34 = bf16[32,2048]{1,0:T(8,128)(2,1)S(1)} collective-permute-done((bf16[32,2048]{1,0:T(8,128)(2,1)S(1)}, bf16[32,2048]{1,0:T(8,128)(2,1)S(1)}, u32[]{:S(2)}, u32[]{:S(2)}) %collective-permute-start.34) | collective-permute-done | bytes 131104 | tf_op jit(solution)/shard_map/ppermute | solution.py:414
  180.2 2.4 collective-permute-start.35
  182.7 5.7 %collective-permute-done.33.refs_2_ = bf16[32,2048]{1,0:T(8,128)(2,1)S(1)} collective-permute-done((bf16[32,2048]{1,0:T(8,128)(2,1)S(1)}, bf16[32,2048]{1,0:T(8,128)(2,1)S(1)}, u32[]{:S(2)}, u32[]{:S(2)}) %collective-permute-start.33) | collective-permute-done | bytes 131104 | tf_op jit(solution)/shard_map/ppermute | solution.py:414
  190.1 1.9 collective-permute-start.43
  192.9 2.1 collective-permute-done.45.refs_8_
  197.6 3.8 %collective-permute-done.41.refs_4_ = bf16[32,2048]{1,0:T(8,128)(2,1)S(1)} collective-permute-done((bf16[32,2048]{1,0:T(8,128)(2,1)S(1)}, bf16[32,2048]{1,0:T(8,128)(2,1)S(1)}, u32[]{:S(2)}, u32[]{:S(2)}) %collective-permute-start.41) | collective-permute-done | bytes 131104 | tf_op jit(solution)/shard_map/ppermute | solution.py:414
  204.0 2.4 collective-permute-done.51.refs_14_
  223.0 10.1 %vocab_scores.1 = f32[3,4,128]{2,1,0:T(4,128)} custom-call(s32[3]{0:T(128)} %get-tuple-element.35.flag_ref, s32[1,512]{1,0:T(1,128)} %pad_add_fusion.gold_ref, bf16[32,2048]{1,0:T(8,128)(2,1)} %copy-done.4, bf16[32,2048]{1,0:T(8,128)(2,1)} %copy-done.11, bf16[32,2048]{1,0:T(8,128)(2,1)} %copy-done.10, bf16[32,2048]{1,0:T(8,128)(2,1)} %copy-done.17, ...), custom_call_target="tpu_custom_call" | custom-call | tf_op jit(solution)/shard_map/vocab_scores/pallas_call | solution.py:306
  233.0 2.0 collective-permute-start.56
  235.1 1.9 collective-permute-done.56
  245.6 2.0 collective-permute-done.60.there_ref
  (190 shorter events, 80.3 us)
Async XLA Ops:
  0.7 93.5 %collective-permute-start.23 = (bf16[320,1024]{1,0:T(8,128)(2,1)}, bf16[320,1024]{1,0:T(8,128)(2,1)}, u32[]{:S(2)}, u32[]{:S(2)}) collective-permute-start(bf16[320,1024]{1,0:T(8,128)(2,1)} %bitcast.26), channel_id=1, source_target_pairs={{0,2},{2,0},{4,6},{6,4},{8,10},{10,8},{12,14},{14,12},{16,18},{18,... | collective-permute-start | bytes 1966088 | tf_op jit(solution)/shard_map/ppermute | solution.py:414
  1.2 94.8 %collective-permute-start.22 = (bf16[320,1024]{1,0:T(8,128)(2,1)}, bf16[320,1024]{1,0:T(8,128)(2,1)}, u32[]{:S(2)}, u32[]{:S(2)}) collective-permute-start(bf16[320,1024]{1,0:T(8,128)(2,1)} %bitcast.27), channel_id=1, source_target_pairs={{0,1},{1,0},{2,3},{3,2},{4,5},{5,4},{6,7},{7,6},{8,9},{9,8},{10,11... | collective-permute-start | bytes 1966088 | tf_op jit(solution)/shard_map/ppermute | solution.py:417
  3.9 25.5 %collective-permute-start = (s32[1,256]{1,0:T(1,128)S(1)}, s32[1,256]{1,0:T(1,128)S(1)}, u32[]{:S(2)}, u32[]{:S(2)}) collective-permute-start(s32[1,256]{1,0:T(1,128)S(1)} %reshape.38), channel_id=1, source_target_pairs={{0,1},{1,0},{2,3},{3,2},{4,5},{5,4},{6,7},{7,6},{8,9},{9,8},{10,11... | collective-permute-start | bytes 3080 | tf_op jit(solution)/shard_map/ppermute | solution.py:417
  4.4 20.7 %collective-permute-start.1 = (bf16[1024,128]{1,0:T(8,128)(2,1)}, bf16[1024,128]{1,0:T(8,128)(2,1)}, u32[]{:S(2)}, u32[]{:S(2)}) collective-permute-start(bf16[1024,128]{1,0:T(8,128)(2,1)} %param.22), channel_id=1, source_target_pairs={{0,1},{1,0},{2,3},{3,2},{4,5},{5,4},{6,7},{7,6},{8,9},{9,8},{10,11... | collective-permute-start | bytes 786440 | tf_op jit(solution)/shard_map/ppermute | solution.py:417
  8.4 70.2 %all-to-all-start = ((bf16[16,2,128,128]{3,2,1,0:T(8,128)(2,1)}), bf16[16,2,128,128]{3,2,1,0:T(8,128)(2,1)S(1)}, u32[]{:S(2)}, u32[]{:S(2)}) async-start(bf16[16,2,128,128]{3,2,1,0:T(8,128)(2,1)} %by_heads.1), calls=%async_computation | async-start | bytes 2097152 | tf_op jit(solution)/shard_map/all_to_all | solution.py:464
  14.3 95.4 %collective-permute-start.53 = (bf16[2008,1024]{1,0:T(8,128)(2,1)}, bf16[2008,1024]{1,0:T(8,128)(2,1)}, u32[]{:S(2)}, u32[]{:S(2)}) collective-permute-start(bf16[2008,1024]{1,0:T(8,128)(2,1)} %bitcast.32), channel_id=1, source_target_pairs={{1,2},{5,6},{9,10},{13,14},{17,18},{21,22},{25,26},{29,30},{2,1},{... | collective-permute-start | bytes 12337160 | tf_op jit(solution)/shard_map/ppermute | solution.py:527
  25.1 50.4 %collective-permute-start.5 = (bf16[128,1024]{1,0:T(8,128)(2,1)S(1)}, bf16[128,1024]{1,0:T(8,128)(2,1)}, u32[]{:S(2)}, u32[]{:S(2)}) collective-permute-start(bf16[128,1024]{1,0:T(8,128)(2,1)S(1)} %copy-done.5), channel_id=1, source_target_pairs={{0,1},{1,0},{2,3},{3,2},{4,5},{5,4},{6,7},{7,6},{8,9},{9,8},{10,11... | collective-permute-start | bytes 786440 | tf_op jit(solution)/shard_map/ppermute | solution.py:417
  29.4 46.8 %collective-permute-start.2 = (bf16[256,128]{1,0:T(8,128)(2,1)}, bf16[256,128]{1,0:T(8,128)(2,1)}, u32[]{:S(2)}, u32[]{:S(2)}) collective-permute-start(bf16[256,128]{1,0:T(8,128)(2,1)} %get-tuple-element.72), channel_id=1, source_target_pairs={{0,1},{1,0},{2,3},{3,2},{4,5},{5,4},{6,7},{7,6},{8,9},{9,8},{10,11... | collective-permute-start | bytes 196616 | tf_op jit(solution)/shard_map/ppermute | solution.py:417
  75.5 8.4 %collective-permute-start.6 = (bf16[128,1024]{1,0:T(8,128)(2,1)S(1)}, bf16[128,1024]{1,0:T(8,128)(2,1)}, u32[]{:S(2)}, u32[]{:S(2)}) collective-permute-start(bf16[128,1024]{1,0:T(8,128)(2,1)S(1)} %copy-done.5), channel_id=1, source_target_pairs={{0,2},{2,0},{4,6},{6,4},{8,10},{10,8},{12,14},{14,12},{16,18},{18,... | collective-permute-start | bytes 786440 | tf_op jit(solution)/shard_map/ppermute | solution.py:414
  76.2 8.6 %collective-permute-start.7 = (bf16[128,1024]{1,0:T(8,128)(2,1)}, bf16[128,1024]{1,0:T(8,128)(2,1)}, u32[]{:S(2)}, u32[]{:S(2)}) collective-permute-start(bf16[128,1024]{1,0:T(8,128)(2,1)} %collective-permute-done.5.refs_1_), channel_id=1, source_target_pairs={{0,2},{2,0},{4,6},{6,4},{8,10},{10,8},{12,14},{14,12},{16,18},{18,... | collective-permute-start | bytes 786440 | tf_op jit(solution)/shard_map/ppermute | solution.py:414
  88.1 12.9 %collective-permute-start.26 = (bf16[320,1024]{1,0:T(8,128)(2,1)S(1)}, bf16[320,1024]{1,0:T(8,128)(2,1)S(1)}, u32[]{:S(2)}, u32[]{:S(2)}) collective-permute-start(bf16[320,1024]{1,0:T(8,128)(2,1)S(1)} %bitcast.29), channel_id=1, source_target_pairs={{0,2},{2,0},{4,6},{6,4},{8,10},{10,8},{12,14},{14,12},{16,18},{18,... | collective-permute-start | bytes 1966088 | tf_op jit(solution)/shard_map/ppermute | solution.py:414
  90.0 17.9 %collective-permute-start.25 = (bf16[320,1024]{1,0:T(8,128)(2,1)S(1)}, bf16[320,1024]{1,0:T(8,128)(2,1)S(1)}, u32[]{:S(2)}, u32[]{:S(2)}) collective-permute-start(bf16[320,1024]{1,0:T(8,128)(2,1)S(1)} %bitcast.30), channel_id=1, source_target_pairs={{0,1},{1,0},{2,3},{3,2},{4,5},{5,4},{6,7},{7,6},{8,9},{9,8},{10,11... | collective-permute-start | bytes 1966088 | tf_op jit(solution)/shard_map/ppermute | solution.py:417
  96.0 25.4 %collective-permute-start.28 = (bf16[320,1024]{1,0:T(8,128)(2,1)S(1)}, bf16[320,1024]{1,0:T(8,128)(2,1)S(1)}, u32[]{:S(2)}, u32[]{:S(2)}) collective-permute-start(bf16[320,1024]{1,0:T(8,128)(2,1)S(1)} %copy-done.3), channel_id=1, source_target_pairs={{0,1},{1,0},{2,3},{3,2},{4,5},{5,4},{6,7},{7,6},{8,9},{9,8},{10,11... | collective-permute-start | bytes 1966088 | tf_op jit(solution)/shard_map/ppermute | solution.py:417
  99.2 8.7 %collective-permute-start.11 = (bf16[32,2048]{1,0:T(8,128)(2,1)S(1)}, bf16[32,2048]{1,0:T(8,128)(2,1)S(1)}, u32[]{:S(2)}, u32[]{:S(2)}) collective-permute-start(bf16[32,2048]{1,0:T(8,128)(2,1)S(1)} %get-tuple-element.48), channel_id=1, source_target_pairs={{0,4},{2,6},{4,0},{6,2},{8,12},{10,14},{12,8},{14,10},{16,20},{18,... | collective-permute-start | bytes 393224 | tf_op jit(solution)/shard_map/ppermute | solution.py:414
  101.1 24.7 %collective-permute-start.29 = (bf16[320,1024]{1,0:T(8,128)(2,1)S(1)}, bf16[320,1024]{1,0:T(8,128)(2,1)S(1)}, u32[]{:S(2)}, u32[]{:S(2)}) collective-permute-start(bf16[320,1024]{1,0:T(8,128)(2,1)S(1)} %copy-done.3), channel_id=1, source_target_pairs={{0,2},{2,0},{4,6},{6,4},{8,10},{10,8},{12,14},{14,12},{16,18},{18,... | collective-permute-start | bytes 1966088 | tf_op jit(solution)/shard_map/ppermute | solution.py:414
  108.0 114.3 %collective-permute-start.54 = (bf16[2008,1024]{1,0:T(8,128)(2,1)}, bf16[2008,1024]{1,0:T(8,128)(2,1)}, u32[]{:S(2)}, u32[]{:S(2)}) collective-permute-start(bf16[2008,1024]{1,0:T(8,128)(2,1)} %bitcast.33), channel_id=1, source_target_pairs={{0,2},{2,0},{4,6},{6,4},{8,10},{10,8},{12,14},{14,12},{16,18},{18,... | collective-permute-start | bytes 12337160 | tf_op jit(solution)/shard_map/ppermute | solution.py:414
  108.0 15.1 %collective-permute-start.13 = (bf16[32,2048]{1,0:T(8,128)(2,1)S(1)}, bf16[32,2048]{1,0:T(8,128)(2,1)S(1)}, u32[]{:S(2)}, u32[]{:S(2)}) collective-permute-start(bf16[32,2048]{1,0:T(8,128)(2,1)S(1)} %get-tuple-element.50), channel_id=1, source_target_pairs={{0,4},{2,6},{4,0},{6,2},{8,12},{10,14},{12,8},{14,10},{16,20},{18,... | collective-permute-start | bytes 393224 | tf_op jit(solution)/shard_map/ppermute | solution.py:414
  109.7 112.6 %collective-permute-start.55 = (bf16[2008,1024]{1,0:T(8,128)(2,1)}, bf16[2008,1024]{1,0:T(8,128)(2,1)}, u32[]{:S(2)}, u32[]{:S(2)}) collective-permute-start(bf16[2008,1024]{1,0:T(8,128)(2,1)} %collective-permute-done.53.refs_17_), channel_id=1, source_target_pairs={{0,2},{2,0},{4,6},{6,4},{8,10},{10,8},{12,14},{14,12},{16,18},{18,... | collective-permute-start | bytes 12337160 | tf_op jit(solution)/shard_map/ppermute | solution.py:414
  123.1 12.2 %collective-permute-start.10 = (bf16[32,2048]{1,0:T(8,128)(2,1)S(1)}, bf16[32,2048]{1,0:T(8,128)(2,1)S(1)}, u32[]{:S(2)}, u32[]{:S(2)}) collective-permute-start(bf16[32,2048]{1,0:T(8,128)(2,1)S(1)} %add_convert_fusion.5), channel_id=1, source_target_pairs={{0,16},{2,18},{4,20},{6,22},{8,24},{10,26},{12,28},{14,30},{16,0},... | collective-permute-start | bytes 393224 | tf_op jit(solution)/shard_map/ppermute | solution.py:414
  125.7 9.6 %collective-permute-start.12 = (bf16[32,2048]{1,0:T(8,128)(2,1)S(1)}, bf16[32,2048]{1,0:T(8,128)(2,1)S(1)}, u32[]{:S(2)}, u32[]{:S(2)}) collective-permute-start(bf16[32,2048]{1,0:T(8,128)(2,1)S(1)} %add_convert_fusion.4), channel_id=1, source_target_pairs={{0,24},{2,26},{4,28},{6,30},{8,16},{10,18},{12,20},{14,22},{16,8},... | collective-permute-start | bytes 393224 | tf_op jit(solution)/shard_map/ppermute | solution.py:414
  127.2 8.7 %collective-permute-start.14 = (bf16[32,2048]{1,0:T(8,128)(2,1)S(1)}, bf16[32,2048]{1,0:T(8,128)(2,1)S(1)}, u32[]{:S(2)}, u32[]{:S(2)}) collective-permute-start(bf16[32,2048]{1,0:T(8,128)(2,1)S(1)} %add_convert_fusion.3), channel_id=1, source_target_pairs={{0,8},{2,10},{4,12},{6,14},{8,0},{10,2},{12,4},{14,6},{16,24},{18,... | collective-permute-start | bytes 393224 | tf_op jit(solution)/shard_map/ppermute | solution.py:414
  137.6 8.3 %collective-permute-start.20 = (bf16[32,2048]{1,0:T(8,128)(2,1)S(1)}, bf16[32,2048]{1,0:T(8,128)(2,1)S(1)}, u32[]{:S(2)}, u32[]{:S(2)}) collective-permute-start(bf16[32,2048]{1,0:T(8,128)(2,1)S(1)} %get-tuple-element.53.refs_0_), channel_id=1, source_target_pairs={{0,24},{2,26},{4,28},{6,30},{8,16},{10,18},{12,20},{14,22},{16,8},... | collective-permute-start | bytes 393224 | tf_op jit(solution)/shard_map/ppermute | solution.py:414
  140.1 12.4 %collective-permute-start.18 = (bf16[32,2048]{1,0:T(8,128)(2,1)S(1)}, bf16[32,2048]{1,0:T(8,128)(2,1)S(1)}, u32[]{:S(2)}, u32[]{:S(2)}) collective-permute-start(bf16[32,2048]{1,0:T(8,128)(2,1)S(1)} %get-tuple-element.53.refs_0_), channel_id=1, source_target_pairs={{0,16},{2,18},{4,20},{6,22},{8,24},{10,26},{12,28},{14,30},{16,0},... | collective-permute-start | bytes 393224 | tf_op jit(solution)/shard_map/ppermute | solution.py:414
  141.7 11.4 %collective-permute-start.16 = (bf16[32,2048]{1,0:T(8,128)(2,1)S(1)}, bf16[32,2048]{1,0:T(8,128)(2,1)S(1)}, u32[]{:S(2)}, u32[]{:S(2)}) collective-permute-start(bf16[32,2048]{1,0:T(8,128)(2,1)S(1)} %get-tuple-element.53.refs_0_), channel_id=1, source_target_pairs={{0,8},{2,10},{4,12},{6,14},{8,0},{10,2},{12,4},{14,6},{16,24},{18,... | collective-permute-start | bytes 393224 | tf_op jit(solution)/shard_map/ppermute | solution.py:414
  145.9 8.6 %collective-permute-start.15 = (bf16[32,2048]{1,0:T(8,128)(2,1)S(1)}, bf16[32,2048]{1,0:T(8,128)(2,1)S(1)}, u32[]{:S(2)}, u32[]{:S(2)}) collective-permute-start(bf16[32,2048]{1,0:T(8,128)(2,1)S(1)} %get-tuple-element.53.refs_0_), channel_id=1, source_target_pairs={{0,4},{2,6},{4,0},{6,2},{8,12},{10,14},{12,8},{14,10},{16,20},{18,... | collective-permute-start | bytes 393224 | tf_op jit(solution)/shard_map/ppermute | solution.py:414
  153.0 8.5 %collective-permute-start.19 = (bf16[32,2048]{1,0:T(8,128)(2,1)S(1)}, bf16[32,2048]{1,0:T(8,128)(2,1)S(1)}, u32[]{:S(2)}, u32[]{:S(2)}) collective-permute-start(bf16[32,2048]{1,0:T(8,128)(2,1)S(1)} %collective-permute-done.18.refs_4_), channel_id=1, source_target_pairs={{0,4},{2,6},{4,0},{6,2},{8,12},{10,14},{12,8},{14,10},{16,20},{18,... | collective-permute-start | bytes 393224 | tf_op jit(solution)/shard_map/ppermute | solution.py:414
  154.5 8.4 %collective-permute-start.17 = (bf16[32,2048]{1,0:T(8,128)(2,1)S(1)}, bf16[32,2048]{1,0:T(8,128)(2,1)S(1)}, u32[]{:S(2)}, u32[]{:S(2)}) collective-permute-start(bf16[32,2048]{1,0:T(8,128)(2,1)S(1)} %collective-permute-done.16.refs_2_), channel_id=1, source_target_pairs={{0,4},{2,6},{4,0},{6,2},{8,12},{10,14},{12,8},{14,10},{16,20},{18,... | collective-permute-start | bytes 393224 | tf_op jit(solution)/shard_map/ppermute | solution.py:414
  168.4 14.3 %collective-permute-start.31 = (bf16[32,2048]{1,0:T(8,128)(2,1)S(1)}, bf16[32,2048]{1,0:T(8,128)(2,1)S(1)}, u32[]{:S(2)}, u32[]{:S(2)}) collective-permute-start(bf16[32,2048]{1,0:T(8,128)(2,1)S(1)} %get-tuple-element.55), channel_id=1, source_target_pairs={{0,4},{2,6},{4,0},{6,2},{8,12},{10,14},{12,8},{14,10},{16,20},{18,... | collective-permute-start | bytes 393224 | tf_op jit(solution)/shard_map/ppermute | solution.py:414
  169.9 9.0 %collective-permute-start.34 = (bf16[32,2048]{1,0:T(8,128)(2,1)S(1)}, bf16[32,2048]{1,0:T(8,128)(2,1)S(1)}, u32[]{:S(2)}, u32[]{:S(2)}) collective-permute-start(bf16[32,2048]{1,0:T(8,128)(2,1)S(1)} %get-tuple-element.59), channel_id=1, source_target_pairs={{0,4},{2,6},{4,0},{6,2},{8,12},{10,14},{12,8},{14,10},{16,20},{18,... | collective-permute-start | bytes 393224 | tf_op jit(solution)/shard_map/ppermute | solution.py:414
  178.8 9.6 %collective-permute-start.33 = (bf16[32,2048]{1,0:T(8,128)(2,1)S(1)}, bf16[32,2048]{1,0:T(8,128)(2,1)S(1)}, u32[]{:S(2)}, u32[]{:S(2)}) collective-permute-start(bf16[32,2048]{1,0:T(8,128)(2,1)S(1)} %add_convert_fusion.2), channel_id=1, source_target_pairs={{0,16},{2,18},{4,20},{6,22},{8,24},{10,26},{12,28},{14,30},{16,0},... | collective-permute-start | bytes 393224 | tf_op jit(solution)/shard_map/ppermute | solution.py:414
  180.2 8.2 %collective-permute-start.35 = (bf16[32,2048]{1,0:T(8,128)(2,1)S(1)}, bf16[32,2048]{1,0:T(8,128)(2,1)S(1)}, u32[]{:S(2)}, u32[]{:S(2)}) collective-permute-start(bf16[32,2048]{1,0:T(8,128)(2,1)S(1)} %add_convert_fusion.1), channel_id=1, source_target_pairs={{0,24},{2,26},{4,28},{6,30},{8,16},{10,18},{12,20},{14,22},{16,8},... | collective-permute-start | bytes 393224 | tf_op jit(solution)/shard_map/ppermute | solution.py:414
  192.0 9.4 %collective-permute-start.41 = (bf16[32,2048]{1,0:T(8,128)(2,1)S(1)}, bf16[32,2048]{1,0:T(8,128)(2,1)S(1)}, u32[]{:S(2)}, u32[]{:S(2)}) collective-permute-start(bf16[32,2048]{1,0:T(8,128)(2,1)S(1)} %residual_norm.3.refs_0_), channel_id=1, source_target_pairs={{0,16},{2,18},{4,20},{6,22},{8,24},{10,26},{12,28},{14,30},{16,0},... | collective-permute-start | bytes 393224 | tf_op jit(solution)/shard_map/ppermute | solution.py:414
  (58 other events, 789.9 us)

commit v3 on v2

--- a/solution.py
+++ b/solution.py
@@ -29,6 +29,11 @@
     return pl.BlockSpec(memory_space=pltpu.MemorySpace.HBM)
 
 
+def place(n_cand):
+    tok = lax.axis_index("tok")
+    return tok % 2, tok // 2, lax.axis_index("cand") // (n_cand // 2)
+
+
 def dot32(a, b):
     return jnp.dot(a, b, preferred_element_type=jnp.float32)
 
@@ -42,14 +47,15 @@
     return 0.5 * v * (1.0 + jnp.tanh(inner))
 
 
-def by_heads_kernel(count, query_ref, keys_ref, values_ref, out_ref, sems):
+def by_heads_kernel(count, n_cand, keys_ref, values_ref, out_ref, sems):
+    query_at = place(n_cand)[2]
     cols = out_ref.shape[3]
     copies = []
     for d in range(count):
         for k, ref in enumerate((keys_ref, values_ref)):
             copies.append(
                 pltpu.make_async_copy(
-                    ref.at[query_ref[0], :, pl.ds(d * cols, cols)], out_ref.at[d, k], sems.at[d, k]
+                    ref.at[query_at, :, pl.ds(d * cols, cols)], out_ref.at[d, k], sems.at[d, k]
                 )
             )
             copies[-1].start()
@@ -57,34 +63,35 @@
         copy.wait()
 
 
-def by_heads(query, keys, values, count):
+def by_heads(query, keys, values, count, n_cand):
     src, model = keys.shape[1:]
     cols = model // count
     if cols % 128:
-        pair = jnp.stack([lax.dynamic_index_in_dim(a, query[0], 0, False) for a in (keys, values)])
+        pair = jnp.stack([lax.dynamic_index_in_dim(a, query, 0, False) for a in (keys, values)])
         return pair.reshape(2, src, count, cols).transpose(2, 0, 1, 3)
     return pl.pallas_call(
-        functools.partial(by_heads_kernel, count),
+        functools.partial(by_heads_kernel, count, n_cand),
         out_shape=jax.ShapeDtypeStruct((count, 2, src, cols), keys.dtype),
-        in_specs=[smem_spec(), hbm_spec(), hbm_spec()],
+        in_specs=[hbm_spec(), hbm_spec()],
         out_specs=vmem_spec(),
         scratch_shapes=[pltpu.SemaphoreType.DMA((count, 2))],
         compiler_params=pltpu.CompilerParams(vmem_limit_bytes=63 << 20),
         name="by_heads",
-    )(query, keys, values)
-
-
-def attention_kernel(live_ref, mine_ref, peer_ref, kv_ref, first_ref, second_ref):
+    )(keys, values)
+
+
+def attention_kernel(n_cand, lengths_ref, mine_ref, peer_ref, kv_ref, first_ref, second_ref):
+    core, _, query_at = place(n_cand)
+    straight = core == query_at
     src = kv_ref.shape[0] * kv_ref.shape[2]
     cols = kv_ref.shape[3]
     keys = kv_ref[:, 0].reshape(src, cols)
     values = kv_ref[:, 1].reshape(src, cols)
     token = lax.broadcasted_iota(jnp.int32, (1, src), 1)
-    bias = jnp.where(token < live_ref[0], 0.0, NEG).astype(jnp.float32)
+    bias = jnp.where(token < lengths_ref[query_at], 0.0, NEG).astype(jnp.float32)
     lane_head = lax.broadcasted_iota(jnp.int32, (1, cols), 1) // HEAD_DIM
     rows = mine_ref.shape[0]
-    step = min(rows, 128)
-    straight = live_ref[1] == 1
+    step = min(rows, 256)
     for out_ref, one_ref, two_ref in (
         (first_ref, mine_ref, peer_ref),
         (second_ref, peer_ref, mine_ref),
@@ -104,26 +111,27 @@
             out_ref[at, :] = mixed.astype(jnp.bfloat16)
 
 
-def attention(live, mine, peer, kv):
+def attention(lengths, mine, peer, kv, n_cand):
     rows, cols = mine.shape
     return pl.pallas_call(
-        attention_kernel,
+        functools.partial(attention_kernel, n_cand),
         out_shape=[jax.ShapeDtypeStruct((rows, cols), jnp.bfloat16)] * 2,
         in_specs=[smem_spec(), vmem_spec(), vmem_spec(), vmem_spec()],
         out_specs=[vmem_spec()] * 2,
         compiler_params=pltpu.CompilerParams(vmem_limit_bytes=24 << 20),
         name="attention",
-    )(live, mine, peer, kv)
-
-
-def project_kernel(n_cand, count, chip_ref, first_ref, second_ref, *refs):
+    )(lengths, mine, peer, kv)
+
+
+def project_kernel(n_cand, count, first_ref, second_ref, *refs):
     weights = refs[: 2 * n_cand]
     outs = refs[2 * n_cand : 2 * n_cand + count]
     own_s, par_s = refs[2 * n_cand + count :]
     share = first_ref.shape[0] // count
-    straight = chip_ref[1] == 1
+    core, chip, query_at = place(n_cand)
+    straight = core == query_at
     for j in range(count):
-        at = pl.multiple_of((chip_ref[0] ^ j) * share, share)
+        at = pl.multiple_of((chip ^ j) * share, share)
         to = slice(j * share, (j + 1) * share)
         first, second = first_ref[pl.ds(at, share), :], second_ref[pl.ds(at, share), :]
         own_s[to, :] = jnp.where(straight, first, second)
@@ -137,43 +145,48 @@
             outs[j][:, s * width : (s + 1) * width] = block[j * share : (j + 1) * share, :]
 
 
-def project(chip, first, second, weights, count):
+def project(first, second, weights, count):
     rows, cols = first.shape
     n_cand = len(weights) // 2
     model = weights[0].shape[1] * n_cand
     return pl.pallas_call(
         functools.partial(project_kernel, n_cand, count),
         out_shape=[jax.ShapeDtypeStruct((rows // count, model), jnp.bfloat16)] * count,
-        in_specs=[smem_spec()] + [vmem_spec()] * (2 + len(weights)),
+        in_specs=[vmem_spec()] * (2 + len(weights)),
         out_specs=[vmem_spec()] * count,
         scratch_shapes=[VMEM((rows, cols), jnp.bfloat16)] * 2,
         compiler_params=pltpu.CompilerParams(vmem_limit_bytes=8 << 20),
         name="project",
-    )(chip, first, second, *weights)
-
-
-def residual_kernel(count, base_ref, gain_ref, *refs):
+    )(first, second, *weights)
+
+
+def residual_kernel(count, n_cand, base_ref, gain_ref, *refs):
     total = base_ref[...].astype(jnp.float32)
     for part in refs[:count]:
         total = total + part[...].astype(jnp.float32)
     squares = jnp.mean(total * total, axis=-1, keepdims=True)
-    refs[count][...] = (total * lax.rsqrt(squares + NORM_EPS) * gain_ref[...]).astype(jnp.bfloat16)
+    scaled = total * lax.rsqrt(squares + NORM_EPS)
+    block = base_ref.shape[1] // n_cand
+    for s in range(n_cand):
+        at = pl.multiple_of(lax.rem(lax.axis_index("cand") + s, n_cand) * block, block)
+        to = slice(s * block, (s + 1) * block)
+        refs[count][:, to] = (scaled[:, to] * gain_ref[:, pl.ds(at, block)]).astype(jnp.bfloat16)
     if len(refs) > count + 1:
         refs[count + 1][...] = total
 
 
-def residual_norm(base, gain, parts, keep):
+def residual_norm(base, gain, parts, n_cand, keep):
     shapes = [jax.ShapeDtypeStruct(base.shape, jnp.bfloat16)]
     if keep:
         shapes.append(jax.ShapeDtypeStruct(base.shape, jnp.float32))
     return pl.pallas_call(
-        functools.partial(residual_kernel, len(parts)),
+        functools.partial(residual_kernel, len(parts), n_cand),
         out_shape=shapes,
         in_specs=[vmem_spec()] * (2 + len(parts)),
         out_specs=[vmem_spec()] * len(shapes),
         compiler_params=pltpu.CompilerParams(vmem_limit_bytes=4 << 20),
         name="residual_norm",
-    )(base, gain, *parts)
+    )(base, gain.reshape(1, -1), *parts)
 
 
 def ffn_kernel(n_cand, count, *refs):
@@ -194,11 +207,11 @@
         for s in range(n_cand):
             i = side * n_cand + s
             block = acts[:, s * depth : (s + 1) * depth]
-            term = dot32_t(block, gates[i][...])
+            term = dot32_t(gates[i][...], block)
             gate_part = term if gate_part is None else gate_part + term
-            term = dot32_t(block, ups[i][...])
+            term = dot32_t(ups[i][...], block)
             up_part = term if up_part is None else up_part + term
-        hidden.append((gelu_tanh(gate_part) * up_part).astype(jnp.bfloat16))
+        hidden.append((gelu_tanh(gate_part) * up_part).astype(jnp.bfloat16).T)
     width = downs[0].shape[1]
     for s in range(n_cand):
         block = dot32(hidden[0], downs[s][...]) + dot32(hidden[1], downs[n_cand + s][...])
@@ -222,60 +235,39 @@
     )(*rows_in, *gates, *ups, *downs)
 
 
-def vocab_kernel(n_cand, count, width, live, flag_ref, gold_ref, *refs):
-    rows_in = refs[: 2 * count]
-    n_w = 2 * n_cand
-    own = refs[2 * count : 2 * count + n_cand]
-    swapped = refs[2 * count + n_cand : 2 * count + n_w]
-    out_ref, acts, held, max_s, sum_s, gold_s, sems = refs[2 * count + n_w :]
-    share = rows_in[0].shape[0]
+def vocab_kernel(n_cand, count, width, live, gold_ref, over_gold_ref, *refs):
+    here, over = refs[:count], refs[count : 2 * count]
+    own, swapped = refs[2 * count : 2 * count + n_cand], refs[2 * count + n_cand : -5]
+    out_ref, acts, max_s, sum_s, gold_s = refs[-5:]
+    share = here[0].shape[0]
     rows = 2 * count * share
     vocab, depth = own[0].shape
-    slots = held.shape[0]
-    chunks = [(at, min(width, vocab - at)) for at in range(0, vocab, width)]
-    mine = flag_ref[0] == 1
-
-    def copy(i, s, source):
-        at, size = chunks[i]
-        return pltpu.make_async_copy(
-            source.at[pl.ds(at, size)], held.at[i % slots, s, pl.ds(0, size)], sems.at[i % slots, s]
-        )
-
-    def start(i):
-        for s in range(n_cand):
-            here, there = (own, swapped) if s == 0 else (swapped, own)
-
-            @pl.when(mine)
-            def _():
-                copy(i, s, here[s]).start()
-
-            @pl.when(jnp.logical_not(mine))
-            def _():
-                copy(i, s, there[s]).start()
-
-    for i in range(min(slots, len(chunks))):
-        start(i)
+    core, chip, query_at = place(n_cand)
+    mine = core == query_at
+    start = (chip * 2 + query_at) * live
+    gold_row = jnp.concatenate([gold_ref[...], over_gold_ref[...]], axis=1) - start
     for j in range(count):
-        at = pl.multiple_of((flag_ref[2] ^ j) * share, share)
-        acts[pl.ds(at, share), :] = rows_in[j][...]
+        at = pl.multiple_of((chip ^ j) * share, share)
+        acts[pl.ds(at, share), :] = here[j][...]
         for s in range(n_cand):
             p = (s - n_cand // 2) % n_cand
-            acts[pl.ds(at + rows // 2, share), s * depth : (s + 1) * depth] = rows_in[count + j][
+            acts[pl.ds(at + rows // 2, share), s * depth : (s + 1) * depth] = over[j][
                 :, p * depth : (p + 1) * depth
             ]
     max_s[...] = jnp.full_like(max_s, NEG)
     sum_s[...] = jnp.zeros_like(sum_s)
     gold_s[...] = jnp.zeros_like(gold_s)
-    for i, (first, size) in enumerate(chunks):
+    for first in range(0, vocab, width):
+        size = min(width, vocab - first)
         logits = None
         for s in range(n_cand):
-            copy(i, s, own[s]).wait()
-            term = dot32_t(held[i % slots, s, :size], acts[:, s * depth : (s + 1) * depth])
+            one, two = (own, swapped) if s == 0 else (swapped, own)
+            at = slice(first, first + size)
+            part = jnp.where(mine, one[s][at, :], two[s][at, :])
+            term = dot32_t(part, acts[:, s * depth : (s + 1) * depth])
             logits = term if logits is None else logits + term
-        if i + slots < len(chunks):
-            start(i + slots)
         column = first + lax.broadcasted_iota(jnp.int32, (size, 1), 0)
-        hit = column == gold_ref[...] - flag_ref[1]
+        hit = column == gold_row
         if first + size > live:
             hit = hit & (column < live)
             logits = jnp.where(column < live, logits, NEG)
@@ -295,31 +287,28 @@
             out_ref[k, i : i + 1, :] = value[:, i * 128 : (i + 1) * 128]
 
 
-def vocab_scores(flags, gold, rows_in, own, swapped, live):
+def vocab_scores(gold, over_gold, rows_in, own, swapped, live):
     count, n_cand = len(rows_in) // 2, len(own)
     share, model = rows_in[0].shape
-    vocab, depth = own[0].shape
+    vocab = own[0].shape[0]
     rows = share * count * 2
-    slots = 3
     width = pl.cdiv(pl.cdiv(vocab, 3), 16) * 16
     assert rows % 256 == 0
+    operands = (gold, over_gold, *rows_in, *own, *swapped)
     return pl.pallas_call(
         functools.partial(vocab_kernel, n_cand, count, width, live),
         out_shape=jax.ShapeDtypeStruct((3, rows // 128, 128), jnp.float32),
-        in_specs=[smem_spec()] + [vmem_spec()] * (1 + len(rows_in)) + [hbm_spec()] * (2 * n_cand),
+        in_specs=[vmem_spec()] * len(operands),
         out_specs=vmem_spec(),
-        scratch_shapes=[
-            VMEM((rows, model), jnp.bfloat16),
-            VMEM((slots, n_cand, width, depth), jnp.bfloat16),
-        ]
-        + [VMEM((8, rows), jnp.float32)] * 3
-        + [pltpu.SemaphoreType.DMA((slots, n_cand))],
-        compiler_params=pltpu.CompilerParams(vmem_limit_bytes=60 << 20),
+        scratch_shapes=[VMEM((rows, model), jnp.bfloat16)] + [VMEM((8, rows), jnp.float32)] * 3,
+        compiler_params=pltpu.CompilerParams(vmem_limit_bytes=20 << 20),
         name="vocab_scores",
-    )(flags, gold, *rows_in, *own, *swapped)
-
-
-def mean_kernel(length, info_ref, here_ref, there_ref, out_ref):
+    )(*operands)
+
+
+def mean_kernel(length, n_cand, counts_ref, here_ref, there_ref, out_ref):
+    core = place(n_cand)[0]
+    cand = lax.axis_index("cand")
     middle = here_ref.shape[1] // 2
     sub = lax.broadcasted_iota(jnp.int32, (middle, 128), 0)
     row = sub * 128 + lax.broadcasted_iota(jnp.int32, (middle, 128), 1)
@@ -333,43 +322,43 @@
         total = here_ref[1, one, :] * jnp.exp(top_here - top)
         total = total + there_ref[1, two, :] * jnp.exp(top_there - top)
         logprob = here_ref[2, one, :] + there_ref[2, two, :] - top - jnp.log(total)
-        first = info_ref[1 + part]
+        first = lax.rem(cand + part * (n_cand // 2), n_cand) * cands
         means = jnp.zeros((1, 128), jnp.float32)
         for c in range(cands):
             picked = jnp.where((row >= c * length) & (row < (c + 1) * length), logprob, 0.0)
             mean = jnp.sum(jnp.sum(picked, axis=0, keepdims=True), axis=1, keepdims=True) / length
             means = jnp.where(lane == c, mean, means)
-            best = jnp.maximum(best, jnp.where(first + c < info_ref[0], mean, NEG))
+            best = jnp.maximum(best, jnp.where(first + c < counts_ref[core], mean, NEG))
         if part == 0:
             own = means
     out_ref[...] = jnp.where(lane < cands, own, best)
 
 
-def candidate_means(info, here, there, length):
-    return pl.pallas_call(
-        functools.partial(mean_kernel, length),
+def candidate_means(counts, here, there, length, n_cand):
+    return pl.pallas_call(
+        functools.partial(mean_kernel, length, n_cand),
         out_shape=jax.ShapeDtypeStruct((1, 128), jnp.float32),
         in_specs=[smem_spec(), vmem_spec(), vmem_spec()],
         out_specs=vmem_spec(),
         compiler_params=pltpu.CompilerParams(vmem_limit_bytes=2 << 20),
         name="candidate_means",
-    )(info, here, there)
-
-
-def result_kernel(info_ref, here_ref, there_ref, scores_ref, best_ref):
+    )(counts, here, there)
+
+
+def result_kernel(n_cand, counts_ref, here_ref, there_ref, scores_ref, best_ref):
     cands = scores_ref.shape[1]
-    low = info_ref[0] == 0
+    low = place(n_cand)[0] == 0
     here, there = here_ref[...], there_ref[...]
-    lane = lax.broadcasted_iota(jnp.int32, (1, cands), 1) + info_ref[1]
+    lane = lax.broadcasted_iota(jnp.int32, (1, cands), 1) + lax.axis_index("cand") * cands
     for q in range(2):
         line = jnp.where(low, here, there) if q == 0 else jnp.where(low, there, here)
-        scores_ref[q : q + 1, :] = jnp.where(lane < info_ref[2 + q], line[:, :cands], 0.0)
+        scores_ref[q : q + 1, :] = jnp.where(lane < counts_ref[q], line[:, :cands], 0.0)
         best_ref[:, q : q + 1] = line[:, cands : cands + 1]
 
 
-def results(info, here, there, cands):
-    return pl.pallas_call(
-        result_kernel,
+def results(counts, here, there, cands, n_cand):
+    return pl.pallas_call(
+        functools.partial(result_kernel, n_cand),
         out_shape=[
             jax.ShapeDtypeStruct((2, cands), jnp.float32),
             jax.ShapeDtypeStruct((1, 2), jnp.float32),
@@ -378,7 +367,7 @@
         out_specs=[vmem_spec(), vmem_spec()],
         compiler_params=pltpu.CompilerParams(vmem_limit_bytes=2 << 20),
         name="results",
-    )(info, here, there)
+    )(counts, here, there)
 
 
 def body(
@@ -432,8 +421,8 @@
             axis=-1,
         )
 
-    def gather_rows(a, both):
-        out, peer = [None] * chips, [None] * chips
+    def gather_rows(a, both=False):
+        out, over = [None] * chips, [None] * chips
         out[0] = a
         for j in range(2, chips, 2):
             out[j] = swap(a, 2 * j)
@@ -442,15 +431,14 @@
         if not both:
             return out
         for j in range(chips):
-            if j % 2 == 0 or j < chips // 2:
-                peer[j] = across(out[j], half)
+            if j % 2 == 0:
+                over[j] = across(out[j], half)
             else:
-                peer[j] = swap(peer[j - 1], 2)
-        return out + peer
+                over[j] = swap(over[j - 1], 2)
+        return out + over
 
     def scatter_rows(parts):
-        order = [j for j in range(2, chips, 2)]
-        order = order[1:] + order[:1] + [0]
+        order = [j for j in range(4, chips, 2)] + [2, 0]
         near = {j: swap(parts[j + 1], 2) for j in order}
         back = [parts[0], near[0]]
         for j in order[:-1]:
@@ -460,7 +448,7 @@
 
     query_at = cand // half
 
-    pair = by_heads(query_at.reshape(1), enc_keys, enc_values, n_tok)
+    pair = by_heads(query_at, enc_keys, enc_values, n_tok, n_cand)
     key_values = lax.all_to_all(pair, "tok", 0, 0, tiled=True)
 
     query_parts = from_cands(w_query)
@@ -474,15 +462,13 @@
         vocab_own = jnp.pad(vocab_own, ((0, -vocab_dev % 8), (0, 0)))
     vocab_swapped = swap(vocab_own, 1)
     gold = lax.dynamic_index_in_dim(gold_ids, core, 0, keepdims=False).reshape(1, rows)
-    gold = jnp.concatenate([gold, across(gold, half)], axis=1)
+    over_gold = across(gold, half)
 
     flat = dec_hidden.reshape(queries * rows, model)
     base = rolled(lax.dynamic_slice_in_dim(flat, core * rows + chip * share, share, 0))
     flat = rolled(flat)
     wide = flat.astype(jnp.float32)
-    gain_first, gain_mid, gain_last = (
-        rolled(g.reshape(1, model)) for g in (gain_cross, gain_ffn, gain_final)
-    )
+    gain_first = rolled(gain_cross.reshape(1, model))
     squares = jnp.mean(wide * wide, axis=-1, keepdims=True)
     normed = (wide * lax.rsqrt(squares + NORM_EPS) * gain_first).astype(jnp.bfloat16)
     query = sum(
@@ -492,20 +478,8 @@
     mine = lax.dynamic_index_in_dim(query, query_at, 0, keepdims=False)
     other = lax.dynamic_index_in_dim(query, 1 - query_at, 0, keepdims=False)
     peer = across(other, half)
-    straight = (core == query_at).astype(jnp.int32)
-    live = jnp.stack([lax.dynamic_index_in_dim(enc_lengths, query_at, 0, keepdims=False), straight])
-    count_here = lax.dynamic_index_in_dim(cand_counts, core, 0, keepdims=False)
-    plane_first, plane_other = cand * cand_dev, ((cand + half) % n_cand) * cand_dev
-    mean_info = jnp.stack([count_here, plane_first, plane_other])
-    result_info = jnp.stack([core, plane_first, cand_counts[0], cand_counts[1]])
-    chip_at = jnp.stack([chip, straight])
-    flags = jnp.stack([straight, (chip * 2 + query_at) * vocab_dev, chip])
-    live, base, gain_mid, gain_last, gold, mean_info, result_info, chip_at, flags = (
-        lax.optimization_barrier(
-            (live, base, gain_mid, gain_last, gold, mean_info, result_info, chip_at, flags)
-        )
-    )
-    first, second = attention(live, mine, peer, key_values)
+    mine, base, gold, over_gold = lax.optimization_barrier((mine, base, gold, over_gold))
+    first, second = attention(enc_lengths, mine, peer, key_values, n_cand)
 
     def route(a, flip):
         perm = []
@@ -526,16 +500,18 @@
                 perm.append(((t + side) * n_cand + (c + s) % n_cand, (t + 1 - side) * n_cand + c))
         vocab_own.append(lax.ppermute(vocab_own[0], ("tok", "cand"), perm))
     vocab_swapped = [vocab_swapped] + [swap(w, 1) for w in vocab_own[1:]]
-    cross_terms = project(chip_at, first, second, out_parts, chips)
+    cross_terms = project(first, second, out_parts, chips)
     cross_terms = scatter_rows(cross_terms)
-    normed_ffn, after_cross = residual_norm(base, gain_mid, cross_terms, True)
-    ffn_rows = gather_rows(normed_ffn, False)
+    normed_ffn, after_cross = residual_norm(base, gain_ffn, cross_terms, n_cand, True)
+    ffn_rows = gather_rows(normed_ffn)
     ffn_terms = feed_forward(ffn_rows, gate_parts, up_parts, down_parts)
     ffn_terms = scatter_rows(ffn_terms)
-    (normed_final,) = residual_norm(after_cross, gain_last, ffn_terms, False)
+    (normed_final,) = residual_norm(after_cross, gain_final, ffn_terms, n_cand, False)
     final_rows = gather_rows(normed_final, True)
 
-    stats = vocab_scores(flags, gold, final_rows, vocab_own, vocab_swapped, vocab_dev)
+    stats = vocab_scores(
+        gold, over_gold, final_rows, vocab_own, vocab_swapped, vocab_dev
+    )
 
     def combine(parts):
         top = functools.reduce(jnp.maximum, [p[0] for p in parts])
@@ -545,14 +521,14 @@
     stats = combine([stats, swap(stats, 2)])
     stats = combine([stats] + [swap(stats, 2 * j) for j in range(2, chips, 2)])
     theirs = across(stats, half)
-    means = candidate_means(mean_info, stats, theirs, length)
+    means = candidate_means(cand_counts, stats, theirs, length, n_cand)
     k = 1
     while k < half:
         other_best = lax.ppermute(means, "cand", [(i, i ^ k) for i in range(n_cand)])
         past = lax.iota(jnp.int32, 128)[None, :] >= cand_dev
         means = jnp.where(past, jnp.maximum(means, other_best), means)
         k *= 2
-    cand_scores, best = results(result_info, means, swap(means, 1), cand_dev)
+    cand_scores, best = results(cand_counts, means, swap(means, 1), cand_dev, n_cand)
     return (cand_scores, best.reshape(2))
 
 

time: 251 us -> 240 us (0.956)
  other arithmetic: 5.92 us -> 1.3 us
  Pallas kernels: 26.5 us -> 22.3 us
  starting transfers between devices: 73.9 us -> 76.6 us
    ppermute x14 -> x12, waiting for transfers between devices: 73.9 us -> 67.9 us  [across(): lax.ppermute(a, 'cand', [(i, (i - shift) % n_cand) for i in range(n_cand)])]
    ppermute x45 -> x47, starting transfers between devices: 44.9 us -> 50.6 us  [swap(): return lax.ppermute(a, 'tok', [(i, i ^ k) for i in range(n_tok)])]
    ppermute x45 -> x47, waiting for transfers between devices: 60.5 us -> 64.3 us  [swap(): return lax.ppermute(a, 'tok', [(i, i ^ k) for i in range(n_tok)])]
    ppermute x14 -> x12, starting transfers between devices: 16.2 us -> 13.6 us  [across(): lax.ppermute(a, 'cand', [(i, (i - shift) % n_cand) for i in range(n_cand)])]
    pallas_call x1, Pallas kernels: 10.1 us -> 7.5 us  [vocab_scores(): pl.pallas_call(functools.partial(vocab_kernel, n_cand, count, width, live...]
  transfers between devices with their start and end apart: 63 -> 63, of which waited for: 37 -> 34; matrix products, arithmetic and copies ran while one was open for 5% -> 3% of each run, Pallas kernels for 6% -> 5%
where the time goes in v3:
time: 240 us
  waiting for transfers between devices  132 us (55%)
  starting transfers between devices  76.6 us (32%)
  Pallas kernels  22.3 us (9%)
  local copies, waits for them, and re-layouts  4.26 us (2%)
    ppermute x12, waiting for transfers between devices, across(): lax.ppermute(a, 'cand', [(i, (i - shift) % n_cand) for i in range(n_cand)])  67.9 us
    ppermute x47, waiting for transfers between devices, swap(): return lax.ppermute(a, 'tok', [(i, i ^ k) for i in range(n_tok)])  64.3 us
    ppermute x47, starting transfers between devices, swap(): return lax.ppermute(a, 'tok', [(i, i ^ k) for i in range(n_tok)])  50.6 us
    ppermute x12, starting transfers between devices, across(): lax.ppermute(a, 'cand', [(i, (i - shift) % n_cand) for i in range(n_cand)])  13.6 us
    pallas_call x1, Pallas kernels, vocab_scores(): pl.pallas_call(functools.partial(vocab_kernel, n_cand, count, width, live...  7.5 us
    all_to_all x1, starting transfers between devices, body(): key_values = lax.all_to_all(pair, 'tok', 0, 0, tiled=True)  5.95 us
  transfers between devices with their start and end apart: 63, of which 34 were waited for; matrix products, arithmetic and copies ran while one was open for 3% of the time, Pallas kernels for 5%

profile of v3, /device:TPU:0, one launch (start us, length us, event | category | flops | bytes accessed | tf_op | source)
XLA Modules:
  0.0 239.6 jit_solution(3876269537613747249)
XLA Ops:
  0.6 2.6 %collective-permute-start.53 = (bf16[2008,1024]{1,0:T(8,128)(2,1)}, bf16[2008,1024]{1,0:T(8,128)(2,1)}, u32[]{:S(2)}, u32[]{:S(2)}) collective-permute-start(bf16[2008,1024]{1,0:T(8,128)(2,1)} %bitcast.17), channel_id=1, source_target_pairs={{1,2},{5,6},{9,10},{13,14},{17,18},{21,22},{25,26},{29,30},{2,1},{... | collective-permute-start | bytes 12337160 | tf_op jit(solution)/shard_map/ppermute | solution.py:501
  3.3 2.3 collective-permute-start
  7.2 2.5 %by_heads.1 = bf16[16,2,128,128]{3,2,1,0:T(8,128)(2,1)} custom-call(bf16[2,128,2048]{2,1,0:T(8,128)(2,1)} %keys_ref.1, bf16[2,128,2048]{2,1,0:T(8,128)(2,1)} %values_ref.1), custom_call_target="tpu_custom_call" | custom-call | tf_op jit(solution)/shard_map/by_heads/pallas_call | solution.py:72
  9.7 6.0 %all-to-all-start = ((bf16[16,2,128,128]{3,2,1,0:T(8,128)(2,1)}), bf16[16,2,128,128]{3,2,1,0:T(8,128)(2,1)S(1)}, u32[]{:S(2)}, u32[]{:S(2)}) async-start(bf16[16,2,128,128]{3,2,1,0:T(8,128)(2,1)} %by_heads.1), calls=%async_computation | async-start | bytes 2097152 | tf_op jit(solution)/shard_map/all_to_all | solution.py:452
  19.0 40.8 %collective-permute-done = bf16[1024,128]{1,0:T(8,128)(2,1)} collective-permute-done((bf16[1024,128]{1,0:T(8,128)(2,1)}, bf16[1024,128]{1,0:T(8,128)(2,1)}, u32[]{:S(2)}, u32[]{:S(2)}) %collective-permute-start) | collective-permute-done | bytes 262176 | tf_op jit(solution)/shard_map/ppermute | solution.py:406
  62.0 2.0 collective-permute-start.1
  64.0 2.4 %collective-permute-done.1.over_gold_ref = s32[1,256]{1,0:T(1,128)S(1)} collective-permute-done((s32[1,256]{1,0:T(1,128)S(1)}, s32[1,256]{1,0:T(1,128)S(1)}, u32[]{:S(2)}, u32[]{:S(2)}) %collective-permute-start.1) | collective-permute-done | bytes 1056 | tf_op jit(solution)/shard_map/ppermute | solution.py:406
  69.9 4.2 %attention.1 = (bf16[256,128]{1,0:T(8,128)(2,1)S(1)}, bf16[256,128]{1,0:T(8,128)(2,1)S(1)}) custom-call(s32[2]{0:T(128)S(1)} %copy-done.12, bf16[256,128]{1,0:T(8,128)(2,1)S(1)} %get-tuple-element.31.mine_ref, bf16[256,128]{1,0:T(8,128)(2,1)S(1)} %collective-permute-done.2.peer_ref, bf16[16,2,128,128]{3,2,1,0:T(8,128)(2,1)S(1)} %all-to-all-done.kv_ref), custom_call_target="tpu_custom_call" | custom-call | tf_op jit(solution)/shard_map/attention/pallas_call | solution.py:116
  74.9 3.0 %collective-permute-start.4 = (bf16[256,128]{1,0:T(8,128)(2,1)S(1)}, bf16[256,128]{1,0:T(8,128)(2,1)S(1)}, u32[]{:S(2)}, u32[]{:S(2)}) collective-permute-start(bf16[256,128]{1,0:T(8,128)(2,1)S(1)} %get-tuple-element.33), channel_id=1, source_target_pairs={{0,1},{1,3},{2,0},{3,2},{4,5},{5,7},{6,4},{7,6},{8,9},{9,11},{10,8... | collective-permute-start | bytes 196616 | tf_op jit(solution)/shard_map/ppermute | solution.py:491
  77.9 5.4 %collective-permute-start.26 = (bf16[320,1024]{1,0:T(8,128)(2,1)S(1)}, bf16[320,1024]{1,0:T(8,128)(2,1)S(1)}, u32[]{:S(2)}, u32[]{:S(2)}) collective-permute-start(bf16[320,1024]{1,0:T(8,128)(2,1)S(1)} %bitcast.23), channel_id=1, source_target_pairs={{0,2},{2,0},{4,6},{6,4},{8,10},{10,8},{12,14},{14,12},{16,18},{18,... | collective-permute-start | bytes 1966088 | tf_op jit(solution)/shard_map/ppermute | solution.py:403
  88.7 3.1 %collective-permute-done.9 = bf16[32,2048]{1,0:T(8,128)(2,1)S(1)} collective-permute-done((bf16[32,2048]{1,0:T(8,128)(2,1)S(1)}, bf16[32,2048]{1,0:T(8,128)(2,1)S(1)}, u32[]{:S(2)}, u32[]{:S(2)}) %collective-permute-start.9) | collective-permute-done | bytes 131104 | tf_op jit(solution)/shard_map/ppermute | solution.py:403
  93.5 7.4 %collective-permute-done.25.refs_13_ = bf16[320,1024]{1,0:T(8,128)(2,1)S(1)} collective-permute-done((bf16[320,1024]{1,0:T(8,128)(2,1)S(1)}, bf16[320,1024]{1,0:T(8,128)(2,1)S(1)}, u32[]{:S(2)}, u32[]{:S(2)}) %collective-permute-start.25) | collective-permute-done | bytes 655392 | tf_op jit(solution)/shard_map/ppermute | solution.py:406
  102.7 11.3 %collective-permute-done.28.refs_17_ = bf16[320,1024]{1,0:T(8,128)(2,1)S(1)} collective-permute-done((bf16[320,1024]{1,0:T(8,128)(2,1)S(1)}, bf16[320,1024]{1,0:T(8,128)(2,1)S(1)}, u32[]{:S(2)}, u32[]{:S(2)}) %collective-permute-start.28) | collective-permute-done | bytes 655392 | tf_op jit(solution)/shard_map/ppermute | solution.py:406
  115.5 2.6 %collective-permute-start.10 = (bf16[32,2048]{1,0:T(8,128)(2,1)S(1)}, bf16[32,2048]{1,0:T(8,128)(2,1)S(1)}, u32[]{:S(2)}, u32[]{:S(2)}) collective-permute-start(bf16[32,2048]{1,0:T(8,128)(2,1)S(1)} %add_convert_fusion.5), channel_id=1, source_target_pairs={{0,16},{2,18},{4,20},{6,22},{8,24},{10,26},{12,28},{14,30},{16,0},... | collective-permute-start | bytes 393224 | tf_op jit(solution)/shard_map/ppermute | solution.py:403
  120.6 6.9 %collective-permute-done.10.refs_2_ = bf16[32,2048]{1,0:T(8,128)(2,1)S(1)} collective-permute-done((bf16[32,2048]{1,0:T(8,128)(2,1)S(1)}, bf16[32,2048]{1,0:T(8,128)(2,1)S(1)}, u32[]{:S(2)}, u32[]{:S(2)}) %collective-permute-start.10) | collective-permute-done | bytes 131104 | tf_op jit(solution)/shard_map/ppermute | solution.py:403
  129.8 2.5 %collective-permute-start.20 = (bf16[32,2048]{1,0:T(8,128)(2,1)S(1)}, bf16[32,2048]{1,0:T(8,128)(2,1)S(1)}, u32[]{:S(2)}, u32[]{:S(2)}) collective-permute-start(bf16[32,2048]{1,0:T(8,128)(2,1)S(1)} %get-tuple-element.43.refs_0_), channel_id=1, source_target_pairs={{0,24},{2,26},{4,28},{6,30},{8,16},{10,18},{12,20},{14,22},{16,8},... | collective-permute-start | bytes 393224 | tf_op jit(solution)/shard_map/ppermute | solution.py:403
  134.3 3.9 %collective-permute-done.20.refs_6_ = bf16[32,2048]{1,0:T(8,128)(2,1)S(1)} collective-permute-done((bf16[32,2048]{1,0:T(8,128)(2,1)S(1)}, bf16[32,2048]{1,0:T(8,128)(2,1)S(1)}, u32[]{:S(2)}, u32[]{:S(2)}) %collective-permute-start.20) | collective-permute-done | bytes 131104 | tf_op jit(solution)/shard_map/ppermute | solution.py:403
  138.7 6.1 %collective-permute-done.18.refs_4_ = bf16[32,2048]{1,0:T(8,128)(2,1)S(1)} collective-permute-done((bf16[32,2048]{1,0:T(8,128)(2,1)S(1)}, bf16[32,2048]{1,0:T(8,128)(2,1)S(1)}, u32[]{:S(2)}, u32[]{:S(2)}) %collective-permute-start.18) | collective-permute-done | bytes 131104 | tf_op jit(solution)/shard_map/ppermute | solution.py:403
  147.3 3.8 %collective-permute-done.21.refs_7_ = bf16[32,2048]{1,0:T(8,128)(2,1)S(1)} collective-permute-done((bf16[32,2048]{1,0:T(8,128)(2,1)S(1)}, bf16[32,2048]{1,0:T(8,128)(2,1)S(1)}, u32[]{:S(2)}, u32[]{:S(2)}) %collective-permute-start.21) | collective-permute-done | bytes 131104 | tf_op jit(solution)/shard_map/ppermute | solution.py:403
  151.1 2.7 %collective-permute-done.19.refs_5_ = bf16[32,2048]{1,0:T(8,128)(2,1)S(1)} collective-permute-done((bf16[32,2048]{1,0:T(8,128)(2,1)S(1)}, bf16[32,2048]{1,0:T(8,128)(2,1)S(1)}, u32[]{:S(2)}, u32[]{:S(2)}) %collective-permute-start.19) | collective-permute-done | bytes 131104 | tf_op jit(solution)/shard_map/ppermute | solution.py:403
  155.2 4.1 %feed_forward.1 = (bf16[32,2048]{1,0:T(8,128)(2,1)S(1)}, bf16[32,2048]{1,0:T(8,128)(2,1)S(1)}, bf16[32,2048]{1,0:T(8,128)(2,1)S(1)}, bf16[32,2048]{1,0:T(8,128)(...) custom-call(bf16[32,2048]{1,0:T(8,128)(2,1)S(1)} %get-tuple-element., ...), custom_call_target="tpu_custom_call" | custom-call | tf_op jit(solution)/shard_map/feed_forward/pallas_call | solution.py:227
  162.0 3.8 %collective-permute-done.32 = bf16[32,2048]{1,0:T(8,128)(2,1)S(1)} collective-permute-done((bf16[32,2048]{1,0:T(8,128)(2,1)S(1)}, bf16[32,2048]{1,0:T(8,128)(2,1)S(1)}, u32[]{:S(2)}, u32[]{:S(2)}) %collective-permute-start.32) | collective-permute-done | bytes 131104 | tf_op jit(solution)/shard_map/ppermute | solution.py:403
  166.4 4.0 %collective-permute-done.34 = bf16[32,2048]{1,0:T(8,128)(2,1)S(1)} collective-permute-done((bf16[32,2048]{1,0:T(8,128)(2,1)S(1)}, bf16[32,2048]{1,0:T(8,128)(2,1)S(1)}, u32[]{:S(2)}, u32[]{:S(2)}) %collective-permute-start.34) | collective-permute-done | bytes 131104 | tf_op jit(solution)/shard_map/ppermute | solution.py:403
  171.8 2.3 collective-permute-start.35
  174.3 5.8 %collective-permute-done.33.refs_2_ = bf16[32,2048]{1,0:T(8,128)(2,1)S(1)} collective-permute-done((bf16[32,2048]{1,0:T(8,128)(2,1)S(1)}, bf16[32,2048]{1,0:T(8,128)(2,1)S(1)}, u32[]{:S(2)}, u32[]{:S(2)}) %collective-permute-start.33) | collective-permute-done | bytes 131104 | tf_op jit(solution)/shard_map/ppermute | solution.py:403
  183.9 2.7 %collective-permute-done.45.refs_8_ = bf16[32,2048]{1,0:T(8,128)(2,1)S(1)} collective-permute-done((bf16[32,2048]{1,0:T(8,128)(2,1)S(1)}, bf16[32,2048]{1,0:T(8,128)(2,1)S(1)}, u32[]{:S(2)}, u32[]{:S(2)}) %collective-permute-start.45) | collective-permute-done | bytes 131104 | tf_op jit(solution)/shard_map/ppermute | solution.py:406
  189.2 3.8 %collective-permute-done.41.refs_4_ = bf16[32,2048]{1,0:T(8,128)(2,1)S(1)} collective-permute-done((bf16[32,2048]{1,0:T(8,128)(2,1)S(1)}, bf16[32,2048]{1,0:T(8,128)(2,1)S(1)}, u32[]{:S(2)}, u32[]{:S(2)}) %collective-permute-start.41) | collective-permute-done | bytes 131104 | tf_op jit(solution)/shard_map/ppermute | solution.py:403
  196.5 2.2 collective-permute-done.46.refs_9_
  215.6 7.5 %vocab_scores.1 = f32[3,4,128]{2,1,0:T(4,128)S(1)} custom-call(s32[1,256]{1,0:T(1,128)S(1)} %copy-done.9, s32[1,256]{1,0:T(1,128)S(1)} %copy-done.11, bf16[32,2048]{1,0:T(8,128)(2,1)S(1)} %residual_norm.3.refs_0_, bf16[32,2048]{1,0:T(8,128)(2,1)S(1)} %collective-permute-done.38.refs_1_, bf16[32,2048]{1,0:T(8,128)(2,1)S(1)} %collective-permute-done.39.refs_2_, ...), custom_call_target="tpu_custom_call" | custom-call | tf_op jit(solution)/shard_map/vocab_scores/pallas_call | solution.py:298
  224.3 2.4 %collective-permute-done.56 = f32[3,4,128]{2,1,0:T(4,128)S(1)} collective-permute-done((f32[3,4,128]{2,1,0:T(4,128)S(1)}, f32[3,4,128]{2,1,0:T(4,128)S(1)}, u32[]{:S(2)}, u32[]{:S(2)}) %collective-permute-start.56) | collective-permute-done | bytes 6176 | tf_op jit(solution)/shard_map/ppermute | solution.py:403
  228.4 2.8 %collective-permute-start.57 = (f32[3,4,128]{2,1,0:T(4,128)S(1)}, f32[3,4,128]{2,1,0:T(4,128)S(1)}, u32[]{:S(2)}, u32[]{:S(2)}) collective-permute-start(f32[3,4,128]{2,1,0:T(4,128)S(1)} %pad_maximum_fusion.3), channel_id=1, source_target_pairs={{0,8},{2,10},{4,12},{6,14},{8,0},{10,2},{12,4},{14,6},{16,24},{18,... | collective-permute-start | bytes 18440 | tf_op jit(solution)/shard_map/ppermute | solution.py:403
  234.2 2.4 %collective-permute-done.60.there_ref = f32[3,4,128]{2,1,0:T(4,128)S(1)} collective-permute-done((f32[3,4,128]{2,1,0:T(4,128)S(1)}, f32[3,4,128]{2,1,0:T(4,128)S(1)}, u32[]{:S(2)}, u32[]{:S(2)}) %collective-permute-start.60) | collective-permute-done | bytes 6176 | tf_op jit(solution)/shard_map/ppermute | solution.py:406
  (158 shorter events, 73.1 us)
Async XLA Ops:
  0.6 101.8 %collective-permute-start.53 = (bf16[2008,1024]{1,0:T(8,128)(2,1)}, bf16[2008,1024]{1,0:T(8,128)(2,1)}, u32[]{:S(2)}, u32[]{:S(2)}) collective-permute-start(bf16[2008,1024]{1,0:T(8,128)(2,1)} %bitcast.17), channel_id=1, source_target_pairs={{1,2},{5,6},{9,10},{13,14},{17,18},{21,22},{25,26},{29,30},{2,1},{... | collective-permute-start | bytes 12337160 | tf_op jit(solution)/shard_map/ppermute | solution.py:501
  3.3 56.6 %collective-permute-start = (bf16[1024,128]{1,0:T(8,128)(2,1)}, bf16[1024,128]{1,0:T(8,128)(2,1)}, u32[]{:S(2)}, u32[]{:S(2)}) collective-permute-start(bf16[1024,128]{1,0:T(8,128)(2,1)} %param.22), channel_id=1, source_target_pairs={{0,1},{1,0},{2,3},{3,2},{4,5},{5,4},{6,7},{7,6},{8,9},{9,8},{10,11... | collective-permute-start | bytes 786440 | tf_op jit(solution)/shard_map/ppermute | solution.py:406
  5.6 62.0 %collective-permute-start.5 = (bf16[128,1024]{1,0:T(8,128)(2,1)}, bf16[128,1024]{1,0:T(8,128)(2,1)}, u32[]{:S(2)}, u32[]{:S(2)}) collective-permute-start(bf16[128,1024]{1,0:T(8,128)(2,1)} %refs_0_.1), channel_id=1, source_target_pairs={{0,1},{1,0},{2,3},{3,2},{4,5},{5,4},{6,7},{7,6},{8,9},{9,8},{10,11... | collective-permute-start | bytes 786440 | tf_op jit(solution)/shard_map/ppermute | solution.py:406
  5.7 81.1 %collective-permute-start.23 = (bf16[320,1024]{1,0:T(8,128)(2,1)}, bf16[320,1024]{1,0:T(8,128)(2,1)}, u32[]{:S(2)}, u32[]{:S(2)}) collective-permute-start(bf16[320,1024]{1,0:T(8,128)(2,1)} %bitcast.20), channel_id=1, source_target_pairs={{0,2},{2,0},{4,6},{6,4},{8,10},{10,8},{12,14},{14,12},{16,18},{18,... | collective-permute-start | bytes 1966088 | tf_op jit(solution)/shard_map/ppermute | solution.py:403
  9.7 59.6 %all-to-all-start = ((bf16[16,2,128,128]{3,2,1,0:T(8,128)(2,1)}), bf16[16,2,128,128]{3,2,1,0:T(8,128)(2,1)S(1)}, u32[]{:S(2)}, u32[]{:S(2)}) async-start(bf16[16,2,128,128]{3,2,1,0:T(8,128)(2,1)} %by_heads.1), calls=%async_computation | async-start | bytes 2097152 | tf_op jit(solution)/shard_map/all_to_all | solution.py:452
  66.4 22.0 %collective-permute-start.22 = (bf16[320,1024]{1,0:T(8,128)(2,1)S(1)}, bf16[320,1024]{1,0:T(8,128)(2,1)}, u32[]{:S(2)}, u32[]{:S(2)}) collective-permute-start(bf16[320,1024]{1,0:T(8,128)(2,1)S(1)} %bitcast.21), channel_id=1, source_target_pairs={{0,1},{1,0},{2,3},{3,2},{4,5},{5,4},{6,7},{7,6},{8,9},{9,8},{10,11... | collective-permute-start | bytes 1966088 | tf_op jit(solution)/shard_map/ppermute | solution.py:406
  67.6 7.3 %collective-permute-start.7 = (bf16[128,1024]{1,0:T(8,128)(2,1)}, bf16[128,1024]{1,0:T(8,128)(2,1)}, u32[]{:S(2)}, u32[]{:S(2)}) collective-permute-start(bf16[128,1024]{1,0:T(8,128)(2,1)} %collective-permute-done.5.refs_1_), channel_id=1, source_target_pairs={{0,2},{2,0},{4,6},{6,4},{8,10},{10,8},{12,14},{14,12},{16,18},{18,... | collective-permute-start | bytes 786440 | tf_op jit(solution)/shard_map/ppermute | solution.py:403
  74.9 8.3 %collective-permute-start.4 = (bf16[256,128]{1,0:T(8,128)(2,1)S(1)}, bf16[256,128]{1,0:T(8,128)(2,1)S(1)}, u32[]{:S(2)}, u32[]{:S(2)}) collective-permute-start(bf16[256,128]{1,0:T(8,128)(2,1)S(1)} %get-tuple-element.33), channel_id=1, source_target_pairs={{0,1},{1,3},{2,0},{3,2},{4,5},{5,7},{6,4},{7,6},{8,9},{9,11},{10,8... | collective-permute-start | bytes 196616 | tf_op jit(solution)/shard_map/ppermute | solution.py:491
  77.9 15.5 %collective-permute-start.26 = (bf16[320,1024]{1,0:T(8,128)(2,1)S(1)}, bf16[320,1024]{1,0:T(8,128)(2,1)S(1)}, u32[]{:S(2)}, u32[]{:S(2)}) collective-permute-start(bf16[320,1024]{1,0:T(8,128)(2,1)S(1)} %bitcast.23), channel_id=1, source_target_pairs={{0,2},{2,0},{4,6},{6,4},{8,10},{10,8},{12,14},{14,12},{16,18},{18,... | collective-permute-start | bytes 1966088 | tf_op jit(solution)/shard_map/ppermute | solution.py:403
  83.3 17.6 %collective-permute-start.25 = (bf16[320,1024]{1,0:T(8,128)(2,1)S(1)}, bf16[320,1024]{1,0:T(8,128)(2,1)S(1)}, u32[]{:S(2)}, u32[]{:S(2)}) collective-permute-start(bf16[320,1024]{1,0:T(8,128)(2,1)S(1)} %bitcast.24), channel_id=1, source_target_pairs={{0,1},{1,0},{2,3},{3,2},{4,5},{5,4},{6,7},{7,6},{8,9},{9,8},{10,11... | collective-permute-start | bytes 1966088 | tf_op jit(solution)/shard_map/ppermute | solution.py:406
  88.4 25.6 %collective-permute-start.28 = (bf16[320,1024]{1,0:T(8,128)(2,1)S(1)}, bf16[320,1024]{1,0:T(8,128)(2,1)S(1)}, u32[]{:S(2)}, u32[]{:S(2)}) collective-permute-start(bf16[320,1024]{1,0:T(8,128)(2,1)S(1)} %copy-done.4), channel_id=1, source_target_pairs={{0,1},{1,0},{2,3},{3,2},{4,5},{5,4},{6,7},{7,6},{8,9},{9,8},{10,11... | collective-permute-start | bytes 1966088 | tf_op jit(solution)/shard_map/ppermute | solution.py:406
  91.9 9.0 %collective-permute-start.11 = (bf16[32,2048]{1,0:T(8,128)(2,1)S(1)}, bf16[32,2048]{1,0:T(8,128)(2,1)S(1)}, u32[]{:S(2)}, u32[]{:S(2)}) collective-permute-start(bf16[32,2048]{1,0:T(8,128)(2,1)S(1)} %get-tuple-element.39), channel_id=1, source_target_pairs={{0,4},{2,6},{4,0},{6,2},{8,12},{10,14},{12,8},{14,10},{16,20},{18,... | collective-permute-start | bytes 393224 | tf_op jit(solution)/shard_map/ppermute | solution.py:403
  93.4 24.8 %collective-permute-start.29 = (bf16[320,1024]{1,0:T(8,128)(2,1)S(1)}, bf16[320,1024]{1,0:T(8,128)(2,1)S(1)}, u32[]{:S(2)}, u32[]{:S(2)}) collective-permute-start(bf16[320,1024]{1,0:T(8,128)(2,1)S(1)} %copy-done.4), channel_id=1, source_target_pairs={{0,2},{2,0},{4,6},{6,4},{8,10},{10,8},{12,14},{14,12},{16,18},{18,... | collective-permute-start | bytes 1966088 | tf_op jit(solution)/shard_map/ppermute | solution.py:403
  100.9 114.6 %collective-permute-start.54 = (bf16[2008,1024]{1,0:T(8,128)(2,1)}, bf16[2008,1024]{1,0:T(8,128)(2,1)S(1)}, u32[]{:S(2)}, u32[]{:S(2)}) collective-permute-start(bf16[2008,1024]{1,0:T(8,128)(2,1)} %bitcast.18), channel_id=1, source_target_pairs={{0,2},{2,0},{4,6},{6,4},{8,10},{10,8},{12,14},{14,12},{16,18},{18,... | collective-permute-start | bytes 12337160 | tf_op jit(solution)/shard_map/ppermute | solution.py:403
  100.9 14.7 %collective-permute-start.13 = (bf16[32,2048]{1,0:T(8,128)(2,1)S(1)}, bf16[32,2048]{1,0:T(8,128)(2,1)S(1)}, u32[]{:S(2)}, u32[]{:S(2)}) collective-permute-start(bf16[32,2048]{1,0:T(8,128)(2,1)S(1)} %get-tuple-element.41), channel_id=1, source_target_pairs={{0,4},{2,6},{4,0},{6,2},{8,12},{10,14},{12,8},{14,10},{16,20},{18,... | collective-permute-start | bytes 393224 | tf_op jit(solution)/shard_map/ppermute | solution.py:403
  102.4 113.1 %collective-permute-start.55 = (bf16[2008,1024]{1,0:T(8,128)(2,1)}, bf16[2008,1024]{1,0:T(8,128)(2,1)S(1)}, u32[]{:S(2)}, u32[]{:S(2)}) collective-permute-start(bf16[2008,1024]{1,0:T(8,128)(2,1)} %collective-permute-done.53.refs_17_), channel_id=1, source_target_pairs={{0,2},{2,0},{4,6},{6,4},{8,10},{10,8},{12,14},{14,12},{16,18},{18,... | collective-permute-start | bytes 12337160 | tf_op jit(solution)/shard_map/ppermute | solution.py:403
  115.5 12.0 %collective-permute-start.10 = (bf16[32,2048]{1,0:T(8,128)(2,1)S(1)}, bf16[32,2048]{1,0:T(8,128)(2,1)S(1)}, u32[]{:S(2)}, u32[]{:S(2)}) collective-permute-start(bf16[32,2048]{1,0:T(8,128)(2,1)S(1)} %add_convert_fusion.5), channel_id=1, source_target_pairs={{0,16},{2,18},{4,20},{6,22},{8,24},{10,26},{12,28},{14,30},{16,0},... | collective-permute-start | bytes 393224 | tf_op jit(solution)/shard_map/ppermute | solution.py:403
  118.2 9.3 %collective-permute-start.12 = (bf16[32,2048]{1,0:T(8,128)(2,1)S(1)}, bf16[32,2048]{1,0:T(8,128)(2,1)S(1)}, u32[]{:S(2)}, u32[]{:S(2)}) collective-permute-start(bf16[32,2048]{1,0:T(8,128)(2,1)S(1)} %add_convert_fusion.4), channel_id=1, source_target_pairs={{0,24},{2,26},{4,28},{6,30},{8,16},{10,18},{12,20},{14,22},{16,8},... | collective-permute-start | bytes 393224 | tf_op jit(solution)/shard_map/ppermute | solution.py:403
  119.6 8.4 %collective-permute-start.14 = (bf16[32,2048]{1,0:T(8,128)(2,1)S(1)}, bf16[32,2048]{1,0:T(8,128)(2,1)S(1)}, u32[]{:S(2)}, u32[]{:S(2)}) collective-permute-start(bf16[32,2048]{1,0:T(8,128)(2,1)S(1)} %add_convert_fusion.3), channel_id=1, source_target_pairs={{0,8},{2,10},{4,12},{6,14},{8,0},{10,2},{12,4},{14,6},{16,24},{18,... | collective-permute-start | bytes 393224 | tf_op jit(solution)/shard_map/ppermute | solution.py:403
  129.8 8.3 %collective-permute-start.20 = (bf16[32,2048]{1,0:T(8,128)(2,1)S(1)}, bf16[32,2048]{1,0:T(8,128)(2,1)S(1)}, u32[]{:S(2)}, u32[]{:S(2)}) collective-permute-start(bf16[32,2048]{1,0:T(8,128)(2,1)S(1)} %get-tuple-element.43.refs_0_), channel_id=1, source_target_pairs={{0,24},{2,26},{4,28},{6,30},{8,16},{10,18},{12,20},{14,22},{16,8},... | collective-permute-start | bytes 393224 | tf_op jit(solution)/shard_map/ppermute | solution.py:403
  132.4 12.4 %collective-permute-start.18 = (bf16[32,2048]{1,0:T(8,128)(2,1)S(1)}, bf16[32,2048]{1,0:T(8,128)(2,1)S(1)}, u32[]{:S(2)}, u32[]{:S(2)}) collective-permute-start(bf16[32,2048]{1,0:T(8,128)(2,1)S(1)} %get-tuple-element.43.refs_0_), channel_id=1, source_target_pairs={{0,16},{2,18},{4,20},{6,22},{8,24},{10,26},{12,28},{14,30},{16,0},... | collective-permute-start | bytes 393224 | tf_op jit(solution)/shard_map/ppermute | solution.py:403
  133.9 11.4 %collective-permute-start.16 = (bf16[32,2048]{1,0:T(8,128)(2,1)S(1)}, bf16[32,2048]{1,0:T(8,128)(2,1)S(1)}, u32[]{:S(2)}, u32[]{:S(2)}) collective-permute-start(bf16[32,2048]{1,0:T(8,128)(2,1)S(1)} %get-tuple-element.43.refs_0_), channel_id=1, source_target_pairs={{0,8},{2,10},{4,12},{6,14},{8,0},{10,2},{12,4},{14,6},{16,24},{18,... | collective-permute-start | bytes 393224 | tf_op jit(solution)/shard_map/ppermute | solution.py:403
  138.2 8.6 %collective-permute-start.15 = (bf16[32,2048]{1,0:T(8,128)(2,1)S(1)}, bf16[32,2048]{1,0:T(8,128)(2,1)S(1)}, u32[]{:S(2)}, u32[]{:S(2)}) collective-permute-start(bf16[32,2048]{1,0:T(8,128)(2,1)S(1)} %get-tuple-element.43.refs_0_), channel_id=1, source_target_pairs={{0,4},{2,6},{4,0},{6,2},{8,12},{10,14},{12,8},{14,10},{16,20},{18,... | collective-permute-start | bytes 393224 | tf_op jit(solution)/shard_map/ppermute | solution.py:403
  145.3 8.5 %collective-permute-start.19 = (bf16[32,2048]{1,0:T(8,128)(2,1)S(1)}, bf16[32,2048]{1,0:T(8,128)(2,1)S(1)}, u32[]{:S(2)}, u32[]{:S(2)}) collective-permute-start(bf16[32,2048]{1,0:T(8,128)(2,1)S(1)} %collective-permute-done.18.refs_4_), channel_id=1, source_target_pairs={{0,4},{2,6},{4,0},{6,2},{8,12},{10,14},{12,8},{14,10},{16,20},{18,... | collective-permute-start | bytes 393224 | tf_op jit(solution)/shard_map/ppermute | solution.py:403
  146.8 8.4 %collective-permute-start.17 = (bf16[32,2048]{1,0:T(8,128)(2,1)S(1)}, bf16[32,2048]{1,0:T(8,128)(2,1)S(1)}, u32[]{:S(2)}, u32[]{:S(2)}) collective-permute-start(bf16[32,2048]{1,0:T(8,128)(2,1)S(1)} %collective-permute-done.16.refs_2_), channel_id=1, source_target_pairs={{0,4},{2,6},{4,0},{6,2},{8,12},{10,14},{12,8},{14,10},{16,20},{18,... | collective-permute-start | bytes 393224 | tf_op jit(solution)/shard_map/ppermute | solution.py:403
  160.0 14.2 %collective-permute-start.31 = (bf16[32,2048]{1,0:T(8,128)(2,1)S(1)}, bf16[32,2048]{1,0:T(8,128)(2,1)S(1)}, u32[]{:S(2)}, u32[]{:S(2)}) collective-permute-start(bf16[32,2048]{1,0:T(8,128)(2,1)S(1)} %get-tuple-element.45), channel_id=1, source_target_pairs={{0,4},{2,6},{4,0},{6,2},{8,12},{10,14},{12,8},{14,10},{16,20},{18,... | collective-permute-start | bytes 393224 | tf_op jit(solution)/shard_map/ppermute | solution.py:403
  161.4 9.0 %collective-permute-start.34 = (bf16[32,2048]{1,0:T(8,128)(2,1)S(1)}, bf16[32,2048]{1,0:T(8,128)(2,1)S(1)}, u32[]{:S(2)}, u32[]{:S(2)}) collective-permute-start(bf16[32,2048]{1,0:T(8,128)(2,1)S(1)} %get-tuple-element.49), channel_id=1, source_target_pairs={{0,4},{2,6},{4,0},{6,2},{8,12},{10,14},{12,8},{14,10},{16,20},{18,... | collective-permute-start | bytes 393224 | tf_op jit(solution)/shard_map/ppermute | solution.py:403
  170.4 9.6 %collective-permute-start.33 = (bf16[32,2048]{1,0:T(8,128)(2,1)S(1)}, bf16[32,2048]{1,0:T(8,128)(2,1)S(1)}, u32[]{:S(2)}, u32[]{:S(2)}) collective-permute-start(bf16[32,2048]{1,0:T(8,128)(2,1)S(1)} %add_convert_fusion.2), channel_id=1, source_target_pairs={{0,16},{2,18},{4,20},{6,22},{8,24},{10,26},{12,28},{14,30},{16,0},... | collective-permute-start | bytes 393224 | tf_op jit(solution)/shard_map/ppermute | solution.py:403
  171.8 8.2 %collective-permute-start.35 = (bf16[32,2048]{1,0:T(8,128)(2,1)S(1)}, bf16[32,2048]{1,0:T(8,128)(2,1)S(1)}, u32[]{:S(2)}, u32[]{:S(2)}) collective-permute-start(bf16[32,2048]{1,0:T(8,128)(2,1)S(1)} %add_convert_fusion.1), channel_id=1, source_target_pairs={{0,24},{2,26},{4,28},{6,30},{8,16},{10,18},{12,20},{14,22},{16,8},... | collective-permute-start | bytes 393224 | tf_op jit(solution)/shard_map/ppermute | solution.py:403
  174.2 7.2 %collective-permute-start.37 = (bf16[32,2048]{1,0:T(8,128)(2,1)S(1)}, bf16[32,2048]{1,0:T(8,128)(2,1)S(1)}, u32[]{:S(2)}, u32[]{:S(2)}) collective-permute-start(bf16[32,2048]{1,0:T(8,128)(2,1)S(1)} %add_convert_fusion), channel_id=1, source_target_pairs={{0,8},{2,10},{4,12},{6,14},{8,0},{10,2},{12,4},{14,6},{16,24},{18,... | collective-permute-start | bytes 393224 | tf_op jit(solution)/shard_map/ppermute | solution.py:403
  183.5 9.4 %collective-permute-start.41 = (bf16[32,2048]{1,0:T(8,128)(2,1)S(1)}, bf16[32,2048]{1,0:T(8,128)(2,1)S(1)}, u32[]{:S(2)}, u32[]{:S(2)}) collective-permute-start(bf16[32,2048]{1,0:T(8,128)(2,1)S(1)} %residual_norm.3.refs_0_), channel_id=1, source_target_pairs={{0,16},{2,18},{4,20},{6,22},{8,24},{10,26},{12,28},{14,30},{16,0},... | collective-permute-start | bytes 393224 | tf_op jit(solution)/shard_map/ppermute | solution.py:403
  186.6 7.2 %collective-permute-start.39 = (bf16[32,2048]{1,0:T(8,128)(2,1)S(1)}, bf16[32,2048]{1,0:T(8,128)(2,1)S(1)}, u32[]{:S(2)}, u32[]{:S(2)}) collective-permute-start(bf16[32,2048]{1,0:T(8,128)(2,1)S(1)} %residual_norm.3.refs_0_), channel_id=1, source_target_pairs={{0,8},{2,10},{4,12},{6,14},{8,0},{10,2},{12,4},{14,6},{16,24},{18,... | collective-permute-start | bytes 393224 | tf_op jit(solution)/shard_map/ppermute | solution.py:403
  (47 other events, 947.5 us)

commit v4 on v3

--- a/solution.py
+++ b/solution.py
@@ -431,7 +431,7 @@
         if not both:
             return out
         for j in range(chips):
-            if j % 2 == 0:
+            if j % 2 == 0 or j < 4:
                 over[j] = across(out[j], half)
             else:
                 over[j] = swap(over[j - 1], 2)
@@ -465,6 +465,7 @@
     over_gold = across(gold, half)
 
     flat = dec_hidden.reshape(queries * rows, model)
+    flat, lengths = lax.optimization_barrier((flat, jnp.maximum(enc_lengths, 1)))
     base = rolled(lax.dynamic_slice_in_dim(flat, core * rows + chip * share, share, 0))
     flat = rolled(flat)
     wide = flat.astype(jnp.float32)
@@ -479,7 +480,7 @@
     other = lax.dynamic_index_in_dim(query, 1 - query_at, 0, keepdims=False)
     peer = across(other, half)
     mine, base, gold, over_gold = lax.optimization_barrier((mine, base, gold, over_gold))
-    first, second = attention(enc_lengths, mine, peer, key_values, n_cand)
+    first, second = attention(lengths, mine, peer, key_values, n_cand)
 
     def route(a, flip):
         perm = []

time: 240 us -> 240 us (level)
    ppermute x12 -> x14, waiting for transfers between devices: 67.9 us -> 73.5 us  [across(): lax.ppermute(a, 'cand', [(i, (i - shift) % n_cand) for i in range(n_cand)])]
    ppermute x47 -> x45, waiting for transfers between devices: 64.3 us -> 58.9 us  [swap(): return lax.ppermute(a, 'tok', [(i, i ^ k) for i in range(n_tok)])]
    ppermute x47 -> x45, starting transfers between devices: 50.6 us -> 49.1 us  [swap(): return lax.ppermute(a, 'tok', [(i, i ^ k) for i in range(n_tok)])]
    ppermute x12 -> x14, starting transfers between devices: 13.6 us -> 13.9 us  [across(): lax.ppermute(a, 'cand', [(i, (i - shift) % n_cand) for i in range(n_cand)])]
  transfers between devices with their start and end apart: 63 -> 63, of which waited for: 34 -> 35; matrix products, arithmetic and copies ran while one was open for 3% -> 3% of each run, Pallas kernels for 5% -> 5%
where the time goes in v4:
time: 240 us; the launch traced here: 239 us
  waiting for transfers between devices  132 us (55%)
  starting transfers between devices  75.5 us (31%)
  Pallas kernels  22.3 us (9%)
  local copies, waits for them, and re-layouts  4.27 us (2%)
    ppermute x14, waiting for transfers between devices, across(): lax.ppermute(a, 'cand', [(i, (i - shift) % n_cand) for i in range(n_cand)])  73.5 us
    ppermute x45, waiting for transfers between devices, swap(): return lax.ppermute(a, 'tok', [(i, i ^ k) for i in range(n_tok)])  58.9 us
    ppermute x45, starting transfers between devices, swap(): return lax.ppermute(a, 'tok', [(i, i ^ k) for i in range(n_tok)])  49.1 us
    ppermute x14, starting transfers between devices, across(): lax.ppermute(a, 'cand', [(i, (i - shift) % n_cand) for i in range(n_cand)])  13.9 us
    pallas_call x1, Pallas kernels, vocab_scores(): pl.pallas_call(functools.partial(vocab_kernel, n_cand, count, width, live...  7.5 us
    all_to_all x1, starting transfers between devices, body(): key_values = lax.all_to_all(pair, 'tok', 0, 0, tiled=True)  5.95 us
  transfers between devices with their start and end apart: 63, of which 35 were waited for; matrix products, arithmetic and copies ran while one was open for 3% of the time, Pallas kernels for 5%

profile of v4, /device:TPU:0, one launch (start us, length us, event | category | flops | bytes accessed | tf_op | source)
XLA Modules:
  0.0 239.3 jit_solution(10745415167022242934)
XLA Ops:
  0.7 2.8 %collective-permute-start.53 = (bf16[2008,1024]{1,0:T(8,128)(2,1)}, bf16[2008,1024]{1,0:T(8,128)(2,1)}, u32[]{:S(2)}, u32[]{:S(2)}) collective-permute-start(bf16[2008,1024]{1,0:T(8,128)(2,1)} %bitcast.17), channel_id=1, source_target_pairs={{1,2},{5,6},{9,10},{13,14},{17,18},{21,22},{25,26},{29,30},{2,1},{... | collective-permute-start | bytes 12337160 | tf_op jit(solution)/shard_map/ppermute | solution.py:502
  3.4 2.3 collective-permute-start
  7.3 2.5 %by_heads.1 = bf16[16,2,128,128]{3,2,1,0:T(8,128)(2,1)} custom-call(bf16[2,128,2048]{2,1,0:T(8,128)(2,1)} %keys_ref.1, bf16[2,128,2048]{2,1,0:T(8,128)(2,1)} %values_ref.1), custom_call_target="tpu_custom_call" | custom-call | tf_op jit(solution)/shard_map/by_heads/pallas_call | solution.py:72
  9.8 6.0 %all-to-all-start = ((bf16[16,2,128,128]{3,2,1,0:T(8,128)(2,1)}), bf16[16,2,128,128]{3,2,1,0:T(8,128)(2,1)S(1)}, u32[]{:S(2)}, u32[]{:S(2)}) async-start(bf16[16,2,128,128]{3,2,1,0:T(8,128)(2,1)} %by_heads.1), calls=%async_computation | async-start | bytes 2097152 | tf_op jit(solution)/shard_map/all_to_all | solution.py:452
  19.7 40.3 %collective-permute-done = bf16[1024,128]{1,0:T(8,128)(2,1)} collective-permute-done((bf16[1024,128]{1,0:T(8,128)(2,1)}, bf16[1024,128]{1,0:T(8,128)(2,1)}, u32[]{:S(2)}, u32[]{:S(2)}) %collective-permute-start) | collective-permute-done | bytes 262176 | tf_op jit(solution)/shard_map/ppermute | solution.py:406
  62.1 2.0 collective-permute-start.1
  64.2 2.4 %collective-permute-done.1.over_gold_ref = s32[1,256]{1,0:T(1,128)S(1)} collective-permute-done((s32[1,256]{1,0:T(1,128)S(1)}, s32[1,256]{1,0:T(1,128)S(1)}, u32[]{:S(2)}, u32[]{:S(2)}) %collective-permute-start.1) | collective-permute-done | bytes 1056 | tf_op jit(solution)/shard_map/ppermute | solution.py:406
  70.1 4.1 %attention.1 = (bf16[256,128]{1,0:T(8,128)(2,1)S(1)}, bf16[256,128]{1,0:T(8,128)(2,1)S(1)}) custom-call(s32[2]{0:T(128)S(1)} %copy-done.12, bf16[256,128]{1,0:T(8,128)(2,1)S(1)} %get-tuple-element.35.mine_ref, bf16[256,128]{1,0:T(8,128)(2,1)S(1)} %collective-permute-done.2.peer_ref, bf16[16,2,128,128]{3,2,1,0:T(8,128)(2,1)S(1)} %all-to-all-done.kv_ref), custom_call_target="tpu_custom_call" | custom-call | tf_op jit(solution)/shard_map/attention/pallas_call | solution.py:116
  75.1 3.0 %collective-permute-start.4 = (bf16[256,128]{1,0:T(8,128)(2,1)S(1)}, bf16[256,128]{1,0:T(8,128)(2,1)S(1)}, u32[]{:S(2)}, u32[]{:S(2)}) collective-permute-start(bf16[256,128]{1,0:T(8,128)(2,1)S(1)} %get-tuple-element.37), channel_id=1, source_target_pairs={{0,1},{1,3},{2,0},{3,2},{4,5},{5,7},{6,4},{7,6},{8,9},{9,11},{10,8... | collective-permute-start | bytes 196616 | tf_op jit(solution)/shard_map/ppermute | solution.py:492
  78.1 5.3 %collective-permute-start.26 = (bf16[320,1024]{1,0:T(8,128)(2,1)S(1)}, bf16[320,1024]{1,0:T(8,128)(2,1)S(1)}, u32[]{:S(2)}, u32[]{:S(2)}) collective-permute-start(bf16[320,1024]{1,0:T(8,128)(2,1)S(1)} %bitcast.23), channel_id=1, source_target_pairs={{0,2},{2,0},{4,6},{6,4},{8,10},{10,8},{12,14},{14,12},{16,18},{18,... | collective-permute-start | bytes 1966088 | tf_op jit(solution)/shard_map/ppermute | solution.py:403
  88.9 3.1 %collective-permute-done.9 = bf16[32,2048]{1,0:T(8,128)(2,1)S(1)} collective-permute-done((bf16[32,2048]{1,0:T(8,128)(2,1)S(1)}, bf16[32,2048]{1,0:T(8,128)(2,1)S(1)}, u32[]{:S(2)}, u32[]{:S(2)}) %collective-permute-start.9) | collective-permute-done | bytes 131104 | tf_op jit(solution)/shard_map/ppermute | solution.py:403
  93.7 7.4 %collective-permute-done.25.refs_13_ = bf16[320,1024]{1,0:T(8,128)(2,1)S(1)} collective-permute-done((bf16[320,1024]{1,0:T(8,128)(2,1)S(1)}, bf16[320,1024]{1,0:T(8,128)(2,1)S(1)}, u32[]{:S(2)}, u32[]{:S(2)}) %collective-permute-start.25) | collective-permute-done | bytes 655392 | tf_op jit(solution)/shard_map/ppermute | solution.py:406
  102.8 11.3 %collective-permute-done.28.refs_17_ = bf16[320,1024]{1,0:T(8,128)(2,1)S(1)} collective-permute-done((bf16[320,1024]{1,0:T(8,128)(2,1)S(1)}, bf16[320,1024]{1,0:T(8,128)(2,1)S(1)}, u32[]{:S(2)}, u32[]{:S(2)}) %collective-permute-start.28) | collective-permute-done | bytes 655392 | tf_op jit(solution)/shard_map/ppermute | solution.py:406
  115.7 2.6 %collective-permute-start.10 = (bf16[32,2048]{1,0:T(8,128)(2,1)S(1)}, bf16[32,2048]{1,0:T(8,128)(2,1)S(1)}, u32[]{:S(2)}, u32[]{:S(2)}) collective-permute-start(bf16[32,2048]{1,0:T(8,128)(2,1)S(1)} %add_convert_fusion.5), channel_id=1, source_target_pairs={{0,16},{2,18},{4,20},{6,22},{8,24},{10,26},{12,28},{14,30},{16,0},... | collective-permute-start | bytes 393224 | tf_op jit(solution)/shard_map/ppermute | solution.py:403
  120.7 6.9 %collective-permute-done.10.refs_2_ = bf16[32,2048]{1,0:T(8,128)(2,1)S(1)} collective-permute-done((bf16[32,2048]{1,0:T(8,128)(2,1)S(1)}, bf16[32,2048]{1,0:T(8,128)(2,1)S(1)}, u32[]{:S(2)}, u32[]{:S(2)}) %collective-permute-start.10) | collective-permute-done | bytes 131104 | tf_op jit(solution)/shard_map/ppermute | solution.py:403
  130.0 2.5 %collective-permute-start.20 = (bf16[32,2048]{1,0:T(8,128)(2,1)S(1)}, bf16[32,2048]{1,0:T(8,128)(2,1)S(1)}, u32[]{:S(2)}, u32[]{:S(2)}) collective-permute-start(bf16[32,2048]{1,0:T(8,128)(2,1)S(1)} %get-tuple-element.47.refs_0_), channel_id=1, source_target_pairs={{0,24},{2,26},{4,28},{6,30},{8,16},{10,18},{12,20},{14,22},{16,8},... | collective-permute-start | bytes 393224 | tf_op jit(solution)/shard_map/ppermute | solution.py:403
  134.4 3.9 %collective-permute-done.20.refs_6_ = bf16[32,2048]{1,0:T(8,128)(2,1)S(1)} collective-permute-done((bf16[32,2048]{1,0:T(8,128)(2,1)S(1)}, bf16[32,2048]{1,0:T(8,128)(2,1)S(1)}, u32[]{:S(2)}, u32[]{:S(2)}) %collective-permute-start.20) | collective-permute-done | bytes 131104 | tf_op jit(solution)/shard_map/ppermute | solution.py:403
  138.8 6.1 %collective-permute-done.18.refs_4_ = bf16[32,2048]{1,0:T(8,128)(2,1)S(1)} collective-permute-done((bf16[32,2048]{1,0:T(8,128)(2,1)S(1)}, bf16[32,2048]{1,0:T(8,128)(2,1)S(1)}, u32[]{:S(2)}, u32[]{:S(2)}) %collective-permute-start.18) | collective-permute-done | bytes 131104 | tf_op jit(solution)/shard_map/ppermute | solution.py:403
  147.5 3.8 %collective-permute-done.21.refs_7_ = bf16[32,2048]{1,0:T(8,128)(2,1)S(1)} collective-permute-done((bf16[32,2048]{1,0:T(8,128)(2,1)S(1)}, bf16[32,2048]{1,0:T(8,128)(2,1)S(1)}, u32[]{:S(2)}, u32[]{:S(2)}) %collective-permute-start.21) | collective-permute-done | bytes 131104 | tf_op jit(solution)/shard_map/ppermute | solution.py:403
  151.3 2.7 %collective-permute-done.19.refs_5_ = bf16[32,2048]{1,0:T(8,128)(2,1)S(1)} collective-permute-done((bf16[32,2048]{1,0:T(8,128)(2,1)S(1)}, bf16[32,2048]{1,0:T(8,128)(2,1)S(1)}, u32[]{:S(2)}, u32[]{:S(2)}) %collective-permute-start.19) | collective-permute-done | bytes 131104 | tf_op jit(solution)/shard_map/ppermute | solution.py:403
  155.4 4.1 %feed_forward.1 = (bf16[32,2048]{1,0:T(8,128)(2,1)S(1)}, bf16[32,2048]{1,0:T(8,128)(2,1)S(1)}, bf16[32,2048]{1,0:T(8,128)(2,1)S(1)}, bf16[32,2048]{1,0:T(8,128)(...) custom-call(bf16[32,2048]{1,0:T(8,128)(2,1)S(1)} %get-tuple-element., ...), custom_call_target="tpu_custom_call" | custom-call | tf_op jit(solution)/shard_map/feed_forward/pallas_call | solution.py:227
  162.2 3.8 %collective-permute-done.32 = bf16[32,2048]{1,0:T(8,128)(2,1)S(1)} collective-permute-done((bf16[32,2048]{1,0:T(8,128)(2,1)S(1)}, bf16[32,2048]{1,0:T(8,128)(2,1)S(1)}, u32[]{:S(2)}, u32[]{:S(2)}) %collective-permute-start.32) | collective-permute-done | bytes 131104 | tf_op jit(solution)/shard_map/ppermute | solution.py:403
  166.5 4.0 %collective-permute-done.34 = bf16[32,2048]{1,0:T(8,128)(2,1)S(1)} collective-permute-done((bf16[32,2048]{1,0:T(8,128)(2,1)S(1)}, bf16[32,2048]{1,0:T(8,128)(2,1)S(1)}, u32[]{:S(2)}, u32[]{:S(2)}) %collective-permute-start.34) | collective-permute-done | bytes 131104 | tf_op jit(solution)/shard_map/ppermute | solution.py:403
  172.0 2.3 collective-permute-start.35
  174.4 5.8 %collective-permute-done.33.refs_2_ = bf16[32,2048]{1,0:T(8,128)(2,1)S(1)} collective-permute-done((bf16[32,2048]{1,0:T(8,128)(2,1)S(1)}, bf16[32,2048]{1,0:T(8,128)(2,1)S(1)}, u32[]{:S(2)}, u32[]{:S(2)}) %collective-permute-start.33) | collective-permute-done | bytes 131104 | tf_op jit(solution)/shard_map/ppermute | solution.py:403
  184.0 2.8 %collective-permute-done.45.refs_8_ = bf16[32,2048]{1,0:T(8,128)(2,1)S(1)} collective-permute-done((bf16[32,2048]{1,0:T(8,128)(2,1)S(1)}, bf16[32,2048]{1,0:T(8,128)(2,1)S(1)}, u32[]{:S(2)}, u32[]{:S(2)}) %collective-permute-start.45) | collective-permute-done | bytes 131104 | tf_op jit(solution)/shard_map/ppermute | solution.py:406
  189.3 3.7 %collective-permute-done.41.refs_4_ = bf16[32,2048]{1,0:T(8,128)(2,1)S(1)} collective-permute-done((bf16[32,2048]{1,0:T(8,128)(2,1)S(1)}, bf16[32,2048]{1,0:T(8,128)(2,1)S(1)}, u32[]{:S(2)}, u32[]{:S(2)}) %collective-permute-start.41) | collective-permute-done | bytes 131104 | tf_op jit(solution)/shard_map/ppermute | solution.py:403
  195.7 3.2 %collective-permute-done.51.refs_14_ = bf16[32,2048]{1,0:T(8,128)(2,1)S(1)} collective-permute-done((bf16[32,2048]{1,0:T(8,128)(2,1)S(1)}, bf16[32,2048]{1,0:T(8,128)(2,1)S(1)}, u32[]{:S(2)}, u32[]{:S(2)}) %collective-permute-start.51) | collective-permute-done | bytes 131104 | tf_op jit(solution)/shard_map/ppermute | solution.py:406
  214.5 7.5 %vocab_scores.1 = f32[3,4,128]{2,1,0:T(4,128)S(1)} custom-call(s32[1,256]{1,0:T(1,128)S(1)} %copy-done.9, s32[1,256]{1,0:T(1,128)S(1)} %copy-done.11, bf16[32,2048]{1,0:T(8,128)(2,1)S(1)} %residual_norm.3.refs_0_, bf16[32,2048]{1,0:T(8,128)(2,1)S(1)} %collective-permute-done.38.refs_1_, bf16[32,2048]{1,0:T(8,128)(2,1)S(1)} %collective-permute-done.39.refs_2_, ...), custom_call_target="tpu_custom_call" | custom-call | tf_op jit(solution)/shard_map/vocab_scores/pallas_call | solution.py:298
  222.0 2.3 collective-permute-start.56
  226.9 2.0 collective-permute-start.58
  233.5 2.8 %collective-permute-done.60.there_ref = f32[3,4,128]{2,1,0:T(4,128)S(1)} collective-permute-done((f32[3,4,128]{2,1,0:T(4,128)S(1)}, f32[3,4,128]{2,1,0:T(4,128)S(1)}, u32[]{:S(2)}, u32[]{:S(2)}) %collective-permute-start.60) | collective-permute-done | bytes 6176 | tf_op jit(solution)/shard_map/ppermute | solution.py:406
  (161 shorter events, 72.7 us)
Async XLA Ops:
  0.7 101.9 %collective-permute-start.53 = (bf16[2008,1024]{1,0:T(8,128)(2,1)}, bf16[2008,1024]{1,0:T(8,128)(2,1)}, u32[]{:S(2)}, u32[]{:S(2)}) collective-permute-start(bf16[2008,1024]{1,0:T(8,128)(2,1)} %bitcast.17), channel_id=1, source_target_pairs={{1,2},{5,6},{9,10},{13,14},{17,18},{21,22},{25,26},{29,30},{2,1},{... | collective-permute-start | bytes 12337160 | tf_op jit(solution)/shard_map/ppermute | solution.py:502
  3.4 56.6 %collective-permute-start = (bf16[1024,128]{1,0:T(8,128)(2,1)}, bf16[1024,128]{1,0:T(8,128)(2,1)}, u32[]{:S(2)}, u32[]{:S(2)}) collective-permute-start(bf16[1024,128]{1,0:T(8,128)(2,1)} %param.22), channel_id=1, source_target_pairs={{0,1},{1,0},{2,3},{3,2},{4,5},{5,4},{6,7},{7,6},{8,9},{9,8},{10,11... | collective-permute-start | bytes 786440 | tf_op jit(solution)/shard_map/ppermute | solution.py:406
  5.8 62.0 %collective-permute-start.5 = (bf16[128,1024]{1,0:T(8,128)(2,1)}, bf16[128,1024]{1,0:T(8,128)(2,1)}, u32[]{:S(2)}, u32[]{:S(2)}) collective-permute-start(bf16[128,1024]{1,0:T(8,128)(2,1)} %refs_0_.1), channel_id=1, source_target_pairs={{0,1},{1,0},{2,3},{3,2},{4,5},{5,4},{6,7},{7,6},{8,9},{9,8},{10,11... | collective-permute-start | bytes 786440 | tf_op jit(solution)/shard_map/ppermute | solution.py:406
  5.8 81.1 %collective-permute-start.23 = (bf16[320,1024]{1,0:T(8,128)(2,1)}, bf16[320,1024]{1,0:T(8,128)(2,1)}, u32[]{:S(2)}, u32[]{:S(2)}) collective-permute-start(bf16[320,1024]{1,0:T(8,128)(2,1)} %bitcast.20), channel_id=1, source_target_pairs={{0,2},{2,0},{4,6},{6,4},{8,10},{10,8},{12,14},{14,12},{16,18},{18,... | collective-permute-start | bytes 1966088 | tf_op jit(solution)/shard_map/ppermute | solution.py:403
  9.8 59.6 %all-to-all-start = ((bf16[16,2,128,128]{3,2,1,0:T(8,128)(2,1)}), bf16[16,2,128,128]{3,2,1,0:T(8,128)(2,1)S(1)}, u32[]{:S(2)}, u32[]{:S(2)}) async-start(bf16[16,2,128,128]{3,2,1,0:T(8,128)(2,1)} %by_heads.1), calls=%async_computation | async-start | bytes 2097152 | tf_op jit(solution)/shard_map/all_to_all | solution.py:452
  66.6 22.0 %collective-permute-start.22 = (bf16[320,1024]{1,0:T(8,128)(2,1)S(1)}, bf16[320,1024]{1,0:T(8,128)(2,1)}, u32[]{:S(2)}, u32[]{:S(2)}) collective-permute-start(bf16[320,1024]{1,0:T(8,128)(2,1)S(1)} %bitcast.21), channel_id=1, source_target_pairs={{0,1},{1,0},{2,3},{3,2},{4,5},{5,4},{6,7},{7,6},{8,9},{9,8},{10,11... | collective-permute-start | bytes 1966088 | tf_op jit(solution)/shard_map/ppermute | solution.py:406
  67.8 7.3 %collective-permute-start.7 = (bf16[128,1024]{1,0:T(8,128)(2,1)}, bf16[128,1024]{1,0:T(8,128)(2,1)}, u32[]{:S(2)}, u32[]{:S(2)}) collective-permute-start(bf16[128,1024]{1,0:T(8,128)(2,1)} %collective-permute-done.5.refs_1_), channel_id=1, source_target_pairs={{0,2},{2,0},{4,6},{6,4},{8,10},{10,8},{12,14},{14,12},{16,18},{18,... | collective-permute-start | bytes 786440 | tf_op jit(solution)/shard_map/ppermute | solution.py:403
  75.1 8.3 %collective-permute-start.4 = (bf16[256,128]{1,0:T(8,128)(2,1)S(1)}, bf16[256,128]{1,0:T(8,128)(2,1)S(1)}, u32[]{:S(2)}, u32[]{:S(2)}) collective-permute-start(bf16[256,128]{1,0:T(8,128)(2,1)S(1)} %get-tuple-element.37), channel_id=1, source_target_pairs={{0,1},{1,3},{2,0},{3,2},{4,5},{5,7},{6,4},{7,6},{8,9},{9,11},{10,8... | collective-permute-start | bytes 196616 | tf_op jit(solution)/shard_map/ppermute | solution.py:492
  78.1 15.5 %collective-permute-start.26 = (bf16[320,1024]{1,0:T(8,128)(2,1)S(1)}, bf16[320,1024]{1,0:T(8,128)(2,1)S(1)}, u32[]{:S(2)}, u32[]{:S(2)}) collective-permute-start(bf16[320,1024]{1,0:T(8,128)(2,1)S(1)} %bitcast.23), channel_id=1, source_target_pairs={{0,2},{2,0},{4,6},{6,4},{8,10},{10,8},{12,14},{14,12},{16,18},{18,... | collective-permute-start | bytes 1966088 | tf_op jit(solution)/shard_map/ppermute | solution.py:403
  83.4 17.6 %collective-permute-start.25 = (bf16[320,1024]{1,0:T(8,128)(2,1)S(1)}, bf16[320,1024]{1,0:T(8,128)(2,1)S(1)}, u32[]{:S(2)}, u32[]{:S(2)}) collective-permute-start(bf16[320,1024]{1,0:T(8,128)(2,1)S(1)} %bitcast.24), channel_id=1, source_target_pairs={{0,1},{1,0},{2,3},{3,2},{4,5},{5,4},{6,7},{7,6},{8,9},{9,8},{10,11... | collective-permute-start | bytes 1966088 | tf_op jit(solution)/shard_map/ppermute | solution.py:406
  88.6 25.6 %collective-permute-start.28 = (bf16[320,1024]{1,0:T(8,128)(2,1)S(1)}, bf16[320,1024]{1,0:T(8,128)(2,1)S(1)}, u32[]{:S(2)}, u32[]{:S(2)}) collective-permute-start(bf16[320,1024]{1,0:T(8,128)(2,1)S(1)} %copy-done.4), channel_id=1, source_target_pairs={{0,1},{1,0},{2,3},{3,2},{4,5},{5,4},{6,7},{7,6},{8,9},{9,8},{10,11... | collective-permute-start | bytes 1966088 | tf_op jit(solution)/shard_map/ppermute | solution.py:406
  92.0 9.0 %collective-permute-start.11 = (bf16[32,2048]{1,0:T(8,128)(2,1)S(1)}, bf16[32,2048]{1,0:T(8,128)(2,1)S(1)}, u32[]{:S(2)}, u32[]{:S(2)}) collective-permute-start(bf16[32,2048]{1,0:T(8,128)(2,1)S(1)} %get-tuple-element.43), channel_id=1, source_target_pairs={{0,4},{2,6},{4,0},{6,2},{8,12},{10,14},{12,8},{14,10},{16,20},{18,... | collective-permute-start | bytes 393224 | tf_op jit(solution)/shard_map/ppermute | solution.py:403
  93.6 24.8 %collective-permute-start.29 = (bf16[320,1024]{1,0:T(8,128)(2,1)S(1)}, bf16[320,1024]{1,0:T(8,128)(2,1)S(1)}, u32[]{:S(2)}, u32[]{:S(2)}) collective-permute-start(bf16[320,1024]{1,0:T(8,128)(2,1)S(1)} %copy-done.4), channel_id=1, source_target_pairs={{0,2},{2,0},{4,6},{6,4},{8,10},{10,8},{12,14},{14,12},{16,18},{18,... | collective-permute-start | bytes 1966088 | tf_op jit(solution)/shard_map/ppermute | solution.py:403
  101.0 113.4 %collective-permute-start.54 = (bf16[2008,1024]{1,0:T(8,128)(2,1)}, bf16[2008,1024]{1,0:T(8,128)(2,1)S(1)}, u32[]{:S(2)}, u32[]{:S(2)}) collective-permute-start(bf16[2008,1024]{1,0:T(8,128)(2,1)} %bitcast.18), channel_id=1, source_target_pairs={{0,2},{2,0},{4,6},{6,4},{8,10},{10,8},{12,14},{14,12},{16,18},{18,... | collective-permute-start | bytes 12337160 | tf_op jit(solution)/shard_map/ppermute | solution.py:403
  101.0 14.7 %collective-permute-start.13 = (bf16[32,2048]{1,0:T(8,128)(2,1)S(1)}, bf16[32,2048]{1,0:T(8,128)(2,1)S(1)}, u32[]{:S(2)}, u32[]{:S(2)}) collective-permute-start(bf16[32,2048]{1,0:T(8,128)(2,1)S(1)} %get-tuple-element.45), channel_id=1, source_target_pairs={{0,4},{2,6},{4,0},{6,2},{8,12},{10,14},{12,8},{14,10},{16,20},{18,... | collective-permute-start | bytes 393224 | tf_op jit(solution)/shard_map/ppermute | solution.py:403
  102.6 111.9 %collective-permute-start.55 = (bf16[2008,1024]{1,0:T(8,128)(2,1)}, bf16[2008,1024]{1,0:T(8,128)(2,1)S(1)}, u32[]{:S(2)}, u32[]{:S(2)}) collective-permute-start(bf16[2008,1024]{1,0:T(8,128)(2,1)} %collective-permute-done.53.refs_17_), channel_id=1, source_target_pairs={{0,2},{2,0},{4,6},{6,4},{8,10},{10,8},{12,14},{14,12},{16,18},{18,... | collective-permute-start | bytes 12337160 | tf_op jit(solution)/shard_map/ppermute | solution.py:403
  115.7 12.0 %collective-permute-start.10 = (bf16[32,2048]{1,0:T(8,128)(2,1)S(1)}, bf16[32,2048]{1,0:T(8,128)(2,1)S(1)}, u32[]{:S(2)}, u32[]{:S(2)}) collective-permute-start(bf16[32,2048]{1,0:T(8,128)(2,1)S(1)} %add_convert_fusion.5), channel_id=1, source_target_pairs={{0,16},{2,18},{4,20},{6,22},{8,24},{10,26},{12,28},{14,30},{16,0},... | collective-permute-start | bytes 393224 | tf_op jit(solution)/shard_map/ppermute | solution.py:403
  118.3 9.3 %collective-permute-start.12 = (bf16[32,2048]{1,0:T(8,128)(2,1)S(1)}, bf16[32,2048]{1,0:T(8,128)(2,1)S(1)}, u32[]{:S(2)}, u32[]{:S(2)}) collective-permute-start(bf16[32,2048]{1,0:T(8,128)(2,1)S(1)} %add_convert_fusion.4), channel_id=1, source_target_pairs={{0,24},{2,26},{4,28},{6,30},{8,16},{10,18},{12,20},{14,22},{16,8},... | collective-permute-start | bytes 393224 | tf_op jit(solution)/shard_map/ppermute | solution.py:403
  119.8 8.4 %collective-permute-start.14 = (bf16[32,2048]{1,0:T(8,128)(2,1)S(1)}, bf16[32,2048]{1,0:T(8,128)(2,1)S(1)}, u32[]{:S(2)}, u32[]{:S(2)}) collective-permute-start(bf16[32,2048]{1,0:T(8,128)(2,1)S(1)} %add_convert_fusion.3), channel_id=1, source_target_pairs={{0,8},{2,10},{4,12},{6,14},{8,0},{10,2},{12,4},{14,6},{16,24},{18,... | collective-permute-start | bytes 393224 | tf_op jit(solution)/shard_map/ppermute | solution.py:403
  130.0 8.3 %collective-permute-start.20 = (bf16[32,2048]{1,0:T(8,128)(2,1)S(1)}, bf16[32,2048]{1,0:T(8,128)(2,1)S(1)}, u32[]{:S(2)}, u32[]{:S(2)}) collective-permute-start(bf16[32,2048]{1,0:T(8,128)(2,1)S(1)} %get-tuple-element.47.refs_0_), channel_id=1, source_target_pairs={{0,24},{2,26},{4,28},{6,30},{8,16},{10,18},{12,20},{14,22},{16,8},... | collective-permute-start | bytes 393224 | tf_op jit(solution)/shard_map/ppermute | solution.py:403
  132.5 12.4 %collective-permute-start.18 = (bf16[32,2048]{1,0:T(8,128)(2,1)S(1)}, bf16[32,2048]{1,0:T(8,128)(2,1)S(1)}, u32[]{:S(2)}, u32[]{:S(2)}) collective-permute-start(bf16[32,2048]{1,0:T(8,128)(2,1)S(1)} %get-tuple-element.47.refs_0_), channel_id=1, source_target_pairs={{0,16},{2,18},{4,20},{6,22},{8,24},{10,26},{12,28},{14,30},{16,0},... | collective-permute-start | bytes 393224 | tf_op jit(solution)/shard_map/ppermute | solution.py:403
  134.1 11.4 %collective-permute-start.16 = (bf16[32,2048]{1,0:T(8,128)(2,1)S(1)}, bf16[32,2048]{1,0:T(8,128)(2,1)S(1)}, u32[]{:S(2)}, u32[]{:S(2)}) collective-permute-start(bf16[32,2048]{1,0:T(8,128)(2,1)S(1)} %get-tuple-element.47.refs_0_), channel_id=1, source_target_pairs={{0,8},{2,10},{4,12},{6,14},{8,0},{10,2},{12,4},{14,6},{16,24},{18,... | collective-permute-start | bytes 393224 | tf_op jit(solution)/shard_map/ppermute | solution.py:403
  138.3 8.6 %collective-permute-start.15 = (bf16[32,2048]{1,0:T(8,128)(2,1)S(1)}, bf16[32,2048]{1,0:T(8,128)(2,1)S(1)}, u32[]{:S(2)}, u32[]{:S(2)}) collective-permute-start(bf16[32,2048]{1,0:T(8,128)(2,1)S(1)} %get-tuple-element.47.refs_0_), channel_id=1, source_target_pairs={{0,4},{2,6},{4,0},{6,2},{8,12},{10,14},{12,8},{14,10},{16,20},{18,... | collective-permute-start | bytes 393224 | tf_op jit(solution)/shard_map/ppermute | solution.py:403
  145.5 8.5 %collective-permute-start.19 = (bf16[32,2048]{1,0:T(8,128)(2,1)S(1)}, bf16[32,2048]{1,0:T(8,128)(2,1)S(1)}, u32[]{:S(2)}, u32[]{:S(2)}) collective-permute-start(bf16[32,2048]{1,0:T(8,128)(2,1)S(1)} %collective-permute-done.18.refs_4_), channel_id=1, source_target_pairs={{0,4},{2,6},{4,0},{6,2},{8,12},{10,14},{12,8},{14,10},{16,20},{18,... | collective-permute-start | bytes 393224 | tf_op jit(solution)/shard_map/ppermute | solution.py:403
  146.9 8.4 %collective-permute-start.17 = (bf16[32,2048]{1,0:T(8,128)(2,1)S(1)}, bf16[32,2048]{1,0:T(8,128)(2,1)S(1)}, u32[]{:S(2)}, u32[]{:S(2)}) collective-permute-start(bf16[32,2048]{1,0:T(8,128)(2,1)S(1)} %collective-permute-done.16.refs_2_), channel_id=1, source_target_pairs={{0,4},{2,6},{4,0},{6,2},{8,12},{10,14},{12,8},{14,10},{16,20},{18,... | collective-permute-start | bytes 393224 | tf_op jit(solution)/shard_map/ppermute | solution.py:403
  160.1 14.2 %collective-permute-start.31 = (bf16[32,2048]{1,0:T(8,128)(2,1)S(1)}, bf16[32,2048]{1,0:T(8,128)(2,1)S(1)}, u32[]{:S(2)}, u32[]{:S(2)}) collective-permute-start(bf16[32,2048]{1,0:T(8,128)(2,1)S(1)} %get-tuple-element.49), channel_id=1, source_target_pairs={{0,4},{2,6},{4,0},{6,2},{8,12},{10,14},{12,8},{14,10},{16,20},{18,... | collective-permute-start | bytes 393224 | tf_op jit(solution)/shard_map/ppermute | solution.py:403
  161.6 9.0 %collective-permute-start.34 = (bf16[32,2048]{1,0:T(8,128)(2,1)S(1)}, bf16[32,2048]{1,0:T(8,128)(2,1)S(1)}, u32[]{:S(2)}, u32[]{:S(2)}) collective-permute-start(bf16[32,2048]{1,0:T(8,128)(2,1)S(1)} %get-tuple-element.53), channel_id=1, source_target_pairs={{0,4},{2,6},{4,0},{6,2},{8,12},{10,14},{12,8},{14,10},{16,20},{18,... | collective-permute-start | bytes 393224 | tf_op jit(solution)/shard_map/ppermute | solution.py:403
  170.6 9.6 %collective-permute-start.33 = (bf16[32,2048]{1,0:T(8,128)(2,1)S(1)}, bf16[32,2048]{1,0:T(8,128)(2,1)S(1)}, u32[]{:S(2)}, u32[]{:S(2)}) collective-permute-start(bf16[32,2048]{1,0:T(8,128)(2,1)S(1)} %add_convert_fusion.2), channel_id=1, source_target_pairs={{0,16},{2,18},{4,20},{6,22},{8,24},{10,26},{12,28},{14,30},{16,0},... | collective-permute-start | bytes 393224 | tf_op jit(solution)/shard_map/ppermute | solution.py:403
  172.0 8.2 %collective-permute-start.35 = (bf16[32,2048]{1,0:T(8,128)(2,1)S(1)}, bf16[32,2048]{1,0:T(8,128)(2,1)S(1)}, u32[]{:S(2)}, u32[]{:S(2)}) collective-permute-start(bf16[32,2048]{1,0:T(8,128)(2,1)S(1)} %add_convert_fusion.1), channel_id=1, source_target_pairs={{0,24},{2,26},{4,28},{6,30},{8,16},{10,18},{12,20},{14,22},{16,8},... | collective-permute-start | bytes 393224 | tf_op jit(solution)/shard_map/ppermute | solution.py:403
  174.4 7.2 %collective-permute-start.37 = (bf16[32,2048]{1,0:T(8,128)(2,1)S(1)}, bf16[32,2048]{1,0:T(8,128)(2,1)S(1)}, u32[]{:S(2)}, u32[]{:S(2)}) collective-permute-start(bf16[32,2048]{1,0:T(8,128)(2,1)S(1)} %add_convert_fusion), channel_id=1, source_target_pairs={{0,8},{2,10},{4,12},{6,14},{8,0},{10,2},{12,4},{14,6},{16,24},{18,... | collective-permute-start | bytes 393224 | tf_op jit(solution)/shard_map/ppermute | solution.py:403
  183.7 9.4 %collective-permute-start.41 = (bf16[32,2048]{1,0:T(8,128)(2,1)S(1)}, bf16[32,2048]{1,0:T(8,128)(2,1)S(1)}, u32[]{:S(2)}, u32[]{:S(2)}) collective-permute-start(bf16[32,2048]{1,0:T(8,128)(2,1)S(1)} %residual_norm.3.refs_0_), channel_id=1, source_target_pairs={{0,16},{2,18},{4,20},{6,22},{8,24},{10,26},{12,28},{14,30},{16,0},... | collective-permute-start | bytes 393224 | tf_op jit(solution)/shard_map/ppermute | solution.py:403
  186.8 7.9 %collective-permute-start.39 = (bf16[32,2048]{1,0:T(8,128)(2,1)S(1)}, bf16[32,2048]{1,0:T(8,128)(2,1)S(1)}, u32[]{:S(2)}, u32[]{:S(2)}) collective-permute-start(bf16[32,2048]{1,0:T(8,128)(2,1)S(1)} %residual_norm.3.refs_0_), channel_id=1, source_target_pairs={{0,8},{2,10},{4,12},{6,14},{8,0},{10,2},{12,4},{14,6},{16,24},{18,... | collective-permute-start | bytes 393224 | tf_op jit(solution)/shard_map/ppermute | solution.py:403
  (48 other events, 951.3 us)

commit v5 on v4

--- a/solution.py
+++ b/solution.py
@@ -75,20 +75,19 @@
         in_specs=[hbm_spec(), hbm_spec()],
         out_specs=vmem_spec(),
         scratch_shapes=[pltpu.SemaphoreType.DMA((count, 2))],
-        compiler_params=pltpu.CompilerParams(vmem_limit_bytes=63 << 20),
+        compiler_params=pltpu.CompilerParams(vmem_limit_bytes=62 << 20),
         name="by_heads",
     )(keys, values)
 
 
-def attention_kernel(n_cand, lengths_ref, mine_ref, peer_ref, kv_ref, first_ref, second_ref):
+def attention_kernel(n_cand, bias_ref, mine_ref, peer_ref, kv_ref, first_ref, second_ref):
     core, _, query_at = place(n_cand)
     straight = core == query_at
     src = kv_ref.shape[0] * kv_ref.shape[2]
     cols = kv_ref.shape[3]
     keys = kv_ref[:, 0].reshape(src, cols)
     values = kv_ref[:, 1].reshape(src, cols)
-    token = lax.broadcasted_iota(jnp.int32, (1, src), 1)
-    bias = jnp.where(token < lengths_ref[query_at], 0.0, NEG).astype(jnp.float32)
+    bias = bias_ref[...]
     lane_head = lax.broadcasted_iota(jnp.int32, (1, cols), 1) // HEAD_DIM
     rows = mine_ref.shape[0]
     step = min(rows, 256)
@@ -111,16 +110,16 @@
             out_ref[at, :] = mixed.astype(jnp.bfloat16)
 
 
-def attention(lengths, mine, peer, kv, n_cand):
+def attention(bias, mine, peer, kv, n_cand):
     rows, cols = mine.shape
     return pl.pallas_call(
         functools.partial(attention_kernel, n_cand),
         out_shape=[jax.ShapeDtypeStruct((rows, cols), jnp.bfloat16)] * 2,
-        in_specs=[smem_spec(), vmem_spec(), vmem_spec(), vmem_spec()],
+        in_specs=[vmem_spec()] * 4,
         out_specs=[vmem_spec()] * 2,
         compiler_params=pltpu.CompilerParams(vmem_limit_bytes=24 << 20),
         name="attention",
-    )(lengths, mine, peer, kv)
+    )(bias, mine, peer, kv)
 
 
 def project_kernel(n_cand, count, first_ref, second_ref, *refs):
@@ -160,33 +159,30 @@
     )(first, second, *weights)
 
 
-def residual_kernel(count, n_cand, base_ref, gain_ref, *refs):
-    total = base_ref[...].astype(jnp.float32)
+def residual_kernel(count, which, base_ref, gains_ref, *refs):
+    share = refs[0].shape[0]
+    total = base_ref[:share, :].astype(jnp.float32)
     for part in refs[:count]:
         total = total + part[...].astype(jnp.float32)
     squares = jnp.mean(total * total, axis=-1, keepdims=True)
-    scaled = total * lax.rsqrt(squares + NORM_EPS)
-    block = base_ref.shape[1] // n_cand
-    for s in range(n_cand):
-        at = pl.multiple_of(lax.rem(lax.axis_index("cand") + s, n_cand) * block, block)
-        to = slice(s * block, (s + 1) * block)
-        refs[count][:, to] = (scaled[:, to] * gain_ref[:, pl.ds(at, block)]).astype(jnp.bfloat16)
+    gain = gains_ref[share + which : share + which + 1, :]
+    refs[count][...] = (total * lax.rsqrt(squares + NORM_EPS) * gain).astype(jnp.bfloat16)
     if len(refs) > count + 1:
         refs[count + 1][...] = total
 
 
-def residual_norm(base, gain, parts, n_cand, keep):
-    shapes = [jax.ShapeDtypeStruct(base.shape, jnp.bfloat16)]
+def residual_norm(base, gains, parts, which, keep):
+    shapes = [jax.ShapeDtypeStruct(parts[0].shape, jnp.bfloat16)]
     if keep:
-        shapes.append(jax.ShapeDtypeStruct(base.shape, jnp.float32))
-    return pl.pallas_call(
-        functools.partial(residual_kernel, len(parts), n_cand),
+        shapes.append(jax.ShapeDtypeStruct(parts[0].shape, jnp.float32))
+    return pl.pallas_call(
+        functools.partial(residual_kernel, len(parts), which),
         out_shape=shapes,
         in_specs=[vmem_spec()] * (2 + len(parts)),
         out_specs=[vmem_spec()] * len(shapes),
         compiler_params=pltpu.CompilerParams(vmem_limit_bytes=4 << 20),
         name="residual_norm",
-    )(base, gain.reshape(1, -1), *parts)
+    )(base, gains, *parts)
 
 
 def ffn_kernel(n_cand, count, *refs):
@@ -465,8 +461,15 @@
     over_gold = across(gold, half)
 
     flat = dec_hidden.reshape(queries * rows, model)
-    flat, lengths = lax.optimization_barrier((flat, jnp.maximum(enc_lengths, 1)))
+    token = lax.iota(jnp.int32, enc_keys.shape[1] * n_tok)[None, :]
+    length_here = lax.dynamic_index_in_dim(enc_lengths, query_at, 0, keepdims=False)
+    bias = jnp.where(token < length_here, 0.0, NEG).astype(jnp.float32)
+    flat, bias = lax.optimization_barrier((flat, bias))
     base = rolled(lax.dynamic_slice_in_dim(flat, core * rows + chip * share, share, 0))
+    base = jnp.concatenate(
+        [base.astype(jnp.float32)]
+        + [rolled(gain.reshape(1, model)) for gain in (gain_ffn, gain_final)]
+    )
     flat = rolled(flat)
     wide = flat.astype(jnp.float32)
     gain_first = rolled(gain_cross.reshape(1, model))
@@ -480,7 +483,7 @@
     other = lax.dynamic_index_in_dim(query, 1 - query_at, 0, keepdims=False)
     peer = across(other, half)
     mine, base, gold, over_gold = lax.optimization_barrier((mine, base, gold, over_gold))
-    first, second = attention(lengths, mine, peer, key_values, n_cand)
+    first, second = attention(bias, mine, peer, key_values, n_cand)
 
     def route(a, flip):
         perm = []
@@ -503,11 +506,11 @@
     vocab_swapped = [vocab_swapped] + [swap(w, 1) for w in vocab_own[1:]]
     cross_terms = project(first, second, out_parts, chips)
     cross_terms = scatter_rows(cross_terms)
-    normed_ffn, after_cross = residual_norm(base, gain_ffn, cross_terms, n_cand, True)
+    normed_ffn, after_cross = residual_norm(base, base, cross_terms, 0, True)
     ffn_rows = gather_rows(normed_ffn)
     ffn_terms = feed_forward(ffn_rows, gate_parts, up_parts, down_parts)
     ffn_terms = scatter_rows(ffn_terms)
-    (normed_final,) = residual_norm(after_cross, gain_final, ffn_terms, n_cand, False)
+    (normed_final,) = residual_norm(after_cross, base, ffn_terms, 1, False)
     final_rows = gather_rows(normed_final, True)
 
     stats = vocab_scores(

time: 240 us -> 248 us (1.033)
  waiting for transfers between devices: 132 us -> 142 us
  starting transfers between devices: 75.5 us -> 71.9 us
    ppermute x14, waiting for transfers between devices: 73.5 us -> 82.5 us  [across(): lax.ppermute(a, 'cand', [(i, (i - shift) % n_cand) for i in range(n_cand)])]
    ppermute x45, starting transfers between devices: 49.1 us -> 45.5 us  [swap(): return lax.ppermute(a, 'tok', [(i, i ^ k) for i in range(n_tok)])]
  transfers between devices with their start and end apart: 63 -> 63, of which waited for: 35 -> 34; matrix products, arithmetic and copies ran while one was open for 3% -> 4% of each run, Pallas kernels for 5% -> 5%
where the time goes in v5:
time: 248 us; the launch traced here: 247 us
  waiting for transfers between devices  142 us (57%)
  starting transfers between devices  71.9 us (29%)
  Pallas kernels  21.6 us (9%)
  local copies, waits for them, and re-layouts  4.25 us (2%)
  matrix products  2.88 us (1%)
  other arithmetic  2.86 us (1%)
    ppermute x14, waiting for transfers between devices, across(): lax.ppermute(a, 'cand', [(i, (i - shift) % n_cand) for i in range(n_cand)])  82.5 us
    ppermute x45, waiting for transfers between devices, swap(): return lax.ppermute(a, 'tok', [(i, i ^ k) for i in range(n_tok)])  59.9 us
    ppermute x45, starting transfers between devices, swap(): return lax.ppermute(a, 'tok', [(i, i ^ k) for i in range(n_tok)])  45.5 us
    ppermute x14, starting transfers between devices, across(): lax.ppermute(a, 'cand', [(i, (i - shift) % n_cand) for i in range(n_cand)])  13.5 us
    pallas_call x1, Pallas kernels, vocab_scores(): pl.pallas_call(functools.partial(vocab_kernel, n_cand, count, width, live...  7.36 us
    all_to_all x1, starting transfers between devices, body(): key_values = lax.all_to_all(pair, 'tok', 0, 0, tiled=True)  5.95 us
  transfers between devices with their start and end apart: 63, of which 34 were waited for; matrix products, arithmetic and copies ran while one was open for 4% of the time, Pallas kernels for 5%

profile of v5, /device:TPU:0, one launch (start us, length us, event | category | flops | bytes accessed | tf_op | source)
XLA Modules:
  0.0 247.0 jit_solution(3076104228428099987)
XLA Ops:
  0.7 2.8 %collective-permute-start.53 = (bf16[2008,1024]{1,0:T(8,128)(2,1)}, bf16[2008,1024]{1,0:T(8,128)(2,1)}, u32[]{:S(2)}, u32[]{:S(2)}) collective-permute-start(bf16[2008,1024]{1,0:T(8,128)(2,1)} %bitcast.20), channel_id=1, source_target_pairs={{1,2},{5,6},{9,10},{13,14},{17,18},{21,22},{25,26},{29,30},{2,1},{... | collective-permute-start | bytes 12337160 | tf_op jit(solution)/shard_map/ppermute | solution.py:505
  3.4 2.4 collective-permute-start.23
  8.3 2.5 %by_heads.1 = bf16[16,2,128,128]{3,2,1,0:T(8,128)(2,1)} custom-call(bf16[2,128,2048]{2,1,0:T(8,128)(2,1)} %keys_ref.1, bf16[2,128,2048]{2,1,0:T(8,128)(2,1)} %values_ref.1), custom_call_target="tpu_custom_call" | custom-call | tf_op jit(solution)/shard_map/by_heads/pallas_call | solution.py:72
  10.8 6.0 %all-to-all-start = ((bf16[16,2,128,128]{3,2,1,0:T(8,128)(2,1)}), bf16[16,2,128,128]{3,2,1,0:T(8,128)(2,1)S(1)}, u32[]{:S(2)}, u32[]{:S(2)}) async-start(bf16[16,2,128,128]{3,2,1,0:T(8,128)(2,1)} %by_heads.1), calls=%async_computation | async-start | bytes 2097152 | tf_op jit(solution)/shard_map/all_to_all | solution.py:448
  24.3 47.0 %collective-permute-done = bf16[1024,128]{1,0:T(8,128)(2,1)} collective-permute-done((bf16[1024,128]{1,0:T(8,128)(2,1)}, bf16[1024,128]{1,0:T(8,128)(2,1)}, u32[]{:S(2)}, u32[]{:S(2)}) %collective-permute-start) | collective-permute-done | bytes 262176 | tf_op jit(solution)/shard_map/ppermute | solution.py:402
  72.7 2.1 collective-permute-start.2
  75.7 4.3 %collective-permute-done.5.refs_1_ = bf16[128,1024]{1,0:T(8,128)(2,1)} collective-permute-done((bf16[128,1024]{1,0:T(8,128)(2,1)}, bf16[128,1024]{1,0:T(8,128)(2,1)}, u32[]{:S(2)}, u32[]{:S(2)}) %collective-permute-start.5) | collective-permute-done | bytes 262176 | tf_op jit(solution)/shard_map/ppermute | solution.py:402
  80.7 3.5 %attention.1 = (bf16[256,128]{1,0:T(8,128)(2,1)S(1)}, bf16[256,128]{1,0:T(8,128)(2,1)S(1)}) custom-call(f32[1,2048]{1,0:T(1,128)S(1)} %compare_select_fusion.bias_ref, bf16[256,128]{1,0:T(8,128)(2,1)S(1)} %get-tuple-element.35.mine_ref, bf16[256,128]{1,0:T(8,128)(2,1)S(1)} %collective-permute-done.2.peer_ref, bf16[16,2,128,128]{3,2,1,0:T(8,128)(2,1)S(1)} %all-to-all-done.kv_ref), custom_call_target="tpu_custom_call" | custom-call | tf_op jit(solution)/shard_map/attention/pallas_call | solution.py:115
  85.1 3.4 %collective-permute-start.4 = (bf16[256,128]{1,0:T(8,128)(2,1)S(1)}, bf16[256,128]{1,0:T(8,128)(2,1)S(1)}, u32[]{:S(2)}, u32[]{:S(2)}) collective-permute-start(bf16[256,128]{1,0:T(8,128)(2,1)S(1)} %get-tuple-element.37), channel_id=1, source_target_pairs={{0,1},{1,3},{2,0},{3,2},{4,5},{5,7},{6,4},{7,6},{8,9},{9,11},{10,8... | collective-permute-start | bytes 196616 | tf_op jit(solution)/shard_map/ppermute | solution.py:495
  90.5 2.3 collective-permute-start.25
  96.3 3.4 %collective-permute-done.9 = bf16[32,2048]{1,0:T(8,128)(2,1)S(1)} collective-permute-done((bf16[32,2048]{1,0:T(8,128)(2,1)S(1)}, bf16[32,2048]{1,0:T(8,128)(2,1)S(1)}, u32[]{:S(2)}, u32[]{:S(2)}) %collective-permute-start.9) | collective-permute-done | bytes 131104 | tf_op jit(solution)/shard_map/ppermute | solution.py:399
  101.3 7.0 %collective-permute-done.25.refs_13_ = bf16[320,1024]{1,0:T(8,128)(2,1)S(1)} collective-permute-done((bf16[320,1024]{1,0:T(8,128)(2,1)S(1)}, bf16[320,1024]{1,0:T(8,128)(2,1)S(1)}, u32[]{:S(2)}, u32[]{:S(2)}) %collective-permute-start.25) | collective-permute-done | bytes 655392 | tf_op jit(solution)/shard_map/ppermute | solution.py:402
  110.1 11.6 %collective-permute-done.28.refs_17_ = bf16[320,1024]{1,0:T(8,128)(2,1)S(1)} collective-permute-done((bf16[320,1024]{1,0:T(8,128)(2,1)S(1)}, bf16[320,1024]{1,0:T(8,128)(2,1)S(1)}, u32[]{:S(2)}, u32[]{:S(2)}) %collective-permute-start.28) | collective-permute-done | bytes 655392 | tf_op jit(solution)/shard_map/ppermute | solution.py:402
  123.2 2.6 %collective-permute-start.10 = (bf16[32,2048]{1,0:T(8,128)(2,1)S(1)}, bf16[32,2048]{1,0:T(8,128)(2,1)S(1)}, u32[]{:S(2)}, u32[]{:S(2)}) collective-permute-start(bf16[32,2048]{1,0:T(8,128)(2,1)S(1)} %add_convert_fusion.5), channel_id=1, source_target_pairs={{0,16},{2,18},{4,20},{6,22},{8,24},{10,26},{12,28},{14,30},{16,0},... | collective-permute-start | bytes 393224 | tf_op jit(solution)/shard_map/ppermute | solution.py:399
  128.3 7.2 %collective-permute-done.10.refs_2_ = bf16[32,2048]{1,0:T(8,128)(2,1)S(1)} collective-permute-done((bf16[32,2048]{1,0:T(8,128)(2,1)S(1)}, bf16[32,2048]{1,0:T(8,128)(2,1)S(1)}, u32[]{:S(2)}, u32[]{:S(2)}) %collective-permute-start.10) | collective-permute-done | bytes 131104 | tf_op jit(solution)/shard_map/ppermute | solution.py:399
  137.8 2.4 collective-permute-start.20
  142.2 3.9 %collective-permute-done.20.refs_6_ = bf16[32,2048]{1,0:T(8,128)(2,1)S(1)} collective-permute-done((bf16[32,2048]{1,0:T(8,128)(2,1)S(1)}, bf16[32,2048]{1,0:T(8,128)(2,1)S(1)}, u32[]{:S(2)}, u32[]{:S(2)}) %collective-permute-start.20) | collective-permute-done | bytes 131104 | tf_op jit(solution)/shard_map/ppermute | solution.py:399
  146.5 6.1 %collective-permute-done.18.refs_4_ = bf16[32,2048]{1,0:T(8,128)(2,1)S(1)} collective-permute-done((bf16[32,2048]{1,0:T(8,128)(2,1)S(1)}, bf16[32,2048]{1,0:T(8,128)(2,1)S(1)}, u32[]{:S(2)}, u32[]{:S(2)}) %collective-permute-start.18) | collective-permute-done | bytes 131104 | tf_op jit(solution)/shard_map/ppermute | solution.py:399
  155.2 3.8 %collective-permute-done.21.refs_7_ = bf16[32,2048]{1,0:T(8,128)(2,1)S(1)} collective-permute-done((bf16[32,2048]{1,0:T(8,128)(2,1)S(1)}, bf16[32,2048]{1,0:T(8,128)(2,1)S(1)}, u32[]{:S(2)}, u32[]{:S(2)}) %collective-permute-start.21) | collective-permute-done | bytes 131104 | tf_op jit(solution)/shard_map/ppermute | solution.py:399
  159.0 2.7 %collective-permute-done.19.refs_5_ = bf16[32,2048]{1,0:T(8,128)(2,1)S(1)} collective-permute-done((bf16[32,2048]{1,0:T(8,128)(2,1)S(1)}, bf16[32,2048]{1,0:T(8,128)(2,1)S(1)}, u32[]{:S(2)}, u32[]{:S(2)}) %collective-permute-start.19) | collective-permute-done | bytes 131104 | tf_op jit(solution)/shard_map/ppermute | solution.py:399
  163.1 4.1 %feed_forward.1 = (bf16[32,2048]{1,0:T(8,128)(2,1)S(1)}, bf16[32,2048]{1,0:T(8,128)(2,1)S(1)}, bf16[32,2048]{1,0:T(8,128)(2,1)S(1)}, bf16[32,2048]{1,0:T(8,128)(...) custom-call(bf16[32,2048]{1,0:T(8,128)(2,1)S(1)} %get-tuple-element., ...), custom_call_target="tpu_custom_call" | custom-call | tf_op jit(solution)/shard_map/feed_forward/pallas_call | solution.py:223
  169.8 3.8 %collective-permute-done.32 = bf16[32,2048]{1,0:T(8,128)(2,1)S(1)} collective-permute-done((bf16[32,2048]{1,0:T(8,128)(2,1)S(1)}, bf16[32,2048]{1,0:T(8,128)(2,1)S(1)}, u32[]{:S(2)}, u32[]{:S(2)}) %collective-permute-start.32) | collective-permute-done | bytes 131104 | tf_op jit(solution)/shard_map/ppermute | solution.py:399
  174.2 4.0 %collective-permute-done.34 = bf16[32,2048]{1,0:T(8,128)(2,1)S(1)} collective-permute-done((bf16[32,2048]{1,0:T(8,128)(2,1)S(1)}, bf16[32,2048]{1,0:T(8,128)(2,1)S(1)}, u32[]{:S(2)}, u32[]{:S(2)}) %collective-permute-start.34) | collective-permute-done | bytes 131104 | tf_op jit(solution)/shard_map/ppermute | solution.py:399
  179.7 2.4 collective-permute-start.35
  182.2 5.8 %collective-permute-done.33.refs_2_ = bf16[32,2048]{1,0:T(8,128)(2,1)S(1)} collective-permute-done((bf16[32,2048]{1,0:T(8,128)(2,1)S(1)}, bf16[32,2048]{1,0:T(8,128)(2,1)S(1)}, u32[]{:S(2)}, u32[]{:S(2)}) %collective-permute-start.33) | collective-permute-done | bytes 131104 | tf_op jit(solution)/shard_map/ppermute | solution.py:399
  191.7 2.8 %collective-permute-done.45.refs_8_ = bf16[32,2048]{1,0:T(8,128)(2,1)S(1)} collective-permute-done((bf16[32,2048]{1,0:T(8,128)(2,1)S(1)}, bf16[32,2048]{1,0:T(8,128)(2,1)S(1)}, u32[]{:S(2)}, u32[]{:S(2)}) %collective-permute-start.45) | collective-permute-done | bytes 131104 | tf_op jit(solution)/shard_map/ppermute | solution.py:402
  197.0 3.8 %collective-permute-done.41.refs_4_ = bf16[32,2048]{1,0:T(8,128)(2,1)S(1)} collective-permute-done((bf16[32,2048]{1,0:T(8,128)(2,1)S(1)}, bf16[32,2048]{1,0:T(8,128)(2,1)S(1)}, u32[]{:S(2)}, u32[]{:S(2)}) %collective-permute-start.41) | collective-permute-done | bytes 131104 | tf_op jit(solution)/shard_map/ppermute | solution.py:399
  203.4 3.3 %collective-permute-done.51.refs_14_ = bf16[32,2048]{1,0:T(8,128)(2,1)S(1)} collective-permute-done((bf16[32,2048]{1,0:T(8,128)(2,1)S(1)}, bf16[32,2048]{1,0:T(8,128)(2,1)S(1)}, u32[]{:S(2)}, u32[]{:S(2)}) %collective-permute-start.51) | collective-permute-done | bytes 131104 | tf_op jit(solution)/shard_map/ppermute | solution.py:402
  222.4 7.4 %vocab_scores.1 = f32[3,4,128]{2,1,0:T(4,128)S(1)} custom-call(s32[1,256]{1,0:T(1,128)S(1)} %reshape.48.gold_ref, s32[1,256]{1,0:T(1,128)S(1)} %collective-permute-done.1.over_gold_ref, bf16[32,2048]{1,0:T(8,128)(2,1)S(1)} %residual_norm.3.refs_0_, bf16[32,2048]{1,0:T(8,128)(2,1)S(1)} %collective-permute-done.38.refs_1_, ...), custom_call_target="tpu_custom_call" | custom-call | tf_op jit(solution)/shard_map/vocab_scores/pallas_call | solution.py:294
  229.7 2.2 collective-permute-start.56
  234.5 2.1 collective-permute-start.58
  241.2 2.7 %collective-permute-done.60.there_ref = f32[3,4,128]{2,1,0:T(4,128)S(1)} collective-permute-done((f32[3,4,128]{2,1,0:T(4,128)S(1)}, f32[3,4,128]{2,1,0:T(4,128)S(1)}, u32[]{:S(2)}, u32[]{:S(2)}) %collective-permute-start.60) | collective-permute-done | bytes 6176 | tf_op jit(solution)/shard_map/ppermute | solution.py:402
  (150 shorter events, 74.7 us)
Async XLA Ops:
  0.7 109.2 %collective-permute-start.53 = (bf16[2008,1024]{1,0:T(8,128)(2,1)}, bf16[2008,1024]{1,0:T(8,128)(2,1)}, u32[]{:S(2)}, u32[]{:S(2)}) collective-permute-start(bf16[2008,1024]{1,0:T(8,128)(2,1)} %bitcast.20), channel_id=1, source_target_pairs={{1,2},{5,6},{9,10},{13,14},{17,18},{21,22},{25,26},{29,30},{2,1},{... | collective-permute-start | bytes 12337160 | tf_op jit(solution)/shard_map/ppermute | solution.py:505
  3.4 91.2 %collective-permute-start.23 = (bf16[320,1024]{1,0:T(8,128)(2,1)}, bf16[320,1024]{1,0:T(8,128)(2,1)}, u32[]{:S(2)}, u32[]{:S(2)}) collective-permute-start(bf16[320,1024]{1,0:T(8,128)(2,1)} %bitcast.23), channel_id=1, source_target_pairs={{0,2},{2,0},{4,6},{6,4},{8,10},{10,8},{12,14},{14,12},{16,18},{18,... | collective-permute-start | bytes 1966088 | tf_op jit(solution)/shard_map/ppermute | solution.py:399
  5.9 90.4 %collective-permute-start.22 = (bf16[320,1024]{1,0:T(8,128)(2,1)}, bf16[320,1024]{1,0:T(8,128)(2,1)}, u32[]{:S(2)}, u32[]{:S(2)}) collective-permute-start(bf16[320,1024]{1,0:T(8,128)(2,1)} %bitcast.24), channel_id=1, source_target_pairs={{0,1},{1,0},{2,3},{3,2},{4,5},{5,4},{6,7},{7,6},{8,9},{9,8},{10,11... | collective-permute-start | bytes 1966088 | tf_op jit(solution)/shard_map/ppermute | solution.py:402
  6.3 66.4 %collective-permute-start.1 = (s32[1,256]{1,0:T(1,128)S(1)}, s32[1,256]{1,0:T(1,128)S(1)}, u32[]{:S(2)}, u32[]{:S(2)}) collective-permute-start(s32[1,256]{1,0:T(1,128)S(1)} %reshape.48.gold_ref), channel_id=1, source_target_pairs={{0,1},{1,0},{2,3},{3,2},{4,5},{5,4},{6,7},{7,6},{8,9},{9,8},{10,11... | collective-permute-start | bytes 3080 | tf_op jit(solution)/shard_map/ppermute | solution.py:402
  8.0 63.3 %collective-permute-start = (bf16[1024,128]{1,0:T(8,128)(2,1)}, bf16[1024,128]{1,0:T(8,128)(2,1)}, u32[]{:S(2)}, u32[]{:S(2)}) collective-permute-start(bf16[1024,128]{1,0:T(8,128)(2,1)} %param.22), channel_id=1, source_target_pairs={{0,1},{1,0},{2,3},{3,2},{4,5},{5,4},{6,7},{7,6},{8,9},{9,8},{10,11... | collective-permute-start | bytes 786440 | tf_op jit(solution)/shard_map/ppermute | solution.py:402
  10.8 69.8 %all-to-all-start = ((bf16[16,2,128,128]{3,2,1,0:T(8,128)(2,1)}), bf16[16,2,128,128]{3,2,1,0:T(8,128)(2,1)S(1)}, u32[]{:S(2)}, u32[]{:S(2)}) async-start(bf16[16,2,128,128]{3,2,1,0:T(8,128)(2,1)} %by_heads.1), calls=%async_computation | async-start | bytes 2097152 | tf_op jit(solution)/shard_map/all_to_all | solution.py:448
  71.3 8.7 %collective-permute-start.5 = (bf16[128,1024]{1,0:T(8,128)(2,1)}, bf16[128,1024]{1,0:T(8,128)(2,1)}, u32[]{:S(2)}, u32[]{:S(2)}) collective-permute-start(bf16[128,1024]{1,0:T(8,128)(2,1)} %refs_0_.1), channel_id=1, source_target_pairs={{0,1},{1,0},{2,3},{3,2},{4,5},{5,4},{6,7},{7,6},{8,9},{9,8},{10,11... | collective-permute-start | bytes 786440 | tf_op jit(solution)/shard_map/ppermute | solution.py:402
  72.7 7.9 %collective-permute-start.2 = (bf16[256,128]{1,0:T(8,128)(2,1)S(1)}, bf16[256,128]{1,0:T(8,128)(2,1)S(1)}, u32[]{:S(2)}, u32[]{:S(2)}) collective-permute-start(bf16[256,128]{1,0:T(8,128)(2,1)S(1)} %get-tuple-element.66), channel_id=1, source_target_pairs={{0,1},{1,0},{2,3},{3,2},{4,5},{5,4},{6,7},{7,6},{8,9},{9,8},{10,11... | collective-permute-start | bytes 196616 | tf_op jit(solution)/shard_map/ppermute | solution.py:402
  88.5 12.8 %collective-permute-start.26 = (bf16[320,1024]{1,0:T(8,128)(2,1)S(1)}, bf16[320,1024]{1,0:T(8,128)(2,1)S(1)}, u32[]{:S(2)}, u32[]{:S(2)}) collective-permute-start(bf16[320,1024]{1,0:T(8,128)(2,1)S(1)} %bitcast.26), channel_id=1, source_target_pairs={{0,2},{2,0},{4,6},{6,4},{8,10},{10,8},{12,14},{14,12},{16,18},{18,... | collective-permute-start | bytes 1966088 | tf_op jit(solution)/shard_map/ppermute | solution.py:399
  90.5 17.8 %collective-permute-start.25 = (bf16[320,1024]{1,0:T(8,128)(2,1)S(1)}, bf16[320,1024]{1,0:T(8,128)(2,1)S(1)}, u32[]{:S(2)}, u32[]{:S(2)}) collective-permute-start(bf16[320,1024]{1,0:T(8,128)(2,1)S(1)} %bitcast.27), channel_id=1, source_target_pairs={{0,1},{1,0},{2,3},{3,2},{4,5},{5,4},{6,7},{7,6},{8,9},{9,8},{10,11... | collective-permute-start | bytes 1966088 | tf_op jit(solution)/shard_map/ppermute | solution.py:402
  96.3 25.5 %collective-permute-start.28 = (bf16[320,1024]{1,0:T(8,128)(2,1)S(1)}, bf16[320,1024]{1,0:T(8,128)(2,1)S(1)}, u32[]{:S(2)}, u32[]{:S(2)}) collective-permute-start(bf16[320,1024]{1,0:T(8,128)(2,1)S(1)} %copy-done.4), channel_id=1, source_target_pairs={{0,1},{1,0},{2,3},{3,2},{4,5},{5,4},{6,7},{7,6},{8,9},{9,8},{10,11... | collective-permute-start | bytes 1966088 | tf_op jit(solution)/shard_map/ppermute | solution.py:402
  99.7 8.7 %collective-permute-start.11 = (bf16[32,2048]{1,0:T(8,128)(2,1)S(1)}, bf16[32,2048]{1,0:T(8,128)(2,1)S(1)}, u32[]{:S(2)}, u32[]{:S(2)}) collective-permute-start(bf16[32,2048]{1,0:T(8,128)(2,1)S(1)} %get-tuple-element.43), channel_id=1, source_target_pairs={{0,4},{2,6},{4,0},{6,2},{8,12},{10,14},{12,8},{14,10},{16,20},{18,... | collective-permute-start | bytes 393224 | tf_op jit(solution)/shard_map/ppermute | solution.py:399
  101.3 24.6 %collective-permute-start.29 = (bf16[320,1024]{1,0:T(8,128)(2,1)S(1)}, bf16[320,1024]{1,0:T(8,128)(2,1)S(1)}, u32[]{:S(2)}, u32[]{:S(2)}) collective-permute-start(bf16[320,1024]{1,0:T(8,128)(2,1)S(1)} %copy-done.4), channel_id=1, source_target_pairs={{0,2},{2,0},{4,6},{6,4},{8,10},{10,8},{12,14},{14,12},{16,18},{18,... | collective-permute-start | bytes 1966088 | tf_op jit(solution)/shard_map/ppermute | solution.py:399
  108.3 114.0 %collective-permute-start.54 = (bf16[2008,1024]{1,0:T(8,128)(2,1)}, bf16[2008,1024]{1,0:T(8,128)(2,1)S(1)}, u32[]{:S(2)}, u32[]{:S(2)}) collective-permute-start(bf16[2008,1024]{1,0:T(8,128)(2,1)} %bitcast.21), channel_id=1, source_target_pairs={{0,2},{2,0},{4,6},{6,4},{8,10},{10,8},{12,14},{14,12},{16,18},{18,... | collective-permute-start | bytes 12337160 | tf_op jit(solution)/shard_map/ppermute | solution.py:399
  108.4 14.9 %collective-permute-start.13 = (bf16[32,2048]{1,0:T(8,128)(2,1)S(1)}, bf16[32,2048]{1,0:T(8,128)(2,1)S(1)}, u32[]{:S(2)}, u32[]{:S(2)}) collective-permute-start(bf16[32,2048]{1,0:T(8,128)(2,1)S(1)} %get-tuple-element.45), channel_id=1, source_target_pairs={{0,4},{2,6},{4,0},{6,2},{8,12},{10,14},{12,8},{14,10},{16,20},{18,... | collective-permute-start | bytes 393224 | tf_op jit(solution)/shard_map/ppermute | solution.py:399
  109.9 112.5 %collective-permute-start.55 = (bf16[2008,1024]{1,0:T(8,128)(2,1)}, bf16[2008,1024]{1,0:T(8,128)(2,1)S(1)}, u32[]{:S(2)}, u32[]{:S(2)}) collective-permute-start(bf16[2008,1024]{1,0:T(8,128)(2,1)} %collective-permute-done.53.refs_17_), channel_id=1, source_target_pairs={{0,2},{2,0},{4,6},{6,4},{8,10},{10,8},{12,14},{14,12},{16,18},{18,... | collective-permute-start | bytes 12337160 | tf_op jit(solution)/shard_map/ppermute | solution.py:399
  123.2 12.2 %collective-permute-start.10 = (bf16[32,2048]{1,0:T(8,128)(2,1)S(1)}, bf16[32,2048]{1,0:T(8,128)(2,1)S(1)}, u32[]{:S(2)}, u32[]{:S(2)}) collective-permute-start(bf16[32,2048]{1,0:T(8,128)(2,1)S(1)} %add_convert_fusion.5), channel_id=1, source_target_pairs={{0,16},{2,18},{4,20},{6,22},{8,24},{10,26},{12,28},{14,30},{16,0},... | collective-permute-start | bytes 393224 | tf_op jit(solution)/shard_map/ppermute | solution.py:399
  125.9 9.6 %collective-permute-start.12 = (bf16[32,2048]{1,0:T(8,128)(2,1)S(1)}, bf16[32,2048]{1,0:T(8,128)(2,1)S(1)}, u32[]{:S(2)}, u32[]{:S(2)}) collective-permute-start(bf16[32,2048]{1,0:T(8,128)(2,1)S(1)} %add_convert_fusion.4), channel_id=1, source_target_pairs={{0,24},{2,26},{4,28},{6,30},{8,16},{10,18},{12,20},{14,22},{16,8},... | collective-permute-start | bytes 393224 | tf_op jit(solution)/shard_map/ppermute | solution.py:399
  127.3 8.7 %collective-permute-start.14 = (bf16[32,2048]{1,0:T(8,128)(2,1)S(1)}, bf16[32,2048]{1,0:T(8,128)(2,1)S(1)}, u32[]{:S(2)}, u32[]{:S(2)}) collective-permute-start(bf16[32,2048]{1,0:T(8,128)(2,1)S(1)} %add_convert_fusion.3), channel_id=1, source_target_pairs={{0,8},{2,10},{4,12},{6,14},{8,0},{10,2},{12,4},{14,6},{16,24},{18,... | collective-permute-start | bytes 393224 | tf_op jit(solution)/shard_map/ppermute | solution.py:399
  137.8 8.3 %collective-permute-start.20 = (bf16[32,2048]{1,0:T(8,128)(2,1)S(1)}, bf16[32,2048]{1,0:T(8,128)(2,1)S(1)}, u32[]{:S(2)}, u32[]{:S(2)}) collective-permute-start(bf16[32,2048]{1,0:T(8,128)(2,1)S(1)} %get-tuple-element.47.refs_0_), channel_id=1, source_target_pairs={{0,24},{2,26},{4,28},{6,30},{8,16},{10,18},{12,20},{14,22},{16,8},... | collective-permute-start | bytes 393224 | tf_op jit(solution)/shard_map/ppermute | solution.py:399
  140.2 12.4 %collective-permute-start.18 = (bf16[32,2048]{1,0:T(8,128)(2,1)S(1)}, bf16[32,2048]{1,0:T(8,128)(2,1)S(1)}, u32[]{:S(2)}, u32[]{:S(2)}) collective-permute-start(bf16[32,2048]{1,0:T(8,128)(2,1)S(1)} %get-tuple-element.47.refs_0_), channel_id=1, source_target_pairs={{0,16},{2,18},{4,20},{6,22},{8,24},{10,26},{12,28},{14,30},{16,0},... | collective-permute-start | bytes 393224 | tf_op jit(solution)/shard_map/ppermute | solution.py:399
  141.8 11.4 %collective-permute-start.16 = (bf16[32,2048]{1,0:T(8,128)(2,1)S(1)}, bf16[32,2048]{1,0:T(8,128)(2,1)S(1)}, u32[]{:S(2)}, u32[]{:S(2)}) collective-permute-start(bf16[32,2048]{1,0:T(8,128)(2,1)S(1)} %get-tuple-element.47.refs_0_), channel_id=1, source_target_pairs={{0,8},{2,10},{4,12},{6,14},{8,0},{10,2},{12,4},{14,6},{16,24},{18,... | collective-permute-start | bytes 393224 | tf_op jit(solution)/shard_map/ppermute | solution.py:399
  146.0 8.6 %collective-permute-start.15 = (bf16[32,2048]{1,0:T(8,128)(2,1)S(1)}, bf16[32,2048]{1,0:T(8,128)(2,1)S(1)}, u32[]{:S(2)}, u32[]{:S(2)}) collective-permute-start(bf16[32,2048]{1,0:T(8,128)(2,1)S(1)} %get-tuple-element.47.refs_0_), channel_id=1, source_target_pairs={{0,4},{2,6},{4,0},{6,2},{8,12},{10,14},{12,8},{14,10},{16,20},{18,... | collective-permute-start | bytes 393224 | tf_op jit(solution)/shard_map/ppermute | solution.py:399
  153.2 8.5 %collective-permute-start.19 = (bf16[32,2048]{1,0:T(8,128)(2,1)S(1)}, bf16[32,2048]{1,0:T(8,128)(2,1)S(1)}, u32[]{:S(2)}, u32[]{:S(2)}) collective-permute-start(bf16[32,2048]{1,0:T(8,128)(2,1)S(1)} %collective-permute-done.18.refs_4_), channel_id=1, source_target_pairs={{0,4},{2,6},{4,0},{6,2},{8,12},{10,14},{12,8},{14,10},{16,20},{18,... | collective-permute-start | bytes 393224 | tf_op jit(solution)/shard_map/ppermute | solution.py:399
  154.7 8.4 %collective-permute-start.17 = (bf16[32,2048]{1,0:T(8,128)(2,1)S(1)}, bf16[32,2048]{1,0:T(8,128)(2,1)S(1)}, u32[]{:S(2)}, u32[]{:S(2)}) collective-permute-start(bf16[32,2048]{1,0:T(8,128)(2,1)S(1)} %collective-permute-done.16.refs_2_), channel_id=1, source_target_pairs={{0,4},{2,6},{4,0},{6,2},{8,12},{10,14},{12,8},{14,10},{16,20},{18,... | collective-permute-start | bytes 393224 | tf_op jit(solution)/shard_map/ppermute | solution.py:399
  167.8 14.3 %collective-permute-start.31 = (bf16[32,2048]{1,0:T(8,128)(2,1)S(1)}, bf16[32,2048]{1,0:T(8,128)(2,1)S(1)}, u32[]{:S(2)}, u32[]{:S(2)}) collective-permute-start(bf16[32,2048]{1,0:T(8,128)(2,1)S(1)} %get-tuple-element.49), channel_id=1, source_target_pairs={{0,4},{2,6},{4,0},{6,2},{8,12},{10,14},{12,8},{14,10},{16,20},{18,... | collective-permute-start | bytes 393224 | tf_op jit(solution)/shard_map/ppermute | solution.py:399
  169.3 9.0 %collective-permute-start.34 = (bf16[32,2048]{1,0:T(8,128)(2,1)S(1)}, bf16[32,2048]{1,0:T(8,128)(2,1)S(1)}, u32[]{:S(2)}, u32[]{:S(2)}) collective-permute-start(bf16[32,2048]{1,0:T(8,128)(2,1)S(1)} %get-tuple-element.53), channel_id=1, source_target_pairs={{0,4},{2,6},{4,0},{6,2},{8,12},{10,14},{12,8},{14,10},{16,20},{18,... | collective-permute-start | bytes 393224 | tf_op jit(solution)/shard_map/ppermute | solution.py:399
  178.3 9.7 %collective-permute-start.33 = (bf16[32,2048]{1,0:T(8,128)(2,1)S(1)}, bf16[32,2048]{1,0:T(8,128)(2,1)S(1)}, u32[]{:S(2)}, u32[]{:S(2)}) collective-permute-start(bf16[32,2048]{1,0:T(8,128)(2,1)S(1)} %add_convert_fusion.2), channel_id=1, source_target_pairs={{0,16},{2,18},{4,20},{6,22},{8,24},{10,26},{12,28},{14,30},{16,0},... | collective-permute-start | bytes 393224 | tf_op jit(solution)/shard_map/ppermute | solution.py:399
  179.7 8.2 %collective-permute-start.35 = (bf16[32,2048]{1,0:T(8,128)(2,1)S(1)}, bf16[32,2048]{1,0:T(8,128)(2,1)S(1)}, u32[]{:S(2)}, u32[]{:S(2)}) collective-permute-start(bf16[32,2048]{1,0:T(8,128)(2,1)S(1)} %add_convert_fusion.1), channel_id=1, source_target_pairs={{0,24},{2,26},{4,28},{6,30},{8,16},{10,18},{12,20},{14,22},{16,8},... | collective-permute-start | bytes 393224 | tf_op jit(solution)/shard_map/ppermute | solution.py:399
  182.1 7.1 %collective-permute-start.37 = (bf16[32,2048]{1,0:T(8,128)(2,1)S(1)}, bf16[32,2048]{1,0:T(8,128)(2,1)S(1)}, u32[]{:S(2)}, u32[]{:S(2)}) collective-permute-start(bf16[32,2048]{1,0:T(8,128)(2,1)S(1)} %add_convert_fusion), channel_id=1, source_target_pairs={{0,8},{2,10},{4,12},{6,14},{8,0},{10,2},{12,4},{14,6},{16,24},{18,... | collective-permute-start | bytes 393224 | tf_op jit(solution)/shard_map/ppermute | solution.py:399
  191.4 9.4 %collective-permute-start.41 = (bf16[32,2048]{1,0:T(8,128)(2,1)S(1)}, bf16[32,2048]{1,0:T(8,128)(2,1)S(1)}, u32[]{:S(2)}, u32[]{:S(2)}) collective-permute-start(bf16[32,2048]{1,0:T(8,128)(2,1)S(1)} %residual_norm.3.refs_0_), channel_id=1, source_target_pairs={{0,16},{2,18},{4,20},{6,22},{8,24},{10,26},{12,28},{14,30},{16,0},... | collective-permute-start | bytes 393224 | tf_op jit(solution)/shard_map/ppermute | solution.py:399
  194.5 7.9 %collective-permute-start.39 = (bf16[32,2048]{1,0:T(8,128)(2,1)S(1)}, bf16[32,2048]{1,0:T(8,128)(2,1)S(1)}, u32[]{:S(2)}, u32[]{:S(2)}) collective-permute-start(bf16[32,2048]{1,0:T(8,128)(2,1)S(1)} %residual_norm.3.refs_0_), channel_id=1, source_target_pairs={{0,8},{2,10},{4,12},{6,14},{8,0},{10,2},{12,4},{14,6},{16,24},{18,... | collective-permute-start | bytes 393224 | tf_op jit(solution)/shard_map/ppermute | solution.py:399
  (41 other events, 724.5 us)
